TPU v7x, 32 devices: a whole 2x2x4 slice. The times are simulated.
32 devices in a mesh: dp: 2 (over x), ty: 4 (over z), tx: 4 (over y, core).
Axes of the slice: x: 2, y: 2, z: 4, core: 2. Of those that a mesh axis runs over, the one named last changes fastest.
Arguments:
- hidden: bfloat16 [8192, 2048], P(('dp', 'ty'), 'tx'), parts along dimension 0
- positions: int32 [8192], P(('dp', 'tx')), parts along dimension 0
- g_ffn: bfloat16 [2048], P('tx')
- w_gate: bfloat16 [2048, 8192], P('tx', 'ty')
- w_up: bfloat16 [2048, 8192], P('tx', 'ty')
- w_down: bfloat16 [8192, 2048], P('ty', 'tx')
- g_attn: bfloat16 [2048], P('tx')
- w_q: bfloat16 [2048, 32, 64], P('tx', 'ty')
- w_kv: bfloat16 [2048, 16, 64], P('tx', 'ty')
- grad_h2: bfloat16 [8192, 2048], P(('dp', 'ty'), 'tx'), parts along dimension 0
- grad_q: bfloat16 [8192, 32, 64], P(('dp', 'tx'), 'ty'), parts along dimension 0
- grad_kv: bfloat16 [8192, 16, 64], P(('dp', 'tx'), 'ty'), parts along dimension 0
Outputs:
- output 1: bfloat16 [8192, 2048], P(('dp', 'ty'), 'tx'), parts along dimension 0
- output 2: bfloat16 [8192, 32, 64], P(('dp', 'tx'), 'ty'), parts along dimension 0
- output 3: bfloat16 [8192, 16, 64], P(('dp', 'tx'), 'ty'), parts along dimension 0
- output 4: bfloat16 [8192, 2048], P(('dp', 'ty'), 'tx'), parts along dimension 0
- output 5: float32 [4096], P(('dp', 'tx')), parts along dimension 0
- output 6: float32 [4096], P(('dp', 'tx')), parts along dimension 0
- output 7: float32 [4096, 8192], P(('dp', 'tx'), 'ty'), parts along dimension 0
- output 8: float32 [4096, 8192], P(('dp', 'tx'), 'ty'), parts along dimension 0
- output 9: float32 [16384, 2048], P(('dp', 'ty'), 'tx'), parts along dimension 0
- output 10: float32 [4096, 32, 64], P(('dp', 'tx'), 'ty'), parts along dimension 0
- output 11: float32 [4096, 16, 64], P(('dp', 'tx'), 'ty'), parts along dimension 0
There are 2 independent parts. A program takes and returns all parts, laid end to end along the dimension named above; an argument that names none is the same for every part.
All inputs are finite; a program needn't handle non-finite values.
Results may differ from a plain program's by a relative error of at most 0.02.
Values are sent between devices in bfloat16 or wider.
A program may use at most 1 GiB of HBM per device.

v0:
```python
import functools

import jax
import jax.numpy as jnp
from jax import lax
from jax.experimental import pallas as pl
from jax.experimental.pallas import tpu as pltpu
from jax.sharding import PartitionSpec as P

NORM_EPS = 1e-5
ROPE_BASE = 10000.0
F32 = jnp.float32
BF16 = jnp.bfloat16


def dot(a, b, dims=(((1,), (0,)), ((), ()))):
    return lax.dot_general(a, b, dims, preferred_element_type=F32)


MESH = pl.DeviceIdType.MESH
ANY = pl.BlockSpec(memory_space=pl.ANY)
VMEM = pltpu.VMEM
NT_DIMS = (((1,), (1,)), ((), ()))
VMEM_LIMIT = 67000000


def ds(start, size, align=None):
    if isinstance(start, int):
        return pl.ds(start, size)
    return pl.ds(pl.multiple_of(start, align or size), size)


def mid(z):
    return jnp.logical_and(z > 0, z < 3)


def end(z):
    return jnp.logical_or(z == 0, z == 3)


def slots(z):
    return (z + 1 - 2 * (z % 2), 2 - z // 2, 3 - 3 * (z // 2))


def turn(src, dst, rows, width, q_width, cos_ref, sin_ref, swap_ref, back):
    step = min(256, rows)

    @pl.loop(0, rows // step)
    def _(r):
        for c in range(width // 128):
            cols = pl.ds(c * 128, 128)
            table = ds(r * step + (0 if c * 128 < q_width else rows), step, step)
            x = src[ds(r * step, step), cols]
            main = x.astype(F32) * cos_ref[table, :]
            side = dot(x, swap_ref[...]) * sin_ref[table, :]
            dst[ds(r * step, step), cols] = (main - side if back else main + side).astype(BF16)


class Wires:
    def __init__(self, send, recv, local):
        self.send, self.recv, self.local = send, recv, local
        self.n_remote = 0
        self.n_local = 0

    def take(self, n=1):
        base = self.n_remote
        self.n_remote += n
        assert self.n_remote <= self.send.shape[0]
        return base

    def copy(self, src, dst, si, ri, **dev):
        return pltpu.make_async_remote_copy(
            src_ref=src, dst_ref=dst, send_sem=self.send.at[si], recv_sem=self.recv.at[ri],
            device_id=dev, device_id_type=MESH)

    def here(self, src, dst):
        i = self.n_local
        self.n_local += 1
        assert i < self.local.shape[0]
        c = pltpu.make_async_copy(src, dst, self.local.at[i])
        c.start()
        return c


def entry_barrier(axes, z):
    sem = pltpu.get_barrier_semaphore()
    for dev in axes:
        pl.semaphore_signal(sem, inc=1, device_id=dev, device_id_type=MESH)

    @pl.when(z > 0)
    def _():
        pl.semaphore_signal(sem, inc=1, device_id={"ty": z - 1}, device_id_type=MESH)

    @pl.when(z < 3)
    def _():
        pl.semaphore_signal(sem, inc=1, device_id={"ty": z + 1}, device_id_type=MESH)

    @pl.when(mid(z))
    def _():
        pl.semaphore_wait(sem, len(axes) + 2)

    @pl.when(end(z))
    def _():
        pl.semaphore_wait(sem, len(axes) + 1)


class LineGather:
    def __init__(self, net, buf, rows, z):
        self.net, self.buf, self.rows, self.z = net, buf, rows, z
        self.base = net.take(8)
        self.slots = slots(z)

    def blk(self, b):
        return self.buf.at[ds(b * self.rows, self.rows), :]

    def cp(self, b, side, target):
        return self.net.copy(self.blk(b), self.blk(b), self.base + side * 4 + b, self.base + b, ty=target)

    def start(self):
        z = self.z

        @pl.when(z < 3)
        def _():
            self.cp(z, 0, z + 1).start()

        @pl.when(z > 0)
        def _():
            self.cp(z, 1, z - 1).start()

    def take(self, i):
        b = self.slots[i]
        self.cp(b, 0, self.z).wait_recv()

    def forward(self, i):
        z, b = self.z, self.slots[i]
        target = 3 - z if i == 0 else 3 * (z - 1)
        self.cp(b, 0, target).start()

    def step1(self):
        self.take(0)

        @pl.when(mid(self.z))
        def _():
            self.forward(0)
            self.take(1)
            self.forward(1)

    def step2(self):
        @pl.when(end(self.z))
        def _():
            self.take(1)

    def step3(self):
        self.take(2)

        @pl.when(mid(self.z))
        def _():
            self.forward(2)

    def drain(self):
        z = self.z

        @pl.when(z < 3)
        def _():
            self.cp(z, 0, z + 1).wait_send()

        @pl.when(z > 0)
        def _():
            self.cp(z, 1, z - 1).wait_send()

        @pl.when(mid(z))
        def _():
            for i in range(3):
                self.cp(self.slots[i], 0, 3 - z if i == 0 else 3 * (z - 1)).wait_send()


class LineScatter:
    def __init__(self, net, part, rbuf, rows, z):
        self.net, self.part, self.rbuf, self.rows, self.z = net, part, rbuf, rows, z
        self.base = net.take(5)
        self.slots = slots(z)
        one = (z % 2) * (1 - z // 2)
        self.dst = (self.slots[0] + (1 - z % 2) * (3 - z), self.slots[1] + 2 * one, self.slots[2])
        self.target = (z + 1 - 2 * (z % 2), 1 + z % 2, 1 + z % 2)

    def cp(self, i):
        return self.net.copy(
            self.part.at[ds(self.slots[i] * self.rows, self.rows), :], self.rbuf.at[ds(self.dst[i] * self.rows, self.rows), :],
            self.base + i, self.base + self.dst[i], ty=self.target[i])

    def wait_slot(self, s):
        view = self.rbuf.at[ds(s * self.rows, self.rows), :]
        self.net.copy(view, view, self.base, self.base + s, ty=self.z).wait_recv()

    def send_end(self, i):
        @pl.when(end(self.z))
        def _():
            self.cp(i).start()

    def send_mid(self, i):
        @pl.when(mid(self.z))
        def _():
            b = self.slots[i]
            self.wait_slot(b)
            step = min(32, self.rows)

            @pl.loop(0, self.rows // step)
            def _(r):
                view = ds(b * self.rows + r * step, step, step)
                self.part[view, :] = (self.part[view, :].astype(F32) + self.rbuf[view, :].astype(F32)).astype(BF16)

            self.cp(i).start()

    def finish(self):
        z = self.z

        @pl.when(z < 3)
        def _():
            self.wait_slot(z)

        @pl.when(z > 0)
        def _():
            self.wait_slot(4)

    def drain(self):
        for i in range(3):
            self.cp(i).wait_send()


class WeightGather:
    def __init__(self, net, w, full, pos, by_rows, chunks):
        self.net, self.w, self.full, self.by_rows = net, w, full, by_rows
        self.dp, self.t1, self.t2 = pos
        self.len = w.shape[0]
        self.width = w.shape[0] if by_rows else w.shape[1]
        self.chunks = chunks
        self.piece = self.len // 2 // chunks
        self.base = net.take(1 + 4 * chunks)

    def dst(self, k, off, n):
        if self.by_rows:
            return self.full.at[ds(k * self.width + off, n, min(n, 16)), :]
        return self.full.at[ds(off, n, 16), pl.ds(k * self.width, self.width)]

    def off(self, half, ch):
        return half * (self.len // 2) + ch * self.piece

    def near(self, ch):
        o = self.off(self.dp, ch)
        i = self.base + 1 + ch
        return self.net.copy(self.w.at[ds(o, self.piece, 16), :], self.dst(2, o, self.piece), i, i, tx=self.t2)

    def cross(self, ch, half):
        o = self.off(half, ch)
        i = self.base + 1 + self.chunks + ch
        return self.net.copy(self.dst(2, o, self.piece), self.dst(2, o, self.piece), i, i, dp=1 - self.dp)

    def diag(self, ch, which, half):
        o = self.off(half, ch)
        i = self.base + 1 + (2 + which) * self.chunks + ch
        return self.net.copy(self.dst(2, o, self.piece), self.dst(3, o, self.piece), i, i, tx=self.t1)

    def mate(self):
        return self.net.copy(self.w, self.dst(1, 0, self.len), self.base, self.base, tx=self.t1)

    def start_y(self):
        for ch in range(self.chunks):
            self.near(ch).start()

    def start_local(self):
        self.own = self.net.here(self.w, self.dst(0, 0, self.len))
        self.mate().start()

    def y_event(self, ch):
        self.near(ch).wait_recv()
        self.cross(ch, self.dp).start()
        self.diag(ch, 0, self.dp).start()

    def x_event(self, ch):
        self.cross(ch, 1 - self.dp).wait_recv()
        self.diag(ch, 1, 1 - self.dp).start()

    def finish(self):
        self.own.wait()
        self.mate().wait_recv()
        for ch in range(self.chunks):
            self.diag(ch, 0, self.dp).wait_recv()
            self.diag(ch, 1, 1 - self.dp).wait_recv()

    def drain(self):
        self.mate().wait_send()
        for ch in range(self.chunks):
            self.near(ch).wait_send()
            self.cross(ch, self.dp).wait_send()
            self.diag(ch, 0, self.dp).wait_send()
            self.diag(ch, 1, 1 - self.dp).wait_send()


def places():
    dp, z, tx = lax.axis_index("dp"), lax.axis_index("ty"), lax.axis_index("tx")
    return dp, z, tx, (tx, tx + 1 - 2 * (tx % 2), (tx + 2) % 4, 3 - tx)


def kernel_a(q_width, hid, eqh, cosh, sinh, swaph, dh2h, wg, wu, wd, wq, gin,
             n_o, a_o, b_o, u_o, wg_o, wu_o, wd_o, wq_o, eq_o, h_o, dh2_o, dn2_o, g_o,
             rows, n_v, a_v, b_v, u_v, wg_v, wu_v, wq_v, eq_v, p_v, rbuf, gains, dn2_v, cos_v, sin_v, swap_v, send, recv, local):
    dp, z, tx, peer = places()
    sub, dim = rows.shape
    width = eq_v.shape[1]
    dt = dim // 4
    ff = wg.shape[1]
    tile = min(512, ff)
    dtile = min(512, dim)
    net = Wires(send, recv, local)
    eq_raw = p_v.at[:, pl.ds(0, width)]
    turn_in = [net.here(eqh, eq_raw), net.here(cosh, cos_v), net.here(sinh, sin_v), net.here(swaph, swap_v)]
    entry_barrier([{"tx": peer[1]}, {"tx": peer[2]}, {"tx": peer[3]}, {"dp": 1 - dp}], z)

    pos = (dp, peer[1], peer[2])
    far_first = (2, 3, 1)
    g_id, h_id, e_id, d_id = net.take(4), net.take(4), net.take(4), net.take(4)

    def g_cp(k):
        return net.copy(gin, gains.at[:, pl.ds(k * dt, dt)], g_id + k, g_id + k, tx=peer[k])

    def h_cp(k):
        return net.copy(hid.at[ds(peer[k] * sub, sub), :], rows.at[:, pl.ds(k * dt, dt)], h_id + k, h_id + k, tx=peer[k])

    def e_cp(k, block):
        return net.copy(p_v.at[ds(peer[k] * sub, sub), pl.ds(0, width)], eq_v.at[ds(block * sub, sub), :], e_id + k, e_id + k, tx=peer[k])

    def d_cp(k):
        return net.copy(dh2h.at[ds(peer[k] * sub, sub), :], dh2_o.at[:, pl.ds(k * dt, dt)], d_id + k, d_id + k, tx=peer[k])

    gate = WeightGather(net, wg, wg_v, pos, True, 2)
    up = WeightGather(net, wu, wu_v, pos, True, 2)
    down = WeightGather(net, wd, wd_o, pos, False, 2)
    qkv = WeightGather(net, wq, wq_v, pos, True, 1)
    ag = LineGather(net, n_v, sub, z)
    rsc = LineScatter(net, p_v, rbuf, sub, z)

    for k in far_first:
        g_cp(k).start()
    for k in far_first:
        h_cp(k).start()
    g_own = net.here(gin, gains.at[:, pl.ds(0, dt)])
    h_own = net.here(hid.at[ds(tx * sub, sub), :], rows.at[:, pl.ds(0, dt)])
    for c in turn_in:
        c.wait()
    turn(p_v, p_v, 4 * sub, width, q_width, cos_v, sin_v, swap_v, True)
    for k in far_first:
        e_cp(k, tx).start()
    e_own = net.here(p_v.at[ds(tx * sub, sub), pl.ds(0, width)], eq_v.at[ds(tx * sub, sub), :])
    for w in (qkv, gate, up, down):
        w.start_y()
    for k in far_first:
        d_cp(k).start()
    for w in (qkv, gate, up, down):
        w.start_local()
    d_own = net.here(dh2h.at[ds(tx * sub, sub), :], dh2_o.at[:, pl.ds(0, dt)])

    for k in far_first:
        g_cp(k).wait_recv()
        h_cp(k).wait_recv()
    g_own.wait()
    h_own.wait()

    @pl.loop(0, sub // 16)
    def _(r):
        x = rows[ds(r * 16, 16), :].astype(F32)
        inv = lax.rsqrt(jnp.sum(x * x, axis=1, keepdims=True) / dim + NORM_EPS)
        n_v[ds(z * sub + r * 16, 16), :] = (x * inv * gains[0:1, :]).astype(BF16)

    outs = [net.here(rows, h_o), net.here(gains, g_o)]
    ag.start()
    for k in far_first:
        e_cp(k, peer[k]).wait_recv()
    e_own.wait()
    ag.step1()
    qkv.y_event(0)
    gate.y_event(0)
    qkv.x_event(0)
    qkv.finish()
    for k in far_first:
        e_cp(k, tx).wait_send()

    @pl.loop(0, 4)
    def _(b):
        @pl.loop(0, dim // dtile)
        def _(j):
            w = wq_v[ds(j * dtile, dtile), :]
            p_v[ds(b * sub, sub), ds(j * dtile, dtile)] = dot(eq_v[ds(b * sub, sub), :], w, NT_DIMS).astype(BF16)

    for i in (2, 1, 0):
        rsc.send_end(i)
    gate.x_event(0)
    ag.step2()
    ag.step3()
    gate.y_event(1)
    gate.x_event(1)
    up.y_event(0)
    rsc.send_mid(2)
    gate.finish()

    def gate_block(b):
        @pl.loop(0, ff // tile)
        def _(j):
            cols = ds(j * tile, tile)
            a_v[ds(b * sub, sub), cols] = dot(n_v[ds(b * sub, sub), :], wg_v[:, cols]).astype(BF16)

    def up_block(b):
        @pl.loop(0, ff // tile)
        def _(j):
            cols = ds(j * tile, tile)
            bb = dot(n_v[ds(b * sub, sub), :], wu_v[:, cols]).astype(BF16)
            b_v[ds(b * sub, sub), cols] = bb
            aa = a_v[ds(b * sub, sub), cols].astype(F32)
            u_v[ds(b * sub, sub), cols] = (aa * jax.nn.sigmoid(aa) * bb.astype(F32)).astype(BF16)

    gate_block(z)
    gate_block(ag.slots[0])
    gate_block(ag.slots[1])
    up.x_event(0)
    up.y_event(1)
    gate_block(ag.slots[2])
    outs += [net.here(n_v, n_o), net.here(a_v, a_o), net.here(wg_v, wg_o), net.here(wq_v, wq_o), net.here(eq_v, eq_o)]
    up.x_event(1)
    down.y_event(0)
    rsc.send_mid(1)
    rsc.send_mid(0)
    up.finish()
    up_block(z)
    up_block(ag.slots[0])
    down.x_event(0)
    down.y_event(1)
    up_block(ag.slots[1])
    up_block(ag.slots[2])
    outs += [net.here(b_v, b_o), net.here(u_v, u_o), net.here(wu_v, wu_o)]
    down.x_event(1)
    rsc.finish()

    @pl.loop(0, sub // 16)
    def _(r):
        dn2_v[ds(r * 16, 16), :] = p_v[ds(z * sub + r * 16, 16), :].astype(F32)

    @pl.when(z < 3)
    def _():
        @pl.loop(0, sub // 16)
        def _(r):
            dn2_v[ds(r * 16, 16), :] += rbuf[ds(z * sub + r * 16, 16), :].astype(F32)

    @pl.when(z > 0)
    def _():
        @pl.loop(0, sub // 16)
        def _(r):
            dn2_v[ds(r * 16, 16), :] += rbuf[ds(4 * sub + r * 16, 16), :].astype(F32)

    outs.append(net.here(dn2_v, dn2_o))
    down.finish()
    for k in far_first:
        d_cp(k).wait_recv()
    d_own.wait()
    for c in outs:
        c.wait()
    for k in far_first:
        g_cp(k).wait_send()
        h_cp(k).wait_send()
        d_cp(k).wait_send()
    for w in (qkv, gate, up, down):
        w.drain()
    ag.drain()
    rsc.drain()


def call_a(q_width, hid, eqh, cos_t, sin_t, swap, dh2h, wg, wu, wd, wq, gin):
    tokens, dt = hid.shape
    sub, dim, ff, width = tokens // 4, dt * 4, wg.shape[1], wq.shape[1]
    s = jax.ShapeDtypeStruct
    tok_ff = s((tokens, ff), BF16)
    shapes = (s((tokens, dim), BF16), tok_ff, tok_ff, tok_ff, s((dim, ff), BF16), s((dim, ff), BF16), s((ff, dim), BF16),
              s((dim, width), BF16), s((tokens, width), BF16), s((sub, dim), BF16), s((sub, dim), BF16), s((sub, dim), F32), s((8, dim), F32))
    return pl.pallas_call(
        functools.partial(kernel_a, q_width), out_shape=shapes, in_specs=[ANY] * 11, out_specs=[ANY] * len(shapes),
        scratch_shapes=[
            VMEM((sub, dim), BF16), VMEM((tokens, dim), BF16), VMEM((tokens, ff), BF16), VMEM((tokens, ff), BF16), VMEM((tokens, ff), BF16),
            VMEM((dim, ff), BF16), VMEM((dim, ff), BF16), VMEM((dim, width), BF16), VMEM((tokens, width), BF16), VMEM((tokens, dim), BF16),
            VMEM((5 * sub, dim), BF16), VMEM((8, dim), F32), VMEM((sub, dim), F32), VMEM((2 * tokens, 128), F32), VMEM((2 * tokens, 128), F32), VMEM((128, 128), BF16),
            pltpu.SemaphoreType.DMA((64,)), pltpu.SemaphoreType.DMA((64,)), pltpu.SemaphoreType.DMA((32,))],
        compiler_params=pltpu.CompilerParams(collective_id=0, has_side_effects=True, vmem_limit_bytes=VMEM_LIMIT),
        cost_estimate=pl.CostEstimate(flops=20 * tokens * dim * ff, bytes_accessed=100000000, transcendentals=0), name="phase_a",
    )(hid, eqh, cos_t, sin_t, swap, dh2h, wg, wu, wd, wq, gin)


def kernel_b(u_h, wd_h, h_h, dh2_h, dn2_h, a_h, b_h, g_h,
             e_o, da_o, db_o, n2_o, dres_o, home_o, dg_o, ux_o, ex_o,
             u_v, wd_v, h_v, dh2_v, dn2_v, a_v, b_v, gains, e_v, p_v, rbuf, res_v, n2_v, dres_v, dg_v, send, recv, local):
    dp, z, tx, peer = places()
    tokens, ff = u_v.shape
    sub, dim = h_v.shape
    dt = dim // 4
    tile = min(512, ff)
    dtile = min(512, dim)
    net = Wires(send, recv, local)
    loads = [net.here(u_h, u_v), net.here(wd_h, wd_v)]
    rows_in = [net.here(h_h, h_v), net.here(dn2_h, dn2_v), net.here(dh2_h, dh2_v), net.here(g_h, gains), net.here(a_h, a_v), net.here(b_h, b_v)]
    entry_barrier([{"tx": peer[1]}, {"tx": peer[2]}, {"tx": peer[3]}], z)
    far_first = (2, 3, 1)
    o_id = net.take(4)

    def o_cp(k, block):
        return net.copy(res_v.at[:, pl.ds(k * dt, dt)], home_o.at[ds(block * sub, sub), :], o_id + k, o_id + k, tx=peer[k])

    u_id, x_id = net.take(3), net.take(12)

    def ux_cp(k):
        src = ux_o.at[1] if k == 3 else u_h
        return net.copy(src, ux_o.at[k - 1], u_id + k - 1, u_id + k - 1, tx=peer[1] if k == 3 else peer[k])

    def ex_cp(k, b):
        i = x_id + (k - 1) * 4 + b
        rows = ds(b * sub, sub)
        return net.copy(e_v.at[rows, pl.ds(k * dt, dt)], ex_o.at[k - 1, rows, :], i, i, tx=peer[k])

    ux_cp(2).start()
    ux_cp(1).start()
    rsc = LineScatter(net, p_v, rbuf, sub, z)
    ag = LineGather(net, e_v, sub, z)
    for c in loads:
        c.wait()

    def down_block(b):
        @pl.loop(0, dim // dtile)
        def _(j):
            cols = ds(j * dtile, dtile)
            p_v[ds(b * sub, sub), cols] = dot(u_v[ds(b * sub, sub), :], wd_v[:, cols]).astype(BF16)

    for i in (2, 1, 0):
        down_block(ag.slots[i])
        rsc.send_end(i)
    down_block(z)
    for i in (2, 1, 0):
        rsc.send_mid(i)
    for c in rows_in:
        c.wait()
    rsc.finish()
    dg_v[...] = jnp.zeros_like(dg_v)
    step = 16

    def mlp(r):
        return p_v[ds(z * sub + r * step, step), :].astype(F32)

    def from_right(r):
        return rbuf[ds(z * sub + r * step, step), :].astype(F32)

    def from_left(r):
        return rbuf[ds(4 * sub + r * step, step), :].astype(F32)

    def norm_rows(total):
        @pl.loop(0, sub // step)
        def _(r):
            view = ds(r * step, step)
            resid = (h_v[view, :].astype(F32) + total(r)).astype(BF16)
            res_v[view, :] = resid
            x = resid.astype(F32)
            inv = lax.rsqrt(jnp.sum(x * x, axis=1, keepdims=True) / dim + NORM_EPS)
            xhat = x * inv
            gain = gains[1:2, :]
            n2_v[view, :] = (xhat * gain).astype(BF16)
            dy = dn2_v[view, :]
            part = dy * xhat
            dg_v[...] += part[:8] + part[8:]
            inner = jnp.sum(part * gain, axis=1, keepdims=True) / dim
            dres = dh2_v[view, :].astype(F32) + inv * (dy * gain) - xhat * (inv * inner)
            dres_v[view, :] = dres
            e_v[ds(z * sub + r * step, step), :] = dres.astype(BF16)

    @pl.when(z == 0)
    def _():
        norm_rows(lambda r: mlp(r) + from_right(r))

    @pl.when(z == 3)
    def _():
        norm_rows(lambda r: mlp(r) + from_left(r))

    @pl.when(mid(z))
    def _():
        norm_rows(lambda r: mlp(r) + from_right(r) + from_left(r))

    ag.start()
    for k in far_first:
        o_cp(k, tx).start()
    outs = [net.here(res_v.at[:, pl.ds(0, dt)], home_o.at[ds(tx * sub, sub), :]), net.here(n2_v, n2_o), net.here(dres_v, dres_o), net.here(dg_v, dg_o)]

    def back_block(b):
        rows = ds(b * sub, sub)

        @pl.loop(0, ff // tile)
        def _(j):
            cols = ds(j * tile, tile)
            du = dot(e_v[rows, :], wd_v[ds(j * tile, tile), :], NT_DIMS)
            aa = a_v[rows, cols].astype(F32)
            bb = b_v[rows, cols].astype(F32)
            sig = jax.nn.sigmoid(aa)
            a_v[rows, cols] = (du * bb * sig * (1.0 + aa * (1.0 - sig))).astype(BF16)
            b_v[rows, cols] = (du * aa * sig).astype(BF16)

    def spread(b):
        for k in far_first:
            ex_cp(k, b).start()

    spread(z)
    back_block(z)
    ag.step1()
    spread(ag.slots[0])
    back_block(ag.slots[0])
    ag.step2()
    spread(ag.slots[1])
    ux_cp(2).wait_recv()
    ux_cp(3).start()
    back_block(ag.slots[1])
    ag.step3()
    spread(ag.slots[2])
    back_block(ag.slots[2])
    outs += [net.here(e_v, e_o), net.here(a_v, da_o), net.here(b_v, db_o)]
    for k in far_first:
        o_cp(k, peer[k]).wait_recv()
        for b in range(4):
            ex_cp(k, b).wait_recv()
    ux_cp(1).wait_recv()
    ux_cp(3).wait_recv()
    for c in outs:
        c.wait()
    for k in far_first:
        o_cp(k, tx).wait_send()
        ux_cp(k).wait_send()
        for b in range(4):
            ex_cp(k, b).wait_send()
    ag.drain()
    rsc.drain()


def call_b(u, wd, h, dh2, dn2, a, b, gains):
    tokens, ff = u.shape
    sub, dim = h.shape
    s = jax.ShapeDtypeStruct
    shapes = (s((tokens, dim), BF16), s((tokens, ff), BF16), s((tokens, ff), BF16), s((sub, dim), BF16), s((sub, dim), F32),
              s((tokens, dim // 4), BF16), s((8, dim), F32), s((3, tokens, ff), BF16), s((3, tokens, dim // 4), BF16))
    return pl.pallas_call(
        kernel_b, out_shape=shapes, in_specs=[ANY] * 8, out_specs=[ANY] * len(shapes),
        scratch_shapes=[
            VMEM((tokens, ff), BF16), VMEM((ff, dim), BF16), VMEM((sub, dim), BF16), VMEM((sub, dim), BF16), VMEM((sub, dim), F32),
            VMEM((tokens, ff), BF16), VMEM((tokens, ff), BF16), VMEM((8, dim), F32), VMEM((tokens, dim), BF16), VMEM((tokens, dim), BF16),
            VMEM((5 * sub, dim), BF16), VMEM((sub, dim), BF16), VMEM((sub, dim), BF16), VMEM((sub, dim), F32), VMEM((8, dim), F32),
            pltpu.SemaphoreType.DMA((40,)), pltpu.SemaphoreType.DMA((40,)), pltpu.SemaphoreType.DMA((20,))],
        compiler_params=pltpu.CompilerParams(collective_id=1, has_side_effects=True, vmem_limit_bytes=VMEM_LIMIT),
        cost_estimate=pl.CostEstimate(flops=20 * tokens * dim * ff, bytes_accessed=60000000, transcendentals=0), name="phase_b",
    )(u, wd, h, dh2, dn2, a, b, gains)


ROWS_ROWS = (((0,), (0,)), ((), ()))


class GradReduce:
    def __init__(self, net, peer, tile, tiles, st3, st1, cross, stage, got2, got0, got_y, out, out_tiles):
        self.net, self.peer, self.tile, self.tiles = net, peer, tile, tiles
        self.st3, self.st1, self.cross, self.stage = st3, st1, cross, stage
        self.got2, self.got0, self.got_y, self.out, self.out_tiles = got2, got0, got_y, out, out_tiles
        self.base = net.take(3)
        self.w = out.shape[1] // tiles

    def cp(self, i):
        src, dst, to = ((self.st3, self.got2, 1), (self.st1, self.got0, 1), (self.cross, self.got_y, 2))[i]
        return self.net.copy(src, dst, self.base + i, self.base + i, tx=self.peer[to])

    def fill(self, k, ref):
        @pl.loop(0, self.tiles)
        def _(j):
            ref[:, ds(j * self.w, self.w)] = self.tile(k, j).astype(BF16)

    def step3(self):
        self.fill(3, self.st3)
        self.cp(0).start()

    def step1(self):
        self.fill(1, self.st1)
        self.cp(1).start()

    def step2(self):
        self.cp(0).wait_recv()
        self.net.here(self.got2, self.stage).wait()

        @pl.loop(0, self.tiles)
        def _(j):
            cols = ds(j * self.w, self.w)
            self.cross[:, cols] = (self.tile(2, j) + self.stage[:, cols].astype(F32)).astype(BF16)

        self.cp(2).start()

    def step0(self):
        self.cp(1).wait_recv()
        self.net.here(self.got0, self.stage).wait()
        for j in range(self.tiles):
            cols = pl.ds(j * self.w, self.w)
            if j >= 2:
                self.copies[j - 2].wait()
            else:
                if j == 0:
                    self.copies = []
            place = self.out_tiles.at[j % 2, :, pl.ds(0, self.w)]
            self.out_tiles[j % 2, :, pl.ds(0, self.w)] = self.tile(0, j) + self.stage[:, cols].astype(F32)
            self.copies.append(self.net.here(place, self.out.at[:, cols]))
        for c in self.copies[-2:]:
            c.wait()

    def sent_locally(self):
        self.cp(0).wait_send()
        self.cp(1).wait_send()

    def finish(self):
        self.cp(2).wait_send()
        self.cp(2).wait_recv()


def kernel_c(q_width, da_h, db_h, wg_h, wu_h, n_h, u_h, ux_h, e_h, ex_h, n2_h, eq_h, wq_h, h_h, dres_h, g_h, dga_h, cosh, sinh, swaph,
             wgo, wgy, wuo, wuy, wdo, wqo, wqy, q_o, dh_o, dg_o, g2, g0, u2, u0, q2, q0, qx,
             wg_v, wu_v, da_v, db_v, n_v, p_v, rbuf, n2_v, st3, st1, cross_g, cross_u, stage, tiles_v, dres_v, wq_v, eq_v,
             gains, dg_v, dgr, dgz, cos_v, sin_v, swap_v, send, recv, local):
    dp, z, tx, peer = places()
    tokens, ff = da_v.shape
    sub, dim = dres_v.shape
    dt = dim // 4
    width = eq_v.shape[1]
    tile = ff // 4
    dtile = min(512, dim)
    qt = min(256, tile)
    far_first = (2, 3, 1)
    net = Wires(send, recv, local)
    n2_in = net.here(n2_h, n2_v.at[ds(z * sub, sub), :])
    first = [net.here(n_h, n_v), net.here(da_h, da_v)]
    second = [net.here(db_h, db_v), net.here(wg_h, wg_v), net.here(wu_h, wu_v)]
    third = [net.here(wq_h, wq_v), net.here(eq_h, eq_v), net.here(dres_h, dres_v), net.here(g_h, gains),
             net.here(dga_h, dg_v.at[pl.ds(8, 8), :]), net.here(cosh, cos_v), net.here(sinh, sin_v), net.here(swaph, swap_v)]
    sem = pltpu.get_barrier_semaphore()
    zs = tuple((z + i) % 4 for i in range(4))
    for i in (1, 2, 3):
        pl.semaphore_signal(sem, inc=1, device_id={"tx": peer[i]}, device_id_type=MESH)
        pl.semaphore_signal(sem, inc=1, device_id={"ty": zs[i]}, device_id_type=MESH)
    pl.semaphore_wait(sem, 6)
    rsc = LineScatter(net, p_v, rbuf, sub, z)
    ag = LineGather(net, n2_v, sub, z)
    q_id, h_id, t_id, z_id = net.take(4), net.take(4), net.take(4), net.take(4)

    def grad_tile(lhs, rhs, w):
        def go(k, j):
            cols = pl.ds(j * w, w) if isinstance(j, int) else ds(j * w, w)
            return dot(lhs[:, pl.ds(k * dt, dt)], rhs[:, cols], ROWS_ROWS)
        return go

    gate = GradReduce(net, peer, grad_tile(n_v, da_v, tile), ff // tile, st3, st1, cross_g, stage, g2, g0, wgy, wgo, tiles_v)
    up = GradReduce(net, peer, grad_tile(n_v, db_v, tile), ff // tile, st3, st1, cross_u, stage, u2, u0, wuy, wuo, tiles_v)
    half = tokens // 2

    def corner(r, c):
        return da_v.at[pl.ds(r * dt, dt), pl.ds(c * width, width)]

    qkv = GradReduce(net, peer, grad_tile(n2_v, eq_v, qt), width // qt, corner(0, 0), corner(1, 0), corner(0, 1), corner(1, 1),
                     q2, q0, wqy, wqo, tiles_v)

    def dn_block(b):
        rows = ds(b * sub, sub)

        @pl.loop(0, dim // dtile)
        def _(j):
            wr = ds(j * dtile, dtile)
            p_v[rows, wr] = (dot(da_v[rows, :], wg_v[wr, :], NT_DIMS) + dot(db_v[rows, :], wu_v[wr, :], NT_DIMS)).astype(BF16)

    n2_in.wait()
    ag.start()
    for c in first:
        c.wait()
    gate.step3()
    gate.step1()
    gate.step2()
    for c in second:
        c.wait()
    dn_block(ag.slots[2])
    rsc.send_end(2)
    ag.step1()
    dn_block(ag.slots[1])
    rsc.send_end(1)
    dn_block(ag.slots[0])
    rsc.send_end(0)
    rsc.send_mid(2)
    dn_block(z)
    gate.step0()
    gate.sent_locally()
    up.step3()
    up.step1()
    ag.step2()
    up.step2()
    rsc.send_mid(1)
    rsc.send_mid(0)

    e_in = [net.here(e_h.at[:, pl.ds(0, dt)], wu_v.at[pl.ds(0, tokens), pl.ds(0, dt)])]
    for k in (1, 2, 3):
        e_in.append(net.here(ex_h.at[k - 1], wu_v.at[pl.ds(0, tokens), pl.ds(k * dt, dt)]))

    def u_place(j, k):
        return wg_v.at[pl.ds((j % 2) * tokens, tokens), pl.ds(k * tile, tile)]

    def u_load(j):
        cols = pl.ds(j * tile, tile)
        return [net.here(u_h.at[:, cols] if k == 0 else ux_h.at[k - 1, :, cols], u_place(j, k)) for k in range(4)]

    def down_tile(j, slot, loads):
        for c in loads:
            c.wait()
        acc = None
        for k in range(4):
            part = dot(u_place(j, k)[...], wu_v[pl.ds(0, tokens), pl.ds(k * dt, dt)], ROWS_ROWS)
            acc = part if acc is None else acc + part
        tiles_v[slot, pl.ds(0, tile), pl.ds(0, dt)] = acc
        return net.here(tiles_v.at[slot, pl.ds(0, tile), pl.ds(0, dt)], wdo.at[pl.ds(j * tile, tile), :])

    up.step0()
    up.sent_locally()
    h_in = net.here(h_h, st3.at[pl.ds(0, sub), :])
    n_tiles = ff // tile
    loads = {0: u_load(0)}
    if n_tiles > 1:
        loads[1] = u_load(1)
    for c in e_in:
        c.wait()
    done = {0: down_tile(0, 0, loads[0])}
    if n_tiles > 1:
        done[1] = down_tile(1, 1, loads[1])
    for c in third:
        c.wait()
    ag.step3()

    @pl.loop(0, 4)
    def _(b):
        rows = ds(b * sub, sub)

        @pl.loop(0, width // qt)
        def _(j):
            cols = ds(j * qt, qt)
            n_v[rows, cols] = dot(n2_v[rows, :], wq_v[:, cols]).astype(BF16)

    def q_cp(k, block):
        return net.copy(n_v.at[ds(peer[k] * sub, sub), pl.ds(0, width)], qx.at[ds(block * sub, sub), :], q_id + k, q_id + k, tx=peer[k])

    for k in far_first:
        q_cp(k, tx).start()
    q_own = net.here(n_v.at[ds(tx * sub, sub), pl.ds(0, width)], qx.at[ds(tx * sub, sub), :])
    for c in done.values():
        c.wait()
    qkv.step3()
    qkv.step1()
    qkv.step2()
    h_in.wait()
    rsc.finish()
    dg_v[pl.ds(0, 8), :] = jnp.zeros((8, dim), F32)
    step = 16

    def norm_rows(right, left):
        @pl.loop(0, sub // step)
        def _(r):
            view = ds(r * step, step)
            dy = p_v[ds(z * sub + r * step, step), :].astype(F32)
            if right:
                dy += rbuf[ds(z * sub + r * step, step), :].astype(F32)
            if left:
                dy += rbuf[ds(4 * sub + r * step, step), :].astype(F32)
            x = st3[view, :].astype(F32)
            inv = lax.rsqrt(jnp.sum(x * x, axis=1, keepdims=True) / dim + NORM_EPS)
            xhat = x * inv
            gain = gains[0:1, :]
            part = dy * xhat
            dg_v[pl.ds(0, 8), :] += part[:8] + part[8:]
            inner = jnp.sum(part * gain, axis=1, keepdims=True) / dim
            db_v[view, :] = (dres_v[view, :] + inv * (dy * gain) - xhat * (inv * inner)).astype(BF16)

    @pl.when(z == 0)
    def _():
        norm_rows(True, False)

    @pl.when(z == 3)
    def _():
        norm_rows(False, True)

    @pl.when(mid(z))
    def _():
        norm_rows(True, True)

    def h_cp(k, block):
        return net.copy(db_v.at[pl.ds(0, sub), pl.ds(k * dt, dt)], dh_o.at[ds(block * sub, sub), :], h_id + k, h_id + k, tx=peer[k])

    def t_cp(k):
        return net.copy(dg_v.at[:, pl.ds(k * dt, dt)], dgr.at[k], t_id + k, t_id + k, tx=peer[k])

    def z_cp(i):
        return net.copy(dgr.at[0], dgz.at[i], z_id + i, z_id + i, ty=zs[i])

    for k in far_first:
        t_cp(k).start()
    for k in far_first:
        h_cp(k, tx).start()
    h_own = net.here(db_v.at[pl.ds(0, sub), pl.ds(0, dt)], dh_o.at[ds(tx * sub, sub), :])
    qkv.step0()
    for j in range(2, n_tiles):
        loads[j] = u_load(j)
    done = [down_tile(j, j % 2, loads[j]) for j in range(2, n_tiles)]
    for k in far_first:
        q_cp(k, peer[k]).wait_recv()
    q_own.wait()
    net.here(qx, n_v.at[:, pl.ds(width, width)]).wait()
    turned = n_v.at[:, pl.ds(width, width)]
    turn(turned, turned, tokens, width, q_width, cos_v, sin_v, swap_v, False)
    q_out = net.here(turned, q_o)
    for k in far_first:
        t_cp(k).wait_recv()
    dgr[0] = dg_v[:, pl.ds(0, dt)] + dgr[1] + dgr[2] + dgr[3]
    for i in (1, 2, 3):
        z_cp(i).start()
    for i in (1, 2, 3):
        z_cp(i).wait_recv()
    dgz[0] = dgr[0] + dgz[1] + dgz[2] + dgz[3]
    dg_out = net.here(dgz.at[0], dg_o)
    for k in far_first:
        h_cp(k, peer[k]).wait_recv()
    for c in done + [q_out, dg_out, h_own]:
        c.wait()
    gate.finish()
    up.finish()
    qkv.sent_locally()
    qkv.finish()
    for k in far_first:
        q_cp(k, tx).wait_send()
        h_cp(k, tx).wait_send()
        t_cp(k).wait_send()
        z_cp(k).wait_send()
    ag.drain()
    rsc.drain()


def call_c(q_width, *args):
    tokens, ff = args[0].shape
    sub, dim = args[9].shape
    dt, width = dim // 4, args[10].shape[1]
    tile = ff // 4
    s = jax.ShapeDtypeStruct
    wf, wb = s((dt, ff), F32), s((dt, ff), BF16)
    qf, qb = s((dt, width), F32), s((dt, width), BF16)
    shapes = (wf, wb, wf, wb, s((ff, dt), F32), qf, qb, s((tokens, width), BF16), s((tokens, dt), BF16), s((16, dt), F32),
              wb, wb, wb, wb, qb, qb, s((tokens, width), BF16))
    return pl.pallas_call(
        functools.partial(kernel_c, q_width), out_shape=shapes, in_specs=[ANY] * len(args), out_specs=[ANY] * len(shapes),
        scratch_shapes=[
            VMEM((dim, ff), BF16), VMEM((dim, ff), BF16), VMEM((tokens, ff), BF16), VMEM((tokens, ff), BF16), VMEM((tokens, dim), BF16),
            VMEM((tokens, dim), BF16), VMEM((5 * sub, dim), BF16), VMEM((tokens, dim), BF16),
            VMEM((dt, ff), BF16), VMEM((dt, ff), BF16), VMEM((dt, ff), BF16), VMEM((dt, ff), BF16), VMEM((dt, ff), BF16),
            VMEM((2, max(dt, tile), max(dt, tile)), F32), VMEM((sub, dim), F32), VMEM((dim, width), BF16), VMEM((tokens, width), BF16),
            VMEM((8, dim), F32), VMEM((16, dim), F32), VMEM((4, 16, dt), F32), VMEM((4, 16, dt), F32), VMEM((2 * tokens, 128), F32), VMEM((2 * tokens, 128), F32), VMEM((128, 128), BF16),
            pltpu.SemaphoreType.DMA((48,)), pltpu.SemaphoreType.DMA((48,)), pltpu.SemaphoreType.DMA((72,))],
        compiler_params=pltpu.CompilerParams(collective_id=2, has_side_effects=True, vmem_limit_bytes=VMEM_LIMIT),
        cost_estimate=pl.CostEstimate(flops=20 * tokens * dim * ff, bytes_accessed=100000000, transcendentals=0), name="phase_c",
    )(*args)


def solution(mesh):
    def local_step(hidden, positions, g_ffn, w_gate, w_up, w_down, g_attn, w_q, w_kv, grad_h2, grad_q, grad_kv):
        tokens, dt = hidden.shape
        q_heads, head_dim = w_q.shape[1:]
        kv_heads = w_kv.shape[1]
        q_width, kv_width = q_heads * head_dim, kv_heads * head_dim
        width = q_width + kv_width

        lane = jnp.arange(128)
        inv_freq = ROPE_BASE ** (-((lane % head_dim) // 2 * 2).astype(F32) / head_dim)
        angles = positions.astype(F32)[:, None] * inv_freq[None, :]
        turned = jnp.where(lax.axis_index("ty") < mesh.shape["ty"] // 2, angles, 0.0)
        angles = jnp.concatenate([angles, turned])
        cos_t = jnp.cos(angles)
        swap = (lane[:, None] == (lane + 1 - lane % 2 * 2)[None, :]).astype(BF16)
        sin_t = jnp.sin(angles) * jnp.where(lane % 2 == 0, -1.0, 1.0)[None, :]

        back = jnp.concatenate([grad_q.reshape(tokens, q_width), grad_kv.reshape(tokens, kv_width)], axis=1)
        w_qkv_own = jnp.concatenate([w_q.reshape(dt, q_width), w_kv.reshape(dt, kv_width)], axis=1)
        gin = jnp.concatenate([jnp.stack([g_ffn, g_attn]).astype(F32), jnp.zeros((6, dt), F32)])

        (normed_all, a_all, b_all, u_all, gate_w, up_w, down_w, w_qkv, back_all, h_rows, dh2_rows, dn2_rows, gains) = call_a(
            q_width, hidden, back, cos_t, sin_t, swap, grad_h2, w_gate, w_up, w_down, w_qkv_own, gin)
        res_all, grad_gate, grad_up, normed2, grad_res, resid_out, gattn8, u_other, e_other = call_b(
            u_all, down_w, h_rows, dh2_rows, dn2_rows, a_all, b_all, gains)
        (wg_own, wg_far, wu_own, wu_far, grad_wdown, wq_own, wq_far, qkv_out, grad_hidden, gain_grads, *_) = call_c(
            q_width, grad_gate, grad_up, gate_w, up_w, normed_all, u_all, u_other, res_all, e_other, normed2, back_all, w_qkv,
            h_rows, grad_res, gains, gattn8, cos_t, sin_t, swap)
        grad_wgate = wg_own + wg_far.astype(F32)
        grad_wup = wu_own + wu_far.astype(F32)
        grad_wqkv = wq_own + wq_far.astype(F32)
        grad_wq = grad_wqkv[:, :q_width].reshape(dt, q_heads, head_dim)
        grad_wkv = grad_wqkv[:, q_width:].reshape(dt, kv_heads, head_dim)
        q_out = qkv_out[:, :q_width].reshape(tokens, q_heads, head_dim)
        kv_out = qkv_out[:, q_width:].reshape(tokens, kv_heads, head_dim)
        grad_gffn = jnp.sum(gain_grads[:8], axis=0)
        grad_gattn = jnp.sum(gain_grads[8:], axis=0)
        return (resid_out, q_out, kv_out, grad_hidden, grad_gffn, grad_gattn, grad_wgate, grad_wup, grad_wdown, grad_wq, grad_wkv)

    row_spec = P(("dp", "ty"), "tx")
    head_spec = P(("dp", "tx"), "ty", None)
    in_specs = (row_spec, P(("dp", "tx")), P("tx"), P("tx", "ty"), P("tx", "ty"), P("ty", "tx"), P("tx"), P("tx", "ty", None), P("tx", "ty", None), row_spec, head_spec, head_spec)
    out_specs = (row_spec, head_spec, head_spec, row_spec, P(("dp", "tx")), P(("dp", "tx")), P(("dp", "tx"), "ty"), P(("dp", "tx"), "ty"), P(("dp", "ty"), "tx"), head_spec, head_spec)
    return jax.shard_map(local_step, mesh=mesh, in_specs=in_specs, out_specs=out_specs, check_vma=False)
```

profile of v0, /device:TPU:0, one launch (start us, length us, event | category | flops | bytes accessed | tf_op | source)
XLA Modules:
  0.0 535.9 jit_solution(11583856529613019244)
XLA Ops:
  0.7 0.7 stack.9
  2.1 0.7 convert_element_type.25
  4.0 1.1 copy.34
  5.1 1.3 copy.33
  6.4 0.9 pad_maximum_fusion.2.wq
  7.8 4.8 sine_multiply_fusion
  13.1 1.2 pad_maximum_fusion.eqh
  14.3 157.8 %phase_a.1 = (bf16[1024,2048]{1,0:T(8,128)(2,1)}, bf16[1024,2048]{1,0:T(8,128)(2,1)}, bf16[1024,2048]{1,0:T(8,128)(2,1)}, bf16[1024,2048]{1,0:T(8,128)(2,1)}, bf...) custom-call(bf16[1024,512]{1,0:T(8,128)(2,1)} %hid.1, ...), custom_call_target="tpu_custom_call" | custom-call | flops 85899345920 | bytes 100000000 | tf_op jit(solution)/shard_map/phase_a/pallas_call | solution.py:482
  172.1 160.9 %phase_b.1 = (bf16[1024,2048]{1,0:T(8,128)(2,1)}, bf16[1024,2048]{1,0:T(8,128)(2,1)}, bf16[1024,2048]{1,0:T(8,128)(2,1)}, bf16[256,2048]{1,0:T(8,128)(2,1)}, f32...) custom-call(bf16[1024,2048]{1,0:T(8,128)(2,1)} %get-tuple-element.43, ...), custom_call_target="tpu_custom_call" | custom-call | flops 85899345920 | bytes 60000000 | tf_op jit(solution)/shard_map/phase_b/pallas_call | solution.py:648
  332.9 176.1 %phase_c.1 = (f32[512,2048]{1,0:T(8,128)}, bf16[512,2048]{1,0:T(8,128)(2,1)}, f32[512,2048]{1,0:T(8,128)}, bf16[512,2048]{1,0:T(8,128)(2,1)}, f32[2048,512]{1,0:...) custom-call(bf16[1024,2048]{1,0:T(8,128)(2,1)} %get-tuple-element.52, ...), custom_call_target="tpu_custom_call" | custom-call | flops 85899345920 | bytes 100000000 | tf_op jit(solution)/shard_map/phase_c/pallas_call | solution.py:957
  509.1 1.3 slice_reduce_fusion
  510.4 1.2 slice.19
  511.6 1.3 slice.18
  512.9 1.3 copy.35
  514.2 1.0 copy.36
  515.2 1.3 convert_add_fusion.2
  516.5 0.8 slice.25
  517.4 1.3 copy.37
  518.8 2.0 copy.38
  520.8 9.7 %convert_add_fusion = (f32[512,2048]{1,0:T(8,128)}, f32[512,2048]{1,0:T(8,128)}) fusion(f32[512,2048]{1,0:T(8,128)} %get-tuple-element.70, bf16[512,2048]{1,0:T(8,128)(2,1)} %get-tuple-element.71, f32[512,2048]{1,0:T(8,128)} %get-tuple-element.68, bf16[512,2048]{1,0:T(8,128)(2,1)S(1)} %copy-done.1), kind=kLoop, calls=%fused_computation | loop fusion | flops 4194304 | bytes 20971520 | tf_op jit(solution)/shard_map/add | solution.py:1000
  530.5 1.0 copy.42
  531.4 1.0 copy.43
  532.4 1.0 copy-done
  533.4 2.0 copy.44
  (23 shorter events, 3.0 us)
Async XLA Ops:
  0.6 6.7 %copy-start.6 = (bf16[1024,4,64]{0,2,1:T(8,128)(2,1)S(1)}, bf16[1024,4,64]{0,2,1:T(8,128)(2,1)}, u32[]{:S(2)}) copy-start(bf16[1024,4,64]{0,2,1:T(8,128)(2,1)} %param.23) | copy-start | bytes 1572868
  6.4 6.1 %copy-start.3 = (bf16[1024,8,64]{0,2,1:T(8,128)(2,1)S(1)}, bf16[1024,8,64]{0,2,1:T(8,128)(2,1)}, u32[]{:S(2)}) copy-start(bf16[1024,8,64]{0,2,1:T(8,128)(2,1)} %param.22) | copy-start | bytes 3145732
  510.4 4.8 copy-start.2
  516.5 4.3 copy-start.1
  520.8 9.7 %copy-start.4 = (bf16[1024,512]{1,0:T(8,128)(2,1)S(1)}, bf16[1024,512]{1,0:T(8,128)(2,1)}, u32[]{:S(2)}) copy-start(bf16[1024,512]{1,0:T(8,128)(2,1)} %get-tuple-element.105) | copy-start | bytes 3145732
  520.8 10.6 %copy-start.5 = (bf16[1024,512]{1,0:T(8,128)(2,1)S(1)}, bf16[1024,512]{1,0:T(8,128)(2,1)}, u32[]{:S(2)}) copy-start(bf16[1024,512]{1,0:T(8,128)(2,1)} %get-tuple-element.108) | copy-start | bytes 3145732
  530.5 2.9 copy-start
where the time goes:
time: 544 us; the launch traced here: 536 us
  Pallas kernels  495 us (91%)
  other arithmetic  21.4 us (4%)
  local copies, waits for them, and re-layouts  18.6 us (3%)
    pallas_call x1, Pallas kernels, call_c(): pl.pallas_call(functools.partial(kernel_c, q_width), out_shape=shapes, in...  176 us
    pallas_call x1, Pallas kernels, call_b(): pl.pallas_call(kernel_b, out_shape=shapes, in_specs=[ANY] * 8, out_specs=...  161 us
    pallas_call x1, Pallas kernels, call_a(): pl.pallas_call(functools.partial(kernel_a, q_width), out_shape=shapes, in...  158 us

commit v1 on v0

--- a/solution.py
+++ b/solution.py
@@ -42,17 +42,17 @@
     return (z + 1 - 2 * (z % 2), 2 - z // 2, 3 - 3 * (z // 2))
 
 
-def turn(src, dst, rows, width, q_width, cos_ref, sin_ref, swap_ref, back):
-    step = min(256, rows)
-
-    @pl.loop(0, rows // step)
+def turn(src, dst, rows, width, q_width, table_ref, swap_ref, back):
+    step = rows // 4
+
+    @pl.loop(0, 4)
     def _(r):
         for c in range(width // 128):
             cols = pl.ds(c * 128, 128)
-            table = ds(r * step + (0 if c * 128 < q_width else rows), step, step)
+            table = ds(r * 128 + (0 if c * 128 < q_width else 512), 128)
             x = src[ds(r * step, step), cols]
-            main = x.astype(F32) * cos_ref[table, :]
-            side = dot(x, swap_ref[...]) * sin_ref[table, :]
+            main = x.astype(F32) * table_ref[:, table]
+            side = dot(x, swap_ref[...]) * table_ref[:, ds(r * 128 + (1024 if c * 128 < q_width else 1536), 128)]
             dst[ds(r * step, step), cols] = (main - side if back else main + side).astype(BF16)
 
 
@@ -105,13 +105,13 @@
 
 
 class LineGather:
-    def __init__(self, net, buf, rows, z):
-        self.net, self.buf, self.rows, self.z = net, buf, rows, z
+    def __init__(self, net, buf, rows, z, off=0, part=None):
+        self.net, self.buf, self.rows, self.z, self.off, self.part = net, buf, rows, z, off, part or rows
         self.base = net.take(8)
         self.slots = slots(z)
 
     def blk(self, b):
-        return self.buf.at[ds(b * self.rows, self.rows), :]
+        return self.buf.at[ds(b * self.rows + self.off, self.part), :]
 
     def cp(self, b, side, target):
         return self.net.copy(self.blk(b), self.blk(b), self.base + side * 4 + b, self.base + b, ty=target)
@@ -150,12 +150,16 @@
         def _():
             self.take(1)
 
-    def step3(self):
-        self.take(2)
-
+    def step3_mid(self):
         @pl.when(mid(self.z))
         def _():
+            self.take(2)
             self.forward(2)
+
+    def step3_end(self):
+        @pl.when(end(self.z))
+        def _():
+            self.take(2)
 
     def drain(self):
         z = self.z
@@ -175,8 +179,8 @@
 
 
 class LineScatter:
-    def __init__(self, net, part, rbuf, rows, z):
-        self.net, self.part, self.rbuf, self.rows, self.z = net, part, rbuf, rows, z
+    def __init__(self, net, part, rbuf, rows, z, off=0, size=None):
+        self.net, self.part, self.rbuf, self.rows, self.z, self.off, self.size = net, part, rbuf, rows, z, off, size or rows
         self.base = net.take(5)
         self.slots = slots(z)
         one = (z % 2) * (1 - z // 2)
@@ -185,11 +189,14 @@
 
     def cp(self, i):
         return self.net.copy(
-            self.part.at[ds(self.slots[i] * self.rows, self.rows), :], self.rbuf.at[ds(self.dst[i] * self.rows, self.rows), :],
+            self.part.at[self.view(self.slots[i]), :], self.rbuf.at[self.view(self.dst[i]), :],
             self.base + i, self.base + self.dst[i], ty=self.target[i])
 
+    def view(self, b):
+        return ds(b * self.rows + self.off, self.size)
+
     def wait_slot(self, s):
-        view = self.rbuf.at[ds(s * self.rows, self.rows), :]
+        view = self.rbuf.at[self.view(s), :]
         self.net.copy(view, view, self.base, self.base + s, ty=self.z).wait_recv()
 
     def send_end(self, i):
@@ -202,11 +209,11 @@
         def _():
             b = self.slots[i]
             self.wait_slot(b)
-            step = min(32, self.rows)
-
-            @pl.loop(0, self.rows // step)
+            step = 16
+
+            @pl.loop(0, self.size // step)
             def _(r):
-                view = ds(b * self.rows + r * step, step, step)
+                view = ds(b * self.rows + self.off + r * step, step)
                 self.part[view, :] = (self.part[view, :].astype(F32) + self.rbuf[view, :].astype(F32)).astype(BF16)
 
             self.cp(i).start()
@@ -301,24 +308,29 @@
     return dp, z, tx, (tx, tx + 1 - 2 * (tx % 2), (tx + 2) % 4, 3 - tx)
 
 
-def kernel_a(q_width, hid, eqh, cosh, sinh, swaph, dh2h, wg, wu, wd, wq, gin,
-             n_o, a_o, b_o, u_o, wg_o, wu_o, wd_o, wq_o, eq_o, h_o, dh2_o, dn2_o, g_o,
-             rows, n_v, a_v, b_v, u_v, wg_v, wu_v, wq_v, eq_v, p_v, rbuf, gains, dn2_v, cos_v, sin_v, swap_v, send, recv, local):
+def kernel_ab(q_width, hid, eqh, tabh, swaph, dh2h, wg, wu, wd, wq, gin,
+              n_o, da_o, db_o, u_o, wg_o, wu_o, wq_o, eq_o, h_o, g_o, e_o, n2_o, dres_o, home_o, dg_o, ux_o, ex_o,
+              rows, dh2_v, n2_v, res_v, dres_v, n_v, a_v, b_v, wg_v, wu_v, wd_v, wq_v, eq_v, p_v, rbuf, rbuf2, gains, dg_v, swap_v, send, recv, local):
     dp, z, tx, peer = places()
     sub, dim = rows.shape
+    tokens = 4 * sub
     width = eq_v.shape[1]
     dt = dim // 4
     ff = wg.shape[1]
+    wide = min(1024, ff)
     tile = min(512, ff)
+    dwide = min(1024, dim)
     dtile = min(512, dim)
+    hs = sub // 2
     net = Wires(send, recv, local)
-    eq_raw = p_v.at[:, pl.ds(0, width)]
-    turn_in = [net.here(eqh, eq_raw), net.here(cosh, cos_v), net.here(sinh, sin_v), net.here(swaph, swap_v)]
+    turn_in = [net.here(eqh, p_v.at[:, pl.ds(0, width)]), net.here(tabh, dres_v), net.here(swaph, swap_v)]
     entry_barrier([{"tx": peer[1]}, {"tx": peer[2]}, {"tx": peer[3]}, {"dp": 1 - dp}], z)
 
     pos = (dp, peer[1], peer[2])
     far_first = (2, 3, 1)
-    g_id, h_id, e_id, d_id = net.take(4), net.take(4), net.take(4), net.take(4)
+    g_id, h_id, e_id, d_id, o_id, u_id, x_id = (net.take(4), net.take(4), net.take(4), net.take(4), net.take(4), net.take(3), net.take(24))
+    u_v = wg_v.at[pl.ds(0, tokens), :]
+    e_v = wg_v.at[pl.ds(tokens, tokens), :]
 
     def g_cp(k):
         return net.copy(gin, gains.at[:, pl.ds(k * dt, dt)], g_id + k, g_id + k, tx=peer[k])
@@ -330,14 +342,28 @@
         return net.copy(p_v.at[ds(peer[k] * sub, sub), pl.ds(0, width)], eq_v.at[ds(block * sub, sub), :], e_id + k, e_id + k, tx=peer[k])
 
     def d_cp(k):
-        return net.copy(dh2h.at[ds(peer[k] * sub, sub), :], dh2_o.at[:, pl.ds(k * dt, dt)], d_id + k, d_id + k, tx=peer[k])
+        return net.copy(dh2h.at[ds(peer[k] * sub, sub), :], dh2_v.at[:, pl.ds(k * dt, dt)], d_id + k, d_id + k, tx=peer[k])
+
+    def o_cp(k, block):
+        return net.copy(res_v.at[:, pl.ds(k * dt, dt)], home_o.at[ds(block * sub, sub), :], o_id + k, o_id + k, tx=peer[k])
+
+    def ux_cp(k):
+        src = ux_o.at[1] if k == 3 else u_v
+        return net.copy(src, ux_o.at[k - 1], u_id + k - 1, u_id + k - 1, tx=peer[1] if k == 3 else peer[k])
+
+    def ex_cp(k, b, half):
+        i = x_id + half * 12 + (k - 1) * 4 + b
+        view = ds(b * sub + half * hs, hs)
+        return net.copy(wg_v.at[ds(tokens + b * sub + half * hs, hs), pl.ds(k * dt, dt)], ex_o.at[k - 1, view, :], i, i, tx=peer[k])
 
     gate = WeightGather(net, wg, wg_v, pos, True, 2)
     up = WeightGather(net, wu, wu_v, pos, True, 2)
-    down = WeightGather(net, wd, wd_o, pos, False, 2)
+    down = WeightGather(net, wd, wd_v, pos, False, 2)
     qkv = WeightGather(net, wq, wq_v, pos, True, 1)
     ag = LineGather(net, n_v, sub, z)
     rsc = LineScatter(net, p_v, rbuf, sub, z)
+    rs2 = [LineScatter(net, n_v, rbuf2, sub, z, h * hs, hs) for h in range(2)]
+    ag2 = [LineGather(net, e_v, sub, z, h * hs, hs) for h in range(2)]
 
     for k in far_first:
         g_cp(k).start()
@@ -345,9 +371,11 @@
         h_cp(k).start()
     g_own = net.here(gin, gains.at[:, pl.ds(0, dt)])
     h_own = net.here(hid.at[ds(tx * sub, sub), :], rows.at[:, pl.ds(0, dt)])
+    for w in (qkv, gate, up, down):
+        w.start_local()
     for c in turn_in:
         c.wait()
-    turn(p_v, p_v, 4 * sub, width, q_width, cos_v, sin_v, swap_v, True)
+    turn(p_v, p_v, tokens, width, q_width, dres_v, swap_v, True)
     for k in far_first:
         e_cp(k, tx).start()
     e_own = net.here(p_v.at[ds(tx * sub, sub), pl.ds(0, width)], eq_v.at[ds(tx * sub, sub), :])
@@ -355,9 +383,7 @@
         w.start_y()
     for k in far_first:
         d_cp(k).start()
-    for w in (qkv, gate, up, down):
-        w.start_local()
-    d_own = net.here(dh2h.at[ds(tx * sub, sub), :], dh2_o.at[:, pl.ds(0, dt)])
+    d_own = net.here(dh2h.at[ds(tx * sub, sub), :], dh2_v.at[:, pl.ds(0, dt)])
 
     for k in far_first:
         g_cp(k).wait_recv()
@@ -371,290 +397,245 @@
         inv = lax.rsqrt(jnp.sum(x * x, axis=1, keepdims=True) / dim + NORM_EPS)
         n_v[ds(z * sub + r * 16, 16), :] = (x * inv * gains[0:1, :]).astype(BF16)
 
+    ag.start()
     outs = [net.here(rows, h_o), net.here(gains, g_o)]
-    ag.start()
     for k in far_first:
         e_cp(k, peer[k]).wait_recv()
     e_own.wait()
     ag.step1()
     qkv.y_event(0)
-    gate.y_event(0)
     qkv.x_event(0)
     qkv.finish()
     for k in far_first:
         e_cp(k, tx).wait_send()
 
-    @pl.loop(0, 4)
-    def _(b):
+    def n2_block(b):
         @pl.loop(0, dim // dtile)
         def _(j):
             w = wq_v[ds(j * dtile, dtile), :]
             p_v[ds(b * sub, sub), ds(j * dtile, dtile)] = dot(eq_v[ds(b * sub, sub), :], w, NT_DIMS).astype(BF16)
 
     for i in (2, 1, 0):
+        n2_block(ag.slots[i])
         rsc.send_end(i)
+    n2_block(z)
+    gate.y_event(0)
+    gate.y_event(1)
     gate.x_event(0)
     ag.step2()
-    ag.step3()
-    gate.y_event(1)
+    ag.step3_mid()
+    up.y_event(0)
     gate.x_event(1)
-    up.y_event(0)
-    rsc.send_mid(2)
     gate.finish()
 
     def gate_block(b):
-        @pl.loop(0, ff // tile)
+        @pl.loop(0, ff // wide)
         def _(j):
-            cols = ds(j * tile, tile)
+            cols = ds(j * wide, wide)
             a_v[ds(b * sub, sub), cols] = dot(n_v[ds(b * sub, sub), :], wg_v[:, cols]).astype(BF16)
 
     def up_block(b):
-        @pl.loop(0, ff // tile)
+        @pl.loop(0, ff // wide)
         def _(j):
-            cols = ds(j * tile, tile)
+            cols = ds(j * wide, wide)
             bb = dot(n_v[ds(b * sub, sub), :], wu_v[:, cols]).astype(BF16)
             b_v[ds(b * sub, sub), cols] = bb
             aa = a_v[ds(b * sub, sub), cols].astype(F32)
-            u_v[ds(b * sub, sub), cols] = (aa * jax.nn.sigmoid(aa) * bb.astype(F32)).astype(BF16)
-
+            wg_v[ds(b * sub, sub), cols] = (aa * jax.nn.sigmoid(aa) * bb.astype(F32)).astype(BF16)
+
+    wg_out = net.here(wg_v, wg_o)
+    outs += [net.here(wq_v, wq_o), net.here(eq_v, eq_o)]
     gate_block(z)
     gate_block(ag.slots[0])
+    rsc.send_mid(2)
     gate_block(ag.slots[1])
+    up.y_event(1)
     up.x_event(0)
-    up.y_event(1)
+    ag.step3_end()
     gate_block(ag.slots[2])
-    outs += [net.here(n_v, n_o), net.here(a_v, a_o), net.here(wg_v, wg_o), net.here(wq_v, wq_o), net.here(eq_v, eq_o)]
+    n_out = net.here(n_v, n_o)
+    wg_out.wait()
+    down.y_event(0)
     up.x_event(1)
-    down.y_event(0)
+    up.finish()
+    outs.append(net.here(wu_v, wu_o))
+    up_block(z)
     rsc.send_mid(1)
     rsc.send_mid(0)
-    up.finish()
-    up_block(z)
     up_block(ag.slots[0])
+    down.y_event(1)
     down.x_event(0)
-    down.y_event(1)
     up_block(ag.slots[1])
     up_block(ag.slots[2])
-    outs += [net.here(b_v, b_o), net.here(u_v, u_o), net.here(wu_v, wu_o)]
-    down.x_event(1)
-    rsc.finish()
-
-    @pl.loop(0, sub // 16)
-    def _(r):
-        dn2_v[ds(r * 16, 16), :] = p_v[ds(z * sub + r * 16, 16), :].astype(F32)
-
-    @pl.when(z < 3)
-    def _():
-        @pl.loop(0, sub // 16)
-        def _(r):
-            dn2_v[ds(r * 16, 16), :] += rbuf[ds(z * sub + r * 16, 16), :].astype(F32)
-
-    @pl.when(z > 0)
-    def _():
-        @pl.loop(0, sub // 16)
-        def _(r):
-            dn2_v[ds(r * 16, 16), :] += rbuf[ds(4 * sub + r * 16, 16), :].astype(F32)
-
-    outs.append(net.here(dn2_v, dn2_o))
-    down.finish()
+    outs.append(net.here(u_v, u_o))
+    ag.drain()
+    gate.drain()
+    n_out.wait()
     for k in far_first:
         d_cp(k).wait_recv()
     d_own.wait()
-    for c in outs:
-        c.wait()
-    for k in far_first:
-        g_cp(k).wait_send()
-        h_cp(k).wait_send()
-        d_cp(k).wait_send()
-    for w in (qkv, gate, up, down):
-        w.drain()
-    ag.drain()
-    rsc.drain()
-
-
-def call_a(q_width, hid, eqh, cos_t, sin_t, swap, dh2h, wg, wu, wd, wq, gin):
-    tokens, dt = hid.shape
-    sub, dim, ff, width = tokens // 4, dt * 4, wg.shape[1], wq.shape[1]
-    s = jax.ShapeDtypeStruct
-    tok_ff = s((tokens, ff), BF16)
-    shapes = (s((tokens, dim), BF16), tok_ff, tok_ff, tok_ff, s((dim, ff), BF16), s((dim, ff), BF16), s((ff, dim), BF16),
-              s((dim, width), BF16), s((tokens, width), BF16), s((sub, dim), BF16), s((sub, dim), BF16), s((sub, dim), F32), s((8, dim), F32))
-    return pl.pallas_call(
-        functools.partial(kernel_a, q_width), out_shape=shapes, in_specs=[ANY] * 11, out_specs=[ANY] * len(shapes),
-        scratch_shapes=[
-            VMEM((sub, dim), BF16), VMEM((tokens, dim), BF16), VMEM((tokens, ff), BF16), VMEM((tokens, ff), BF16), VMEM((tokens, ff), BF16),
-            VMEM((dim, ff), BF16), VMEM((dim, ff), BF16), VMEM((dim, width), BF16), VMEM((tokens, width), BF16), VMEM((tokens, dim), BF16),
-            VMEM((5 * sub, dim), BF16), VMEM((8, dim), F32), VMEM((sub, dim), F32), VMEM((2 * tokens, 128), F32), VMEM((2 * tokens, 128), F32), VMEM((128, 128), BF16),
-            pltpu.SemaphoreType.DMA((64,)), pltpu.SemaphoreType.DMA((64,)), pltpu.SemaphoreType.DMA((32,))],
-        compiler_params=pltpu.CompilerParams(collective_id=0, has_side_effects=True, vmem_limit_bytes=VMEM_LIMIT),
-        cost_estimate=pl.CostEstimate(flops=20 * tokens * dim * ff, bytes_accessed=100000000, transcendentals=0), name="phase_a",
-    )(hid, eqh, cos_t, sin_t, swap, dh2h, wg, wu, wd, wq, gin)
-
-
-def kernel_b(u_h, wd_h, h_h, dh2_h, dn2_h, a_h, b_h, g_h,
-             e_o, da_o, db_o, n2_o, dres_o, home_o, dg_o, ux_o, ex_o,
-             u_v, wd_v, h_v, dh2_v, dn2_v, a_v, b_v, gains, e_v, p_v, rbuf, res_v, n2_v, dres_v, dg_v, send, recv, local):
-    dp, z, tx, peer = places()
-    tokens, ff = u_v.shape
-    sub, dim = h_v.shape
-    dt = dim // 4
-    tile = min(512, ff)
-    dtile = min(512, dim)
-    net = Wires(send, recv, local)
-    loads = [net.here(u_h, u_v), net.here(wd_h, wd_v)]
-    rows_in = [net.here(h_h, h_v), net.here(dn2_h, dn2_v), net.here(dh2_h, dh2_v), net.here(g_h, gains), net.here(a_h, a_v), net.here(b_h, b_v)]
-    entry_barrier([{"tx": peer[1]}, {"tx": peer[2]}, {"tx": peer[3]}], z)
-    far_first = (2, 3, 1)
-    o_id = net.take(4)
-
-    def o_cp(k, block):
-        return net.copy(res_v.at[:, pl.ds(k * dt, dt)], home_o.at[ds(block * sub, sub), :], o_id + k, o_id + k, tx=peer[k])
-
-    u_id, x_id = net.take(3), net.take(12)
-
-    def ux_cp(k):
-        src = ux_o.at[1] if k == 3 else u_h
-        return net.copy(src, ux_o.at[k - 1], u_id + k - 1, u_id + k - 1, tx=peer[1] if k == 3 else peer[k])
-
-    def ex_cp(k, b):
-        i = x_id + (k - 1) * 4 + b
-        rows = ds(b * sub, sub)
-        return net.copy(e_v.at[rows, pl.ds(k * dt, dt)], ex_o.at[k - 1, rows, :], i, i, tx=peer[k])
-
+    down.x_event(1)
+    down.finish()
     ux_cp(2).start()
     ux_cp(1).start()
-    rsc = LineScatter(net, p_v, rbuf, sub, z)
-    ag = LineGather(net, e_v, sub, z)
-    for c in loads:
-        c.wait()
 
     def down_block(b):
-        @pl.loop(0, dim // dtile)
+        @pl.loop(0, dim // dwide)
         def _(j):
-            cols = ds(j * dtile, dtile)
-            p_v[ds(b * sub, sub), cols] = dot(u_v[ds(b * sub, sub), :], wd_v[:, cols]).astype(BF16)
+            cols = ds(j * dwide, dwide)
+            n_v[ds(b * sub, sub), cols] = dot(wg_v[ds(b * sub, sub), :], wd_v[:, cols]).astype(BF16)
 
     for i in (2, 1, 0):
         down_block(ag.slots[i])
-        rsc.send_end(i)
+        rs2[0].send_end(i)
     down_block(z)
+    dg_v[...] = jnp.zeros_like(dg_v)
     for i in (2, 1, 0):
-        rsc.send_mid(i)
-    for c in rows_in:
-        c.wait()
+        rs2[0].send_mid(i)
     rsc.finish()
-    dg_v[...] = jnp.zeros_like(dg_v)
     step = 16
 
-    def mlp(r):
-        return p_v[ds(z * sub + r * step, step), :].astype(F32)
-
-    def from_right(r):
-        return rbuf[ds(z * sub + r * step, step), :].astype(F32)
-
-    def from_left(r):
-        return rbuf[ds(4 * sub + r * step, step), :].astype(F32)
-
-    def norm_rows(total):
-        @pl.loop(0, sub // step)
+    def norm_rows(first, right, left):
+        @pl.loop(0, hs // step)
         def _(r):
-            view = ds(r * step, step)
-            resid = (h_v[view, :].astype(F32) + total(r)).astype(BF16)
+            at = first + r * step
+            view, mine = ds(at, step), ds(z * sub + at, step)
+            total = rows[view, :].astype(F32) + n_v[mine, :].astype(F32)
+            dy = p_v[mine, :].astype(F32)
+            if right:
+                total += rbuf2[mine, :].astype(F32)
+                dy += rbuf[mine, :].astype(F32)
+            if left:
+                total += rbuf2[ds(4 * sub + at, step), :].astype(F32)
+                dy += rbuf[ds(4 * sub + at, step), :].astype(F32)
+            resid = total.astype(BF16)
             res_v[view, :] = resid
             x = resid.astype(F32)
             inv = lax.rsqrt(jnp.sum(x * x, axis=1, keepdims=True) / dim + NORM_EPS)
             xhat = x * inv
             gain = gains[1:2, :]
             n2_v[view, :] = (xhat * gain).astype(BF16)
-            dy = dn2_v[view, :]
             part = dy * xhat
             dg_v[...] += part[:8] + part[8:]
             inner = jnp.sum(part * gain, axis=1, keepdims=True) / dim
             dres = dh2_v[view, :].astype(F32) + inv * (dy * gain) - xhat * (inv * inner)
-            dres_v[view, :] = dres
-            e_v[ds(z * sub + r * step, step), :] = dres.astype(BF16)
-
-    @pl.when(z == 0)
-    def _():
-        norm_rows(lambda r: mlp(r) + from_right(r))
-
-    @pl.when(z == 3)
-    def _():
-        norm_rows(lambda r: mlp(r) + from_left(r))
-
-    @pl.when(mid(z))
-    def _():
-        norm_rows(lambda r: mlp(r) + from_right(r) + from_left(r))
-
-    ag.start()
-    for k in far_first:
-        o_cp(k, tx).start()
-    outs = [net.here(res_v.at[:, pl.ds(0, dt)], home_o.at[ds(tx * sub, sub), :]), net.here(n2_v, n2_o), net.here(dres_v, dres_o), net.here(dg_v, dg_o)]
+            dres_v[view, pl.ds(0, dim)] = dres
+            wg_v[ds(tokens + z * sub + at, step), :] = dres.astype(BF16)
+
+    def norm_half(half):
+        @pl.when(z == 0)
+        def _():
+            norm_rows(half * hs, True, False)
+
+        @pl.when(z == 3)
+        def _():
+            norm_rows(half * hs, False, True)
+
+        @pl.when(mid(z))
+        def _():
+            norm_rows(half * hs, True, True)
+
+    def spread(b, half):
+        for k in far_first:
+            ex_cp(k, b, half).start()
 
     def back_block(b):
-        rows = ds(b * sub, sub)
+        view = ds(b * sub, sub)
 
         @pl.loop(0, ff // tile)
         def _(j):
             cols = ds(j * tile, tile)
-            du = dot(e_v[rows, :], wd_v[ds(j * tile, tile), :], NT_DIMS)
-            aa = a_v[rows, cols].astype(F32)
-            bb = b_v[rows, cols].astype(F32)
+            du = dot(wg_v[ds(tokens + b * sub, sub), :], wd_v[ds(j * tile, tile), :], NT_DIMS)
+            aa = a_v[view, cols].astype(F32)
+            bb = b_v[view, cols].astype(F32)
             sig = jax.nn.sigmoid(aa)
-            a_v[rows, cols] = (du * bb * sig * (1.0 + aa * (1.0 - sig))).astype(BF16)
-            b_v[rows, cols] = (du * aa * sig).astype(BF16)
-
-    def spread(b):
-        for k in far_first:
-            ex_cp(k, b).start()
-
-    spread(z)
+            a_v[view, cols] = (du * bb * sig * (1.0 + aa * (1.0 - sig))).astype(BF16)
+            b_v[view, cols] = (du * aa * sig).astype(BF16)
+
+    s1, s2, s3 = ag.slots
+    rs2[0].finish()
+    norm_half(0)
+    ag2[0].start()
+    for i in (2, 1, 0):
+        rs2[1].send_end(i)
+    spread(z, 0)
+    ag2[0].step1()
+    rs2[1].send_mid(2)
+    ag2[0].step2()
+    ag2[0].step3_mid()
+    rs2[1].send_mid(1)
+    rs2[1].send_mid(0)
+    spread(s1, 0)
+    spread(s2, 0)
+    rs2[1].finish()
+    norm_half(1)
+    ag2[1].start()
+    for k in far_first:
+        o_cp(k, tx).start()
+    outs += [net.here(res_v.at[:, pl.ds(0, dt)], home_o.at[ds(tx * sub, sub), :]), net.here(n2_v, n2_o), net.here(dres_v.at[:, pl.ds(0, dim)], dres_o), net.here(dg_v, dg_o)]
+    spread(z, 1)
+    ag2[0].step3_end()
+    spread(s3, 0)
     back_block(z)
-    ag.step1()
-    spread(ag.slots[0])
-    back_block(ag.slots[0])
-    ag.step2()
-    spread(ag.slots[1])
+    ag2[1].step1()
+    spread(s1, 1)
+    back_block(s1)
+    ag2[1].step2()
+    ag2[1].step3_mid()
+    spread(s2, 1)
     ux_cp(2).wait_recv()
     ux_cp(3).start()
-    back_block(ag.slots[1])
-    ag.step3()
-    spread(ag.slots[2])
-    back_block(ag.slots[2])
-    outs += [net.here(e_v, e_o), net.here(a_v, da_o), net.here(b_v, db_o)]
+    back_block(s2)
+    ag2[1].step3_end()
+    spread(s3, 1)
+    outs.append(net.here(e_v, e_o))
+    back_block(s3)
+    outs += [net.here(a_v, da_o), net.here(b_v, db_o)]
     for k in far_first:
         o_cp(k, peer[k]).wait_recv()
         for b in range(4):
-            ex_cp(k, b).wait_recv()
+            ex_cp(k, b, 0).wait_recv()
+            ex_cp(k, b, 1).wait_recv()
     ux_cp(1).wait_recv()
     ux_cp(3).wait_recv()
     for c in outs:
         c.wait()
     for k in far_first:
+        g_cp(k).wait_send()
+        h_cp(k).wait_send()
+        d_cp(k).wait_send()
         o_cp(k, tx).wait_send()
         ux_cp(k).wait_send()
         for b in range(4):
-            ex_cp(k, b).wait_send()
-    ag.drain()
+            ex_cp(k, b, 0).wait_send()
+            ex_cp(k, b, 1).wait_send()
+    for w in (qkv, up, down):
+        w.drain()
     rsc.drain()
-
-
-def call_b(u, wd, h, dh2, dn2, a, b, gains):
-    tokens, ff = u.shape
-    sub, dim = h.shape
+    for h in range(2):
+        rs2[h].drain()
+        ag2[h].drain()
+
+
+def call_ab(q_width, hid, eqh, tab, swap, dh2h, wg, wu, wd, wq, gin):
+    tokens, dt = hid.shape
+    sub, dim, ff, width = tokens // 4, dt * 4, wg.shape[1], wq.shape[1]
     s = jax.ShapeDtypeStruct
-    shapes = (s((tokens, dim), BF16), s((tokens, ff), BF16), s((tokens, ff), BF16), s((sub, dim), BF16), s((sub, dim), F32),
-              s((tokens, dim // 4), BF16), s((8, dim), F32), s((3, tokens, ff), BF16), s((3, tokens, dim // 4), BF16))
+    tok_ff, tok_d, row = s((tokens, ff), BF16), s((tokens, dim), BF16), s((sub, dim), BF16)
+    shapes = (tok_d, tok_ff, tok_ff, tok_ff, s((dim, ff), BF16), s((dim, ff), BF16), s((dim, width), BF16), s((tokens, width), BF16),
+              row, s((8, dim), F32), tok_d, row, s((sub, dim), F32), s((tokens, dt), BF16), s((8, dim), F32),
+              s((3, tokens, ff), BF16), s((3, tokens, dt), BF16))
+    vrow, vtok, vff = VMEM((sub, dim), BF16), VMEM((tokens, dim), BF16), VMEM((tokens, ff), BF16)
     return pl.pallas_call(
-        kernel_b, out_shape=shapes, in_specs=[ANY] * 8, out_specs=[ANY] * len(shapes),
+        functools.partial(kernel_ab, q_width), out_shape=shapes, in_specs=[ANY] * 10, out_specs=[ANY] * len(shapes),
         scratch_shapes=[
-            VMEM((tokens, ff), BF16), VMEM((ff, dim), BF16), VMEM((sub, dim), BF16), VMEM((sub, dim), BF16), VMEM((sub, dim), F32),
-            VMEM((tokens, ff), BF16), VMEM((tokens, ff), BF16), VMEM((8, dim), F32), VMEM((tokens, dim), BF16), VMEM((tokens, dim), BF16),
-            VMEM((5 * sub, dim), BF16), VMEM((sub, dim), BF16), VMEM((sub, dim), BF16), VMEM((sub, dim), F32), VMEM((8, dim), F32),
-            pltpu.SemaphoreType.DMA((40,)), pltpu.SemaphoreType.DMA((40,)), pltpu.SemaphoreType.DMA((20,))],
-        compiler_params=pltpu.CompilerParams(collective_id=1, has_side_effects=True, vmem_limit_bytes=VMEM_LIMIT),
-        cost_estimate=pl.CostEstimate(flops=20 * tokens * dim * ff, bytes_accessed=60000000, transcendentals=0), name="phase_b",
-    )(u, wd, h, dh2, dn2, a, b, gains)
+            vrow, vrow, vrow, vrow, VMEM((sub, max(dim, 2048)), F32), vtok, vff, vff, VMEM((dim, ff), BF16), VMEM((dim, ff), BF16), VMEM((ff, dim), BF16),
+            VMEM((dim, width), BF16), VMEM((tokens, width), BF16), vtok, VMEM((5 * sub, dim), BF16), VMEM((5 * sub, dim), BF16),
+            VMEM((8, dim), F32), VMEM((8, dim), F32), VMEM((128, 128), BF16),
+            pltpu.SemaphoreType.DMA((136,)), pltpu.SemaphoreType.DMA((136,)), pltpu.SemaphoreType.DMA((40,))],
+        compiler_params=pltpu.CompilerParams(collective_id=0, has_side_effects=True, vmem_limit_bytes=VMEM_LIMIT),
+        cost_estimate=pl.CostEstimate(flops=20 * tokens * dim * ff, bytes_accessed=100000000, transcendentals=0), name="phase_ab",
+    )(hid, eqh, tab, swap, dh2h, wg, wu, wd, wq, gin)
 
 
 ROWS_ROWS = (((0,), (0,)), ((), ()))
@@ -721,10 +702,10 @@
         self.cp(2).wait_recv()
 
 
-def kernel_c(q_width, da_h, db_h, wg_h, wu_h, n_h, u_h, ux_h, e_h, ex_h, n2_h, eq_h, wq_h, h_h, dres_h, g_h, dga_h, cosh, sinh, swaph,
+def kernel_c(q_width, da_h, db_h, wg_h, wu_h, n_h, u_h, ux_h, e_h, ex_h, n2_h, eq_h, wq_h, h_h, dres_h, g_h, dga_h, tabh, swaph,
              wgo, wgy, wuo, wuy, wdo, wqo, wqy, q_o, dh_o, dg_o, g2, g0, u2, u0, q2, q0, qx,
              wg_v, wu_v, da_v, db_v, n_v, p_v, rbuf, n2_v, st3, st1, cross_g, cross_u, stage, tiles_v, dres_v, wq_v, eq_v,
-             gains, dg_v, dgr, dgz, cos_v, sin_v, swap_v, send, recv, local):
+             gains, dg_v, dgr, dgz, tab_v, swap_v, send, recv, local):
     dp, z, tx, peer = places()
     tokens, ff = da_v.shape
     sub, dim = dres_v.shape
@@ -739,7 +720,7 @@
     first = [net.here(n_h, n_v), net.here(da_h, da_v)]
     second = [net.here(db_h, db_v), net.here(wg_h, wg_v), net.here(wu_h, wu_v)]
     third = [net.here(wq_h, wq_v), net.here(eq_h, eq_v), net.here(dres_h, dres_v), net.here(g_h, gains),
-             net.here(dga_h, dg_v.at[pl.ds(8, 8), :]), net.here(cosh, cos_v), net.here(sinh, sin_v), net.here(swaph, swap_v)]
+             net.here(dga_h, dg_v.at[pl.ds(8, 8), :]), net.here(tabh, tab_v), net.here(swaph, swap_v)]
     sem = pltpu.get_barrier_semaphore()
     zs = tuple((z + i) % 4 for i in range(4))
     for i in (1, 2, 3):
@@ -797,6 +778,7 @@
     up.step3()
     up.step1()
     ag.step2()
+    ag.step3_mid()
     up.step2()
     rsc.send_mid(1)
     rsc.send_mid(0)
@@ -836,7 +818,7 @@
         done[1] = down_tile(1, 1, loads[1])
     for c in third:
         c.wait()
-    ag.step3()
+    ag.step3_end()
 
     @pl.loop(0, 4)
     def _(b):
@@ -916,7 +898,7 @@
     q_own.wait()
     net.here(qx, n_v.at[:, pl.ds(width, width)]).wait()
     turned = n_v.at[:, pl.ds(width, width)]
-    turn(turned, turned, tokens, width, q_width, cos_v, sin_v, swap_v, False)
+    turn(turned, turned, tokens, width, q_width, tab_v, swap_v, False)
     q_out = net.here(turned, q_o)
     for k in far_first:
         t_cp(k).wait_recv()
@@ -961,7 +943,7 @@
             VMEM((tokens, dim), BF16), VMEM((5 * sub, dim), BF16), VMEM((tokens, dim), BF16),
             VMEM((dt, ff), BF16), VMEM((dt, ff), BF16), VMEM((dt, ff), BF16), VMEM((dt, ff), BF16), VMEM((dt, ff), BF16),
             VMEM((2, max(dt, tile), max(dt, tile)), F32), VMEM((sub, dim), F32), VMEM((dim, width), BF16), VMEM((tokens, width), BF16),
-            VMEM((8, dim), F32), VMEM((16, dim), F32), VMEM((4, 16, dt), F32), VMEM((4, 16, dt), F32), VMEM((2 * tokens, 128), F32), VMEM((2 * tokens, 128), F32), VMEM((128, 128), BF16),
+            VMEM((8, dim), F32), VMEM((16, dim), F32), VMEM((4, 16, dt), F32), VMEM((4, 16, dt), F32), VMEM((sub, 2048), F32), VMEM((128, 128), BF16),
             pltpu.SemaphoreType.DMA((48,)), pltpu.SemaphoreType.DMA((48,)), pltpu.SemaphoreType.DMA((72,))],
         compiler_params=pltpu.CompilerParams(collective_id=2, has_side_effects=True, vmem_limit_bytes=VMEM_LIMIT),
         cost_estimate=pl.CostEstimate(flops=20 * tokens * dim * ff, bytes_accessed=100000000, transcendentals=0), name="phase_c",
@@ -979,23 +961,22 @@
         lane = jnp.arange(128)
         inv_freq = ROPE_BASE ** (-((lane % head_dim) // 2 * 2).astype(F32) / head_dim)
         angles = positions.astype(F32)[:, None] * inv_freq[None, :]
-        turned = jnp.where(lax.axis_index("ty") < mesh.shape["ty"] // 2, angles, 0.0)
-        angles = jnp.concatenate([angles, turned])
         cos_t = jnp.cos(angles)
         swap = (lane[:, None] == (lane + 1 - lane % 2 * 2)[None, :]).astype(BF16)
         sin_t = jnp.sin(angles) * jnp.where(lane % 2 == 0, -1.0, 1.0)[None, :]
 
+        turns = lax.axis_index("ty") < mesh.shape["ty"] // 2
+        table = jnp.stack([cos_t, jnp.where(turns, cos_t, 1.0), sin_t, jnp.where(turns, sin_t, 0.0)])
+        table = table.reshape(4, 4, tokens // 4, 128).transpose(2, 0, 1, 3).reshape(tokens // 4, 2048)
         back = jnp.concatenate([grad_q.reshape(tokens, q_width), grad_kv.reshape(tokens, kv_width)], axis=1)
         w_qkv_own = jnp.concatenate([w_q.reshape(dt, q_width), w_kv.reshape(dt, kv_width)], axis=1)
         gin = jnp.concatenate([jnp.stack([g_ffn, g_attn]).astype(F32), jnp.zeros((6, dt), F32)])
 
-        (normed_all, a_all, b_all, u_all, gate_w, up_w, down_w, w_qkv, back_all, h_rows, dh2_rows, dn2_rows, gains) = call_a(
-            q_width, hidden, back, cos_t, sin_t, swap, grad_h2, w_gate, w_up, w_down, w_qkv_own, gin)
-        res_all, grad_gate, grad_up, normed2, grad_res, resid_out, gattn8, u_other, e_other = call_b(
-            u_all, down_w, h_rows, dh2_rows, dn2_rows, a_all, b_all, gains)
+        (normed_all, grad_gate, grad_up, u_all, gate_w, up_w, w_qkv, back_all, h_rows, gains, res_all, normed2, grad_res, resid_out, gattn8,
+         u_other, e_other) = call_ab(q_width, hidden, back, table, swap, grad_h2, w_gate, w_up, w_down, w_qkv_own, gin)
         (wg_own, wg_far, wu_own, wu_far, grad_wdown, wq_own, wq_far, qkv_out, grad_hidden, gain_grads, *_) = call_c(
             q_width, grad_gate, grad_up, gate_w, up_w, normed_all, u_all, u_other, res_all, e_other, normed2, back_all, w_qkv,
-            h_rows, grad_res, gains, gattn8, cos_t, sin_t, swap)
+            h_rows, grad_res, gains, gattn8, table, swap)
         grad_wgate = wg_own + wg_far.astype(F32)
         grad_wup = wu_own + wu_far.astype(F32)
         grad_wqkv = wq_own + wq_far.astype(F32)

time: 544 us -> 500 us (0.919)
  the two profiles are of different devices: /device:TPU:0 before, /device:TPU:13 now
where the time goes in v1:
time: 500 us; the launch traced here: 493 us
  Pallas kernels  452 us (90%)
  local copies, waits for them, and re-layouts  20.4 us (4%)
  other arithmetic  19.3 us (4%)
    pallas_call x1, Pallas kernels, call_ab(): pl.pallas_call(functools.partial(kernel_ab, q_width), out_shape=shapes, i...  284 us
    pallas_call x1, Pallas kernels, call_c(): pl.pallas_call(functools.partial(kernel_c, q_width), out_shape=shapes, in...  168 us

profile of v1, /device:TPU:13, one launch (start us, length us, event | category | flops | bytes accessed | tf_op | source)
XLA Modules:
  0.0 493.1 jit_solution(14762802396258409697)
XLA Ops:
  0.7 0.7 stack.17
  4.2 1.2 copy.35
  5.4 1.3 copy.34
  6.6 0.9 pad_maximum_fusion.1.wq
  8.3 1.2 pad_maximum_fusion.eqh
  9.6 4.1 multiply_cosine_fusion
  14.1 1.8 reshape.211.tabh
  16.0 284.1 %phase_ab.1 = (bf16[1024,2048]{1,0:T(8,128)(2,1)}, bf16[1024,2048]{1,0:T(8,128)(2,1)}, bf16[1024,2048]{1,0:T(8,128)(2,1)}, bf16[1024,2048]{1,0:T(8,128)(2,1)}, b...) custom-call(bf16[1024,512]{1,0:T(8,128)(2,1)} %hid.1, ...), custom_call_target="tpu_custom_call" | custom-call | flops 85899345920 | bytes 100000000 | tf_op jit(solution)/shard_map/phase_ab/pallas_call | solution.py:629
  300.1 168.3 %phase_c.1 = (f32[512,2048]{1,0:T(8,128)}, bf16[512,2048]{1,0:T(8,128)(2,1)}, f32[512,2048]{1,0:T(8,128)}, bf16[512,2048]{1,0:T(8,128)(2,1)}, f32[2048,512]{1,0:...) custom-call(bf16[1024,2048]{1,0:T(8,128)(2,1)} %get-tuple-element.39, ...), custom_call_target="tpu_custom_call" | custom-call | flops 85899345920 | bytes 100000000 | tf_op jit(solution)/shard_map/phase_c/pallas_call | solution.py:939
  468.4 1.3 slice_reduce_fusion
  469.7 1.1 slice.19
  470.8 1.3 slice.18
  472.1 1.3 copy.36
  473.4 1.0 copy.37
  474.4 1.3 convert_add_fusion.2
  475.7 0.8 slice.25
  476.7 1.3 copy.38
  478.0 2.0 copy.39
  480.0 5.2 %convert_add_fusion.1 = f32[512,2048]{1,0:T(8,128)} fusion(f32[512,2048]{1,0:T(8,128)} %get-tuple-element.58, bf16[512,2048]{1,0:T(8,128)(2,1)S(1)} %copy-done.3), kind=kLoop, calls=%fused_computation.1 | loop fusion | flops 2097152 | bytes 10485760 | tf_op jit(solution)/shard_map/add | solution.py:980
  485.3 2.8 convert_add_fusion
  488.1 1.0 copy.43
  489.1 0.9 copy-done.7
  489.9 1.0 copy.44
  490.9 2.0 copy.45
  (29 shorter events, 4.1 us)
Async XLA Ops:
  0.6 6.9 %copy-start.8 = (bf16[1024,4,64]{0,2,1:T(8,128)(2,1)S(1)}, bf16[1024,4,64]{0,2,1:T(8,128)(2,1)}, u32[]{:S(2)}) copy-start(bf16[1024,4,64]{0,2,1:T(8,128)(2,1)} %param.23) | copy-start | bytes 1572868
  4.2 3.6 copy-start.5
  472.1 2.3 copy-start.4
  476.7 3.4 copy-start.3
  480.0 5.2 %copy-start.1 = (f32[512,2048]{1,0:T(8,128)S(1)}, f32[512,2048]{1,0:T(8,128)}, u32[]{:S(2)}) copy-start(f32[512,2048]{1,0:T(8,128)} %get-tuple-element.60) | copy-start | bytes 12582916
  480.0 5.2 %copy-start.2 = (bf16[512,2048]{1,0:T(8,128)(2,1)S(1)}, bf16[512,2048]{1,0:T(8,128)(2,1)}, u32[]{:S(2)}) copy-start(bf16[512,2048]{1,0:T(8,128)(2,1)} %get-tuple-element.61) | copy-start | bytes 6291460
  485.3 2.8 copy-start.6
  485.3 5.6 %copy-start = (f32[2048,512]{1,0:T(8,128)S(1)}, f32[2048,512]{1,0:T(8,128)}, u32[]{:S(2)}) copy-start(f32[2048,512]{1,0:T(8,128)} %get-tuple-element.105) | copy-start | bytes 12582916
  488.1 1.9 copy-start.7

commit v2 on v1

--- a/solution.py
+++ b/solution.py
@@ -56,6 +56,12 @@
             dst[ds(r * step, step), cols] = (main - side if back else main + side).astype(BF16)
 
 
+def pick(i, z):
+    s1, s2, s3 = slots(z)
+    first, last = (3 - i) // 3, (i // 2) * (i % 2)
+    return z * first + s1 * ((i % 2) * (1 - i // 2)) + s2 * ((i // 2) * (1 - i % 2)) + s3 * last
+
+
 class Wires:
     def __init__(self, send, recv, local):
         self.send, self.recv, self.local = send, recv, local
@@ -144,6 +150,23 @@
             self.forward(0)
             self.take(1)
             self.forward(1)
+
+    def near_end(self):
+        @pl.when(end(self.z))
+        def _():
+            self.take(0)
+
+    def near_mid(self):
+        @pl.when(mid(self.z))
+        def _():
+            self.take(1)
+            self.forward(1)
+
+    def far_mid(self):
+        @pl.when(mid(self.z))
+        def _():
+            self.take(0)
+            self.forward(0)
 
     def step2(self):
         @pl.when(end(self.z))
@@ -235,14 +258,15 @@
 
 
 class WeightGather:
-    def __init__(self, net, w, full, pos, by_rows, chunks):
+    def __init__(self, net, w, full, pos, by_rows, chunks, direct=0):
         self.net, self.w, self.full, self.by_rows = net, w, full, by_rows
         self.dp, self.t1, self.t2 = pos
         self.len = w.shape[0]
         self.width = w.shape[0] if by_rows else w.shape[1]
         self.chunks = chunks
         self.piece = self.len // 2 // chunks
-        self.base = net.take(1 + 4 * chunks)
+        self.direct = direct
+        self.base = net.take(1 + 4 * chunks + direct)
 
     def dst(self, k, off, n):
         if self.by_rows:
@@ -270,9 +294,16 @@
     def mate(self):
         return self.net.copy(self.w, self.dst(1, 0, self.len), self.base, self.base, tx=self.t1)
 
+    def straight(self, n, half):
+        o = self.off(half, self.chunks - 1 - n)
+        i = self.base + 1 + 4 * self.chunks + n
+        return self.net.copy(self.w.at[ds(o, self.piece, 16), :], self.dst(2, o, self.piece), i, i, tx=self.t2)
+
     def start_y(self):
         for ch in range(self.chunks):
             self.near(ch).start()
+        for n in range(self.direct):
+            self.straight(n, 1 - self.dp).start()
 
     def start_local(self):
         self.own = self.net.here(self.w, self.dst(0, 0, self.len))
@@ -280,11 +311,15 @@
 
     def y_event(self, ch):
         self.near(ch).wait_recv()
-        self.cross(ch, self.dp).start()
+        if ch < self.chunks - self.direct:
+            self.cross(ch, self.dp).start()
         self.diag(ch, 0, self.dp).start()
 
     def x_event(self, ch):
-        self.cross(ch, 1 - self.dp).wait_recv()
+        if ch < self.chunks - self.direct:
+            self.cross(ch, 1 - self.dp).wait_recv()
+        else:
+            self.straight(self.chunks - 1 - ch, 1 - self.dp).wait_recv()
         self.diag(ch, 1, 1 - self.dp).start()
 
     def finish(self):
@@ -298,7 +333,10 @@
         self.mate().wait_send()
         for ch in range(self.chunks):
             self.near(ch).wait_send()
-            self.cross(ch, self.dp).wait_send()
+            if ch < self.chunks - self.direct:
+                self.cross(ch, self.dp).wait_send()
+            else:
+                self.straight(self.chunks - 1 - ch, 1 - self.dp).wait_send()
             self.diag(ch, 0, self.dp).wait_send()
             self.diag(ch, 1, 1 - self.dp).wait_send()
 
@@ -328,7 +366,7 @@
 
     pos = (dp, peer[1], peer[2])
     far_first = (2, 3, 1)
-    g_id, h_id, e_id, d_id, o_id, u_id, x_id = (net.take(4), net.take(4), net.take(4), net.take(4), net.take(4), net.take(3), net.take(24))
+    g_id, h_id, e_id, d_id, o_id, u_id, x_id = (net.take(4), net.take(4), net.take(4), net.take(4), net.take(4), net.take(12), net.take(24))
     u_v = wg_v.at[pl.ds(0, tokens), :]
     e_v = wg_v.at[pl.ds(tokens, tokens), :]
 
@@ -347,9 +385,11 @@
     def o_cp(k, block):
         return net.copy(res_v.at[:, pl.ds(k * dt, dt)], home_o.at[ds(block * sub, sub), :], o_id + k, o_id + k, tx=peer[k])
 
-    def ux_cp(k):
-        src = ux_o.at[1] if k == 3 else u_v
-        return net.copy(src, ux_o.at[k - 1], u_id + k - 1, u_id + k - 1, tx=peer[1] if k == 3 else peer[k])
+    def ux_cp(k, b):
+        view = ds(b * sub, sub)
+        src = ux_o.at[1, view, :] if k == 3 else wg_v.at[view, :]
+        i = u_id + (k - 1) * 4 + b
+        return net.copy(src, ux_o.at[k - 1, view, :], i, i, tx=peer[1] if k == 3 else peer[k])
 
     def ex_cp(k, b, half):
         i = x_id + half * 12 + (k - 1) * 4 + b
@@ -358,7 +398,7 @@
 
     gate = WeightGather(net, wg, wg_v, pos, True, 2)
     up = WeightGather(net, wu, wu_v, pos, True, 2)
-    down = WeightGather(net, wd, wd_v, pos, False, 2)
+    down = WeightGather(net, wd, wd_v, pos, False, 4, 1)
     qkv = WeightGather(net, wq, wq_v, pos, True, 1)
     ag = LineGather(net, n_v, sub, z)
     rsc = LineScatter(net, p_v, rbuf, sub, z)
@@ -415,10 +455,12 @@
             w = wq_v[ds(j * dtile, dtile), :]
             p_v[ds(b * sub, sub), ds(j * dtile, dtile)] = dot(eq_v[ds(b * sub, sub), :], w, NT_DIMS).astype(BF16)
 
-    for i in (2, 1, 0):
-        n2_block(ag.slots[i])
-        rsc.send_end(i)
-    n2_block(z)
+    @pl.loop(0, 4)
+    def _(i):
+        n2_block(pick(3 - i, z))
+        for step in range(3):
+            pl.when(i == step)(lambda step=step: rsc.send_end(2 - step))
+
     gate.y_event(0)
     gate.y_event(1)
     gate.x_event(0)
@@ -445,39 +487,57 @@
 
     wg_out = net.here(wg_v, wg_o)
     outs += [net.here(wq_v, wq_o), net.here(eq_v, eq_o)]
-    gate_block(z)
-    gate_block(ag.slots[0])
-    rsc.send_mid(2)
-    gate_block(ag.slots[1])
-    up.y_event(1)
-    up.x_event(0)
-    ag.step3_end()
-    gate_block(ag.slots[2])
+    def gate_events_2():
+        rsc.send_mid(2)
+
+    def gate_events_3():
+        up.y_event(1)
+        up.x_event(0)
+        ag.step3_end()
+
+    @pl.loop(0, 4)
+    def _(i):
+        pl.when(i == 2)(gate_events_2)
+        pl.when(i == 3)(gate_events_3)
+        gate_block(pick(i, z))
+
     n_out = net.here(n_v, n_o)
     wg_out.wait()
     down.y_event(0)
     up.x_event(1)
     up.finish()
     outs.append(net.here(wu_v, wu_o))
-    up_block(z)
-    rsc.send_mid(1)
-    rsc.send_mid(0)
-    up_block(ag.slots[0])
-    down.y_event(1)
-    down.x_event(0)
-    up_block(ag.slots[1])
-    up_block(ag.slots[2])
+
+    def up_events_1():
+        rsc.send_mid(1)
+        rsc.send_mid(0)
+
+    def up_events_2():
+        down.y_event(1)
+        down.x_event(0)
+
+    def up_events_3():
+        down.y_event(2)
+        down.x_event(1)
+
+    @pl.loop(0, 4)
+    def _(i):
+        pl.when(i == 1)(up_events_1)
+        pl.when(i == 2)(up_events_2)
+        pl.when(i == 3)(up_events_3)
+        b = pick(i, z)
+        up_block(b)
+        ux_cp(2, b).start()
+        ux_cp(1, b).start()
+
     outs.append(net.here(u_v, u_o))
     ag.drain()
     gate.drain()
     n_out.wait()
-    for k in far_first:
-        d_cp(k).wait_recv()
-    d_own.wait()
-    down.x_event(1)
+    down.y_event(3)
+    down.x_event(2)
+    down.x_event(3)
     down.finish()
-    ux_cp(2).start()
-    ux_cp(1).start()
 
     def down_block(b):
         @pl.loop(0, dim // dwide)
@@ -485,30 +545,35 @@
             cols = ds(j * dwide, dwide)
             n_v[ds(b * sub, sub), cols] = dot(wg_v[ds(b * sub, sub), :], wd_v[:, cols]).astype(BF16)
 
-    for i in (2, 1, 0):
-        down_block(ag.slots[i])
-        rs2[0].send_end(i)
-    down_block(z)
+    @pl.loop(0, 4)
+    def _(i):
+        down_block(pick(3 - i, z))
+        for step in range(3):
+            pl.when(i == step)(lambda step=step: rs2[0].send_end(2 - step))
+
+    rs2[1].send_end(2)
     dg_v[...] = jnp.zeros_like(dg_v)
+    for k in far_first:
+        d_cp(k).wait_recv()
+    d_own.wait()
     for i in (2, 1, 0):
         rs2[0].send_mid(i)
     rsc.finish()
     step = 16
 
-    def norm_rows(first, right, left):
+    def norm_half(half):
         @pl.loop(0, hs // step)
         def _(r):
-            at = first + r * step
-            view, mine = ds(at, step), ds(z * sub + at, step)
-            total = rows[view, :].astype(F32) + n_v[mine, :].astype(F32)
-            dy = p_v[mine, :].astype(F32)
-            if right:
-                total += rbuf2[mine, :].astype(F32)
-                dy += rbuf[mine, :].astype(F32)
-            if left:
-                total += rbuf2[ds(4 * sub + at, step), :].astype(F32)
-                dy += rbuf[ds(4 * sub + at, step), :].astype(F32)
-            resid = total.astype(BF16)
+            at = half * hs + r * step
+            view, mine, far = ds(at, step), ds(z * sub + at, step), ds(4 * sub + at, step)
+
+            def whole(part, got):
+                right = jnp.where(z < 3, got[mine, :].astype(F32), 0.0)
+                left = jnp.where(z > 0, got[far, :].astype(F32), 0.0)
+                return part[mine, :].astype(F32) + right + left
+
+            resid = (rows[view, :].astype(F32) + whole(n_v, rbuf2)).astype(BF16)
+            dy = whole(p_v, rbuf)
             res_v[view, :] = resid
             x = resid.astype(F32)
             inv = lax.rsqrt(jnp.sum(x * x, axis=1, keepdims=True) / dim + NORM_EPS)
@@ -522,19 +587,6 @@
             dres_v[view, pl.ds(0, dim)] = dres
             wg_v[ds(tokens + z * sub + at, step), :] = dres.astype(BF16)
 
-    def norm_half(half):
-        @pl.when(z == 0)
-        def _():
-            norm_rows(half * hs, True, False)
-
-        @pl.when(z == 3)
-        def _():
-            norm_rows(half * hs, False, True)
-
-        @pl.when(mid(z))
-        def _():
-            norm_rows(half * hs, True, True)
-
     def spread(b, half):
         for k in far_first:
             ex_cp(k, b, half).start()
@@ -556,48 +608,66 @@
     rs2[0].finish()
     norm_half(0)
     ag2[0].start()
-    for i in (2, 1, 0):
-        rs2[1].send_end(i)
-    spread(z, 0)
-    ag2[0].step1()
+    rs2[1].send_end(1)
+    rs2[1].send_end(0)
     rs2[1].send_mid(2)
-    ag2[0].step2()
-    ag2[0].step3_mid()
+    ag2[0].near_mid()
+    ag2[0].far_mid()
     rs2[1].send_mid(1)
     rs2[1].send_mid(0)
-    spread(s1, 0)
-    spread(s2, 0)
+    ag2[0].step3_mid()
+    spread(z, 0)
     rs2[1].finish()
     norm_half(1)
     ag2[1].start()
+    ag2[0].near_end()
+    spread(z, 1)
     for k in far_first:
         o_cp(k, tx).start()
     outs += [net.here(res_v.at[:, pl.ds(0, dt)], home_o.at[ds(tx * sub, sub), :]), net.here(n2_v, n2_o), net.here(dres_v.at[:, pl.ds(0, dim)], dres_o), net.here(dg_v, dg_o)]
-    spread(z, 1)
-    ag2[0].step3_end()
-    spread(s3, 0)
-    back_block(z)
-    ag2[1].step1()
-    spread(s1, 1)
-    back_block(s1)
-    ag2[1].step2()
-    ag2[1].step3_mid()
-    spread(s2, 1)
-    ux_cp(2).wait_recv()
-    ux_cp(3).start()
-    back_block(s2)
-    ag2[1].step3_end()
-    spread(s3, 1)
+
+    def back_events_1():
+        ag2[1].near_mid()
+        ag2[1].far_mid()
+        spread(s1, 0)
+        ag2[0].step2()
+        spread(s2, 0)
+        ag2[1].near_end()
+        spread(s1, 1)
+
+    def back_events_2():
+        ag2[1].step2()
+        spread(s2, 1)
+        ag2[0].step3_end()
+        spread(s3, 0)
+        ag2[1].step3_mid()
+        for j in range(4):
+            ux_cp(2, ag_order[j]).wait_recv()
+            ux_cp(3, ag_order[j]).start()
+
+    def back_events_3():
+        ag2[1].step3_end()
+        spread(s3, 1)
+
+    ag_order = (z, s1, s2, s3)
+
+    @pl.loop(0, 4)
+    def _(i):
+        pl.when(i == 1)(back_events_1)
+        pl.when(i == 2)(back_events_2)
+        pl.when(i == 3)(back_events_3)
+        back_block(pick(i, z))
+
     outs.append(net.here(e_v, e_o))
-    back_block(s3)
     outs += [net.here(a_v, da_o), net.here(b_v, db_o)]
     for k in far_first:
         o_cp(k, peer[k]).wait_recv()
         for b in range(4):
             ex_cp(k, b, 0).wait_recv()
             ex_cp(k, b, 1).wait_recv()
-    ux_cp(1).wait_recv()
-    ux_cp(3).wait_recv()
+    for b in range(4):
+        ux_cp(1, b).wait_recv()
+        ux_cp(3, b).wait_recv()
     for c in outs:
         c.wait()
     for k in far_first:
@@ -605,8 +675,8 @@
         h_cp(k).wait_send()
         d_cp(k).wait_send()
         o_cp(k, tx).wait_send()
-        ux_cp(k).wait_send()
         for b in range(4):
+            ux_cp(k, b).wait_send()
             ex_cp(k, b, 0).wait_send()
             ex_cp(k, b, 1).wait_send()
     for w in (qkv, up, down):
@@ -632,7 +702,7 @@
             vrow, vrow, vrow, vrow, VMEM((sub, max(dim, 2048)), F32), vtok, vff, vff, VMEM((dim, ff), BF16), VMEM((dim, ff), BF16), VMEM((ff, dim), BF16),
             VMEM((dim, width), BF16), VMEM((tokens, width), BF16), vtok, VMEM((5 * sub, dim), BF16), VMEM((5 * sub, dim), BF16),
             VMEM((8, dim), F32), VMEM((8, dim), F32), VMEM((128, 128), BF16),
-            pltpu.SemaphoreType.DMA((136,)), pltpu.SemaphoreType.DMA((136,)), pltpu.SemaphoreType.DMA((40,))],
+            pltpu.SemaphoreType.DMA((160,)), pltpu.SemaphoreType.DMA((160,)), pltpu.SemaphoreType.DMA((40,))],
         compiler_params=pltpu.CompilerParams(collective_id=0, has_side_effects=True, vmem_limit_bytes=VMEM_LIMIT),
         cost_estimate=pl.CostEstimate(flops=20 * tokens * dim * ff, bytes_accessed=100000000, transcendentals=0), name="phase_ab",
     )(hid, eqh, tab, swap, dh2h, wg, wu, wd, wq, gin)
@@ -677,29 +747,40 @@
 
         self.cp(2).start()
 
-    def step0(self):
+    def step0(self, far):
         self.cp(1).wait_recv()
-        self.net.here(self.got0, self.stage).wait()
-        for j in range(self.tiles):
-            cols = pl.ds(j * self.w, self.w)
-            if j >= 2:
-                self.copies[j - 2].wait()
-            else:
-                if j == 0:
-                    self.copies = []
-            place = self.out_tiles.at[j % 2, :, pl.ds(0, self.w)]
-            self.out_tiles[j % 2, :, pl.ds(0, self.w)] = self.tile(0, j) + self.stage[:, cols].astype(F32)
-            self.copies.append(self.net.here(place, self.out.at[:, cols]))
-        for c in self.copies[-2:]:
+        self.cp(2).wait_recv()
+        loads = [self.net.here(self.got0, self.stage), self.net.here(self.got_y, far)]
+        for c in loads:
             c.wait()
+        base = self.net.n_local
+        self.net.n_local += 2
+
+        def put(j, slot):
+            src = self.out_tiles.at[slot, :, pl.ds(0, self.w)]
+            return pltpu.make_async_copy(src, self.out.at[:, ds(j * self.w, self.w)], self.net.local.at[base + slot])
+
+        @pl.loop(0, self.tiles)
+        def _(j):
+            cols = ds(j * self.w, self.w)
+            slot = j % 2
+
+            @pl.when(j >= 2)
+            def _():
+                put(j, slot).wait()
+
+            self.out_tiles[slot, :, pl.ds(0, self.w)] = self.tile(0, j) + (self.stage[:, cols].astype(F32) + far[:, cols].astype(F32))
+            put(j, slot).start()
+
+        for slot in range(min(2, self.tiles)):
+            put(slot, slot).wait()
 
     def sent_locally(self):
         self.cp(0).wait_send()
         self.cp(1).wait_send()
 
-    def finish(self):
+    def sent(self):
         self.cp(2).wait_send()
-        self.cp(2).wait_recv()
 
 
 def kernel_c(q_width, da_h, db_h, wg_h, wu_h, n_h, u_h, ux_h, e_h, ex_h, n2_h, eq_h, wq_h, h_h, dres_h, g_h, dga_h, tabh, swaph,
@@ -764,24 +845,25 @@
     gate.step2()
     for c in second:
         c.wait()
-    dn_block(ag.slots[2])
-    rsc.send_end(2)
-    ag.step1()
-    dn_block(ag.slots[1])
-    rsc.send_end(1)
-    dn_block(ag.slots[0])
-    rsc.send_end(0)
-    rsc.send_mid(2)
-    dn_block(z)
-    gate.step0()
+
+    @pl.loop(0, 4)
+    def _(i):
+        pl.when(i == 1)(ag.step1)
+        dn_block(pick(3 - i, z))
+        for step in range(3):
+            pl.when(i == step)(lambda step=step: rsc.send_end(2 - step))
+
     gate.sent_locally()
     up.step3()
     up.step1()
+    up.step2()
+    rsc.send_mid(2)
     ag.step2()
     ag.step3_mid()
-    up.step2()
-    rsc.send_mid(1)
-    rsc.send_mid(0)
+    up.sent_locally()
+    h_in = net.here(h_h, st3.at[pl.ds(0, sub), :])
+    gate.step0(st1)
+    gate.sent()
 
     e_in = [net.here(e_h.at[:, pl.ds(0, dt)], wu_v.at[pl.ds(0, tokens), pl.ds(0, dt)])]
     for k in (1, 2, 3):
@@ -804,18 +886,14 @@
         tiles_v[slot, pl.ds(0, tile), pl.ds(0, dt)] = acc
         return net.here(tiles_v.at[slot, pl.ds(0, tile), pl.ds(0, dt)], wdo.at[pl.ds(j * tile, tile), :])
 
-    up.step0()
-    up.sent_locally()
-    h_in = net.here(h_h, st3.at[pl.ds(0, sub), :])
     n_tiles = ff // tile
-    loads = {0: u_load(0)}
-    if n_tiles > 1:
-        loads[1] = u_load(1)
+    loads = {0: u_load(0), 1: u_load(1)}
+    rsc.send_mid(1)
+    rsc.send_mid(0)
     for c in e_in:
         c.wait()
-    done = {0: down_tile(0, 0, loads[0])}
-    if n_tiles > 1:
-        done[1] = down_tile(1, 1, loads[1])
+    done = [down_tile(0, 0, loads[0]), down_tile(1, 1, loads[1])]
+    loads = {2: u_load(2), 3: u_load(3)}
     for c in third:
         c.wait()
     ag.step3_end()
@@ -827,56 +905,41 @@
         @pl.loop(0, width // qt)
         def _(j):
             cols = ds(j * qt, qt)
-            n_v[rows, cols] = dot(n2_v[rows, :], wq_v[:, cols]).astype(BF16)
+            wu_v[ds(tokens + b * sub, sub), cols] = dot(n2_v[rows, :], wq_v[:, cols]).astype(BF16)
 
     def q_cp(k, block):
-        return net.copy(n_v.at[ds(peer[k] * sub, sub), pl.ds(0, width)], qx.at[ds(block * sub, sub), :], q_id + k, q_id + k, tx=peer[k])
+        return net.copy(wu_v.at[ds(tokens + peer[k] * sub, sub), pl.ds(0, width)], qx.at[ds(block * sub, sub), :], q_id + k, q_id + k, tx=peer[k])
 
     for k in far_first:
         q_cp(k, tx).start()
-    q_own = net.here(n_v.at[ds(tx * sub, sub), pl.ds(0, width)], qx.at[ds(tx * sub, sub), :])
-    for c in done.values():
+    q_own = net.here(wu_v.at[ds(tokens + tx * sub, sub), pl.ds(0, width)], qx.at[ds(tx * sub, sub), :])
+    for c in done:
         c.wait()
     qkv.step3()
     qkv.step1()
-    qkv.step2()
+    done = [down_tile(2, 0, loads[2]), down_tile(3, 1, loads[3])]
     h_in.wait()
     rsc.finish()
     dg_v[pl.ds(0, 8), :] = jnp.zeros((8, dim), F32)
     step = 16
 
-    def norm_rows(right, left):
-        @pl.loop(0, sub // step)
-        def _(r):
-            view = ds(r * step, step)
-            dy = p_v[ds(z * sub + r * step, step), :].astype(F32)
-            if right:
-                dy += rbuf[ds(z * sub + r * step, step), :].astype(F32)
-            if left:
-                dy += rbuf[ds(4 * sub + r * step, step), :].astype(F32)
-            x = st3[view, :].astype(F32)
-            inv = lax.rsqrt(jnp.sum(x * x, axis=1, keepdims=True) / dim + NORM_EPS)
-            xhat = x * inv
-            gain = gains[0:1, :]
-            part = dy * xhat
-            dg_v[pl.ds(0, 8), :] += part[:8] + part[8:]
-            inner = jnp.sum(part * gain, axis=1, keepdims=True) / dim
-            db_v[view, :] = (dres_v[view, :] + inv * (dy * gain) - xhat * (inv * inner)).astype(BF16)
-
-    @pl.when(z == 0)
-    def _():
-        norm_rows(True, False)
-
-    @pl.when(z == 3)
-    def _():
-        norm_rows(False, True)
-
-    @pl.when(mid(z))
-    def _():
-        norm_rows(True, True)
+    @pl.loop(0, sub // step)
+    def _(r):
+        view, mine, far = ds(r * step, step), ds(z * sub + r * step, step), ds(4 * sub + r * step, step)
+        right = jnp.where(z < 3, rbuf[mine, :].astype(F32), 0.0)
+        left = jnp.where(z > 0, rbuf[far, :].astype(F32), 0.0)
+        dy = p_v[mine, :].astype(F32) + right + left
+        x = st3[view, :].astype(F32)
+        inv = lax.rsqrt(jnp.sum(x * x, axis=1, keepdims=True) / dim + NORM_EPS)
+        xhat = x * inv
+        gain = gains[0:1, :]
+        part = dy * xhat
+        dg_v[pl.ds(0, 8), :] += part[:8] + part[8:]
+        inner = jnp.sum(part * gain, axis=1, keepdims=True) / dim
+        st1[view, :] = (dres_v[view, :] + inv * (dy * gain) - xhat * (inv * inner)).astype(BF16)
 
     def h_cp(k, block):
-        return net.copy(db_v.at[pl.ds(0, sub), pl.ds(k * dt, dt)], dh_o.at[ds(block * sub, sub), :], h_id + k, h_id + k, tx=peer[k])
+        return net.copy(st1.at[pl.ds(0, sub), pl.ds(k * dt, dt)], dh_o.at[ds(block * sub, sub), :], h_id + k, h_id + k, tx=peer[k])
 
     def t_cp(k):
         return net.copy(dg_v.at[:, pl.ds(k * dt, dt)], dgr.at[k], t_id + k, t_id + k, tx=peer[k])
@@ -888,16 +951,17 @@
         t_cp(k).start()
     for k in far_first:
         h_cp(k, tx).start()
-    h_own = net.here(db_v.at[pl.ds(0, sub), pl.ds(0, dt)], dh_o.at[ds(tx * sub, sub), :])
-    qkv.step0()
-    for j in range(2, n_tiles):
-        loads[j] = u_load(j)
-    done = [down_tile(j, j % 2, loads[j]) for j in range(2, n_tiles)]
+    h_own = net.here(st1.at[pl.ds(0, sub), pl.ds(0, dt)], dh_o.at[ds(tx * sub, sub), :])
+    qkv.step2()
+    up.sent()
+    for c in done:
+        c.wait()
+    up.step0(cross_g)
     for k in far_first:
         q_cp(k, peer[k]).wait_recv()
     q_own.wait()
-    net.here(qx, n_v.at[:, pl.ds(width, width)]).wait()
-    turned = n_v.at[:, pl.ds(width, width)]
+    turned = wu_v.at[pl.ds(tokens, tokens), pl.ds(width, width)]
+    net.here(qx, turned).wait()
     turn(turned, turned, tokens, width, q_width, tab_v, swap_v, False)
     q_out = net.here(turned, q_o)
     for k in far_first:
@@ -911,12 +975,11 @@
     dg_out = net.here(dgz.at[0], dg_o)
     for k in far_first:
         h_cp(k, peer[k]).wait_recv()
-    for c in done + [q_out, dg_out, h_own]:
+    qkv.step0(cross_g.at[:, pl.ds(0, width)])
+    for c in (q_out, dg_out, h_own):
         c.wait()
-    gate.finish()
-    up.finish()
     qkv.sent_locally()
-    qkv.finish()
+    qkv.sent()
     for k in far_first:
         q_cp(k, tx).wait_send()
         h_cp(k, tx).wait_send()
@@ -974,12 +1037,9 @@
 
         (normed_all, grad_gate, grad_up, u_all, gate_w, up_w, w_qkv, back_all, h_rows, gains, res_all, normed2, grad_res, resid_out, gattn8,
          u_other, e_other) = call_ab(q_width, hidden, back, table, swap, grad_h2, w_gate, w_up, w_down, w_qkv_own, gin)
-        (wg_own, wg_far, wu_own, wu_far, grad_wdown, wq_own, wq_far, qkv_out, grad_hidden, gain_grads, *_) = call_c(
+        (grad_wgate, _, grad_wup, _, grad_wdown, grad_wqkv, _, qkv_out, grad_hidden, gain_grads, *_) = call_c(
             q_width, grad_gate, grad_up, gate_w, up_w, normed_all, u_all, u_other, res_all, e_other, normed2, back_all, w_qkv,
             h_rows, grad_res, gains, gattn8, table, swap)
-        grad_wgate = wg_own + wg_far.astype(F32)
-        grad_wup = wu_own + wu_far.astype(F32)
-        grad_wqkv = wq_own + wq_far.astype(F32)
         grad_wq = grad_wqkv[:, :q_width].reshape(dt, q_heads, head_dim)
         grad_wkv = grad_wqkv[:, q_width:].reshape(dt, kv_heads, head_dim)
         q_out = qkv_out[:, :q_width].reshape(tokens, q_heads, head_dim)

time: 500 us -> 475 us (0.950)
  the two profiles are of different devices: /device:TPU:13 before, /device:TPU:0 now
where the time goes in v2:
time: 475 us; the launch traced here: 473 us
  Pallas kernels  436 us (92%)
  local copies, waits for them, and re-layouts  26.2 us (6%)
  other arithmetic  9.98 us (2%)
    pallas_call x1, Pallas kernels, call_ab(): pl.pallas_call(functools.partial(kernel_ab, q_width), out_shape=shapes, i...  275 us
    pallas_call x1, Pallas kernels, call_c(): pl.pallas_call(functools.partial(kernel_c, q_width), out_shape=shapes, in...  161 us
    unnamed x21, local copies, waits for them, and re-layouts  12.5 us

profile of v2, /device:TPU:0, one launch (start us, length us, event | category | flops | bytes accessed | tf_op | source)
XLA Modules:
  0.0 472.6 jit_solution(3993791024312057906)
XLA Ops:
  0.7 0.7 stack.17
  4.2 1.2 copy.35
  5.4 1.3 copy.34
  6.6 0.9 pad_maximum_fusion.1.wq
  8.3 1.2 pad_maximum_fusion.eqh
  9.6 4.1 multiply_cosine_fusion
  14.1 1.8 reshape.211.tabh
  16.0 274.8 %phase_ab.1 = (bf16[1024,2048]{1,0:T(8,128)(2,1)}, bf16[1024,2048]{1,0:T(8,128)(2,1)}, bf16[1024,2048]{1,0:T(8,128)(2,1)}, bf16[1024,2048]{1,0:T(8,128)(2,1)}, b...) custom-call(bf16[1024,512]{1,0:T(8,128)(2,1)} %hid.1, ...), custom_call_target="tpu_custom_call" | custom-call | flops 85899345920 | bytes 100000000 | tf_op jit(solution)/shard_map/phase_ab/pallas_call | solution.py:699
  290.8 160.8 %phase_c.1 = (f32[512,2048]{1,0:T(8,128)}, bf16[512,2048]{1,0:T(8,128)(2,1)}, f32[512,2048]{1,0:T(8,128)}, bf16[512,2048]{1,0:T(8,128)(2,1)}, f32[2048,512]{1,0:...) custom-call(bf16[1024,2048]{1,0:T(8,128)(2,1)} %get-tuple-element.36, ...), custom_call_target="tpu_custom_call" | custom-call | flops 85899345920 | bytes 100000000 | tf_op jit(solution)/shard_map/phase_c/pallas_call | solution.py:1002
  451.6 1.3 slice_reduce_fusion
  453.0 1.1 slice.19
  454.0 1.3 slice.18
  455.3 1.3 copy.36
  456.7 1.0 copy.37
  457.9 1.3 copy.38
  459.2 1.0 copy.39
  460.2 1.0 copy.45
  461.1 1.0 copy.46
  462.1 1.1 copy-done.2
  463.2 2.1 copy.47
  465.3 1.6 copy-done.1
  466.9 2.1 copy.48
  469.0 1.6 copy-done
  470.6 2.0 copy.49
  (26 shorter events, 4.2 us)
Async XLA Ops:
  0.6 6.9 %copy-start.7 = (bf16[1024,4,64]{0,2,1:T(8,128)(2,1)S(1)}, bf16[1024,4,64]{0,2,1:T(8,128)(2,1)}, u32[]{:S(2)}) copy-start(bf16[1024,4,64]{0,2,1:T(8,128)(2,1)} %param.23) | copy-start | bytes 1572868
  4.2 3.6 copy-start.4
  455.3 2.3 copy-start.3
  457.8 2.3 copy-start.5
  459.2 2.0 copy-start.6
  460.2 3.0 copy-start.2
  463.2 3.7 copy-start.1
  466.9 3.7 copy-start

commit v3 on v2

--- a/solution.py
+++ b/solution.py
@@ -2,6 +2,7 @@
 
 import jax
 import jax.numpy as jnp
+import numpy as np
 from jax import lax
 from jax.experimental import pallas as pl
 from jax.experimental.pallas import tpu as pltpu
@@ -346,8 +347,87 @@
     return dp, z, tx, (tx, tx + 1 - 2 * (tx % 2), (tx + 2) % 4, 3 - tx)
 
 
-def kernel_ab(q_width, hid, eqh, tabh, swaph, dh2h, wg, wu, wd, wq, gin,
-              n_o, da_o, db_o, u_o, wg_o, wu_o, wq_o, eq_o, h_o, g_o, e_o, n2_o, dres_o, home_o, dg_o, ux_o, ex_o,
+ROWS_ROWS = (((0,), (0,)), ((), ()))
+
+
+class GradReduce:
+    def __init__(self, net, peer, tile, tiles, st3, st1, cross, stage, got2, got0, got_y, out, out_tiles):
+        self.net, self.peer, self.tile, self.tiles = net, peer, tile, tiles
+        self.st3, self.st1, self.cross, self.stage = st3, st1, cross, stage
+        self.got2, self.got0, self.got_y, self.out, self.out_tiles = got2, got0, got_y, out, out_tiles
+        self.src = None
+        self.base = net.take(3)
+        self.w = out.shape[1] // tiles
+
+    def cp(self, i):
+        src, dst, to = ((self.st3, self.got2, 1), (self.st1, self.got0, 1), (self.src or self.cross, self.got_y, 2))[i]
+        return self.net.copy(src, dst, self.base + i, self.base + i, tx=self.peer[to])
+
+    def fill(self, k, ref):
+        @pl.loop(0, self.tiles)
+        def _(j):
+            ref[:, ds(j * self.w, self.w)] = self.tile(k, j).astype(BF16)
+
+    def step3(self):
+        self.fill(3, self.st3)
+        self.cp(0).start()
+
+    def step1(self):
+        self.fill(1, self.st1)
+        self.cp(1).start()
+
+    def step2(self, received=False):
+        if not received:
+            self.cp(0).wait_recv()
+        self.net.here(self.got2, self.stage).wait()
+
+        @pl.loop(0, self.tiles)
+        def _(j):
+            cols = ds(j * self.w, self.w)
+            self.cross[:, cols] = (self.tile(2, j) + self.stage[:, cols].astype(F32)).astype(BF16)
+
+    def send(self, src=None):
+        self.src = src
+        self.cp(2).start()
+
+    def step0(self, far):
+        self.cp(1).wait_recv()
+        self.cp(2).wait_recv()
+        loads = [self.net.here(self.got0, self.stage), self.net.here(self.got_y, far)]
+        for c in loads:
+            c.wait()
+        base = self.net.n_local
+        self.net.n_local += 2
+
+        def put(j, slot):
+            src = self.out_tiles.at[slot, :, pl.ds(0, self.w)]
+            return pltpu.make_async_copy(src, self.out.at[:, ds(j * self.w, self.w)], self.net.local.at[base + slot])
+
+        @pl.loop(0, self.tiles)
+        def _(j):
+            cols = ds(j * self.w, self.w)
+            slot = j % 2
+
+            @pl.when(j >= 2)
+            def _():
+                put(j, slot).wait()
+
+            self.out_tiles[slot, :, pl.ds(0, self.w)] = self.tile(0, j) + (self.stage[:, cols].astype(F32) + far[:, cols].astype(F32))
+            put(j, slot).start()
+
+        for slot in range(min(2, self.tiles)):
+            put(slot, slot).wait()
+
+    def sent_locally(self):
+        self.cp(0).wait_send()
+        self.cp(1).wait_send()
+
+    def sent(self):
+        self.cp(2).wait_send()
+
+
+def kernel_ab(q_width, hid, eqh, ekvh, angh, swaph, dh2h, wg, wu, wd, wq, gin,
+              n_o, da_o, db_o, u_o, wg_o, wu_o, wq_o, eq_o, h_o, g_o, e_o, n2_o, dres_o, home_o, dg_o, ux_o, ex_o, tab_o, g2_o, d2_o, d0_o, dc_o,
               rows, dh2_v, n2_v, res_v, dres_v, n_v, a_v, b_v, wg_v, wu_v, wd_v, wq_v, eq_v, p_v, rbuf, rbuf2, gains, dg_v, swap_v, send, recv, local):
     dp, z, tx, peer = places()
     sub, dim = rows.shape
@@ -361,7 +441,8 @@
     dtile = min(512, dim)
     hs = sub // 2
     net = Wires(send, recv, local)
-    turn_in = [net.here(eqh, p_v.at[:, pl.ds(0, width)]), net.here(tabh, dres_v), net.here(swaph, swap_v)]
+    turn_in = [net.here(eqh, p_v.at[:, pl.ds(0, q_width)]), net.here(ekvh, p_v.at[:, pl.ds(q_width, width - q_width)]), net.here(swaph, swap_v)]
+    turn_in += [net.here(angh.at[pl.ds(i * sub, sub), :], dres_v.at[:, pl.ds(i * 128, 128)]) for i in range(4)]
     entry_barrier([{"tx": peer[1]}, {"tx": peer[2]}, {"tx": peer[3]}, {"dp": 1 - dp}], z)
 
     pos = (dp, peer[1], peer[2])
@@ -387,7 +468,8 @@
 
     def ux_cp(k, b):
         view = ds(b * sub, sub)
-        src = ux_o.at[1, view, :] if k == 3 else wg_v.at[view, :]
+        cols = pl.ds(0, ff - ff // 4)
+        src = ux_o.at[1, view, :] if k == 3 else wg_v.at[view, cols]
         i = u_id + (k - 1) * 4 + b
         return net.copy(src, ux_o.at[k - 1, view, :], i, i, tx=peer[1] if k == 3 else peer[k])
 
@@ -415,6 +497,25 @@
         w.start_local()
     for c in turn_in:
         c.wait()
+
+    @pl.loop(0, 4)
+    def _(i):
+        cos_q, cos_kv, sin_q, sin_kv = (ds(i * 128 + n * 512, 128) for n in range(4))
+        angles = dres_v[:, cos_q]
+        dres_v[:, sin_q] = jnp.sin(angles)
+        dres_v[:, cos_q] = jnp.cos(angles)
+
+        @pl.when(z < 2)
+        def _():
+            dres_v[:, cos_kv] = dres_v[:, cos_q]
+            dres_v[:, sin_kv] = dres_v[:, sin_q]
+
+        @pl.when(z >= 2)
+        def _():
+            dres_v[:, cos_kv] = jnp.ones((sub, 128), F32)
+            dres_v[:, sin_kv] = jnp.zeros((sub, 128), F32)
+
+    tab_out = net.here(dres_v.at[:, pl.ds(0, 2048)], tab_o)
     turn(p_v, p_v, tokens, width, q_width, dres_v, swap_v, True)
     for k in far_first:
         e_cp(k, tx).start()
@@ -553,12 +654,12 @@
 
     rs2[1].send_end(2)
     dg_v[...] = jnp.zeros_like(dg_v)
-    for k in far_first:
-        d_cp(k).wait_recv()
-    d_own.wait()
     for i in (2, 1, 0):
         rs2[0].send_mid(i)
     rsc.finish()
+    for k in far_first:
+        d_cp(k).wait_recv()
+    d_own.wait()
     step = 16
 
     def norm_half(half):
@@ -606,6 +707,7 @@
 
     s1, s2, s3 = ag.slots
     rs2[0].finish()
+    tab_out.wait()
     norm_half(0)
     ag2[0].start()
     rs2[1].send_end(1)
@@ -626,6 +728,11 @@
         o_cp(k, tx).start()
     outs += [net.here(res_v.at[:, pl.ds(0, dt)], home_o.at[ds(tx * sub, sub), :]), net.here(n2_v, n2_o), net.here(dres_v.at[:, pl.ds(0, dim)], dres_o), net.here(dg_v, dg_o)]
 
+    rsc.drain()
+    for h in range(2):
+        rs2[h].drain()
+    n_in = net.here(n_o, p_v)
+
     def back_events_1():
         ag2[1].near_mid()
         ag2[1].far_mid()
@@ -660,6 +767,24 @@
 
     outs.append(net.here(e_v, e_o))
     outs += [net.here(a_v, da_o), net.here(b_v, db_o)]
+
+    last = pl.ds(ff - ff // 4, ff // 4)
+
+    def down_tile(k, j):
+        return dot(wg_v[pl.ds(0, tokens), last], wg_v[pl.ds(tokens, tokens), pl.ds(k * dt, dt)], ROWS_ROWS)
+
+    def gate_tile(k, j):
+        return dot(p_v[:, pl.ds(k * dt, dt)], a_v[:, ds(j * (ff // 4), ff // 4)], ROWS_ROWS)
+
+    quarter = [rbuf.at[pl.ds(0, ff // 4), pl.ds(i * dt, dt)] for i in range(4)]
+    part_d = GradReduce(net, peer, down_tile, 1, quarter[0], quarter[1], quarter[2], quarter[3], d2_o, d0_o, None, dc_o, None)
+    part_g = GradReduce(net, peer, gate_tile, 4, n_v.at[pl.ds(0, dt), :], None, None, None, g2_o, None, None, wg_o, None)
+    n_in.wait()
+    part_d.step3()
+    part_d.step1()
+    part_g.step3()
+    part_d.step2()
+    outs.append(net.here(quarter[2], dc_o))
     for k in far_first:
         o_cp(k, peer[k]).wait_recv()
         for b in range(4):
@@ -681,110 +806,37 @@
             ex_cp(k, b, 1).wait_send()
     for w in (qkv, up, down):
         w.drain()
-    rsc.drain()
     for h in range(2):
-        rs2[h].drain()
         ag2[h].drain()
-
-
-def call_ab(q_width, hid, eqh, tab, swap, dh2h, wg, wu, wd, wq, gin):
+    part_d.cp(1).wait_recv()
+    part_d.sent_locally()
+    part_g.cp(0).wait_recv()
+    part_g.cp(0).wait_send()
+
+
+def call_ab(hid, eqh, ekvh, ang, swap, dh2h, wg, wu, wd, wq, gin):
     tokens, dt = hid.shape
-    sub, dim, ff, width = tokens // 4, dt * 4, wg.shape[1], wq.shape[1]
+    sub, dim, ff, width, q_width = tokens // 4, dt * 4, wg.shape[1], wq.shape[1], eqh.shape[1]
     s = jax.ShapeDtypeStruct
     tok_ff, tok_d, row = s((tokens, ff), BF16), s((tokens, dim), BF16), s((sub, dim), BF16)
     shapes = (tok_d, tok_ff, tok_ff, tok_ff, s((dim, ff), BF16), s((dim, ff), BF16), s((dim, width), BF16), s((tokens, width), BF16),
               row, s((8, dim), F32), tok_d, row, s((sub, dim), F32), s((tokens, dt), BF16), s((8, dim), F32),
-              s((3, tokens, ff), BF16), s((3, tokens, dt), BF16))
+              s((3, tokens, ff - ff // 4), BF16), s((3, tokens, dt), BF16), s((sub, 2048), F32), s((dt, ff), BF16)) + (s((ff // 4, dt), BF16),) * 3
     vrow, vtok, vff = VMEM((sub, dim), BF16), VMEM((tokens, dim), BF16), VMEM((tokens, ff), BF16)
     return pl.pallas_call(
-        functools.partial(kernel_ab, q_width), out_shape=shapes, in_specs=[ANY] * 10, out_specs=[ANY] * len(shapes),
+        functools.partial(kernel_ab, q_width), out_shape=shapes, in_specs=[ANY] * 11, out_specs=[ANY] * len(shapes),
         scratch_shapes=[
             vrow, vrow, vrow, vrow, VMEM((sub, max(dim, 2048)), F32), vtok, vff, vff, VMEM((dim, ff), BF16), VMEM((dim, ff), BF16), VMEM((ff, dim), BF16),
             VMEM((dim, width), BF16), VMEM((tokens, width), BF16), vtok, VMEM((5 * sub, dim), BF16), VMEM((5 * sub, dim), BF16),
             VMEM((8, dim), F32), VMEM((8, dim), F32), VMEM((128, 128), BF16),
-            pltpu.SemaphoreType.DMA((160,)), pltpu.SemaphoreType.DMA((160,)), pltpu.SemaphoreType.DMA((40,))],
+            pltpu.SemaphoreType.DMA((170,)), pltpu.SemaphoreType.DMA((170,)), pltpu.SemaphoreType.DMA((48,))],
         compiler_params=pltpu.CompilerParams(collective_id=0, has_side_effects=True, vmem_limit_bytes=VMEM_LIMIT),
         cost_estimate=pl.CostEstimate(flops=20 * tokens * dim * ff, bytes_accessed=100000000, transcendentals=0), name="phase_ab",
-    )(hid, eqh, tab, swap, dh2h, wg, wu, wd, wq, gin)
-
-
-ROWS_ROWS = (((0,), (0,)), ((), ()))
-
-
-class GradReduce:
-    def __init__(self, net, peer, tile, tiles, st3, st1, cross, stage, got2, got0, got_y, out, out_tiles):
-        self.net, self.peer, self.tile, self.tiles = net, peer, tile, tiles
-        self.st3, self.st1, self.cross, self.stage = st3, st1, cross, stage
-        self.got2, self.got0, self.got_y, self.out, self.out_tiles = got2, got0, got_y, out, out_tiles
-        self.base = net.take(3)
-        self.w = out.shape[1] // tiles
-
-    def cp(self, i):
-        src, dst, to = ((self.st3, self.got2, 1), (self.st1, self.got0, 1), (self.cross, self.got_y, 2))[i]
-        return self.net.copy(src, dst, self.base + i, self.base + i, tx=self.peer[to])
-
-    def fill(self, k, ref):
-        @pl.loop(0, self.tiles)
-        def _(j):
-            ref[:, ds(j * self.w, self.w)] = self.tile(k, j).astype(BF16)
-
-    def step3(self):
-        self.fill(3, self.st3)
-        self.cp(0).start()
-
-    def step1(self):
-        self.fill(1, self.st1)
-        self.cp(1).start()
-
-    def step2(self):
-        self.cp(0).wait_recv()
-        self.net.here(self.got2, self.stage).wait()
-
-        @pl.loop(0, self.tiles)
-        def _(j):
-            cols = ds(j * self.w, self.w)
-            self.cross[:, cols] = (self.tile(2, j) + self.stage[:, cols].astype(F32)).astype(BF16)
-
-        self.cp(2).start()
-
-    def step0(self, far):
-        self.cp(1).wait_recv()
-        self.cp(2).wait_recv()
-        loads = [self.net.here(self.got0, self.stage), self.net.here(self.got_y, far)]
-        for c in loads:
-            c.wait()
-        base = self.net.n_local
-        self.net.n_local += 2
-
-        def put(j, slot):
-            src = self.out_tiles.at[slot, :, pl.ds(0, self.w)]
-            return pltpu.make_async_copy(src, self.out.at[:, ds(j * self.w, self.w)], self.net.local.at[base + slot])
-
-        @pl.loop(0, self.tiles)
-        def _(j):
-            cols = ds(j * self.w, self.w)
-            slot = j % 2
-
-            @pl.when(j >= 2)
-            def _():
-                put(j, slot).wait()
-
-            self.out_tiles[slot, :, pl.ds(0, self.w)] = self.tile(0, j) + (self.stage[:, cols].astype(F32) + far[:, cols].astype(F32))
-            put(j, slot).start()
-
-        for slot in range(min(2, self.tiles)):
-            put(slot, slot).wait()
-
-    def sent_locally(self):
-        self.cp(0).wait_send()
-        self.cp(1).wait_send()
-
-    def sent(self):
-        self.cp(2).wait_send()
-
-
-def kernel_c(q_width, da_h, db_h, wg_h, wu_h, n_h, u_h, ux_h, e_h, ex_h, n2_h, eq_h, wq_h, h_h, dres_h, g_h, dga_h, tabh, swaph,
-             wgo, wgy, wuo, wuy, wdo, wqo, wqy, q_o, dh_o, dg_o, g2, g0, u2, u0, q2, q0, qx,
+    )(hid, eqh, ekvh, ang, swap, dh2h, wg, wu, wd, wq, gin)
+
+
+def kernel_c(q_width, da_h, db_h, wg_h, wu_h, n_h, u_h, ux_h, e_h, ex_h, n2_h, eq_h, wq_h, h_h, dres_h, g_h, dga_h, tabh, swaph, g2, d0, dc,
+             wgo, wgy, wuo, wuy, wdo, wqo, wqy, q_o, kv_o, dh_o, dg_o, g0, u2, u0, q2, q0, qx, dy,
              wg_v, wu_v, da_v, db_v, n_v, p_v, rbuf, n2_v, st3, st1, cross_g, cross_u, stage, tiles_v, dres_v, wq_v, eq_v,
              gains, dg_v, dgr, dgz, tab_v, swap_v, send, recv, local):
     dp, z, tx, peer = places()
@@ -820,7 +872,12 @@
 
     gate = GradReduce(net, peer, grad_tile(n_v, da_v, tile), ff // tile, st3, st1, cross_g, stage, g2, g0, wgy, wgo, tiles_v)
     up = GradReduce(net, peer, grad_tile(n_v, db_v, tile), ff // tile, st3, st1, cross_u, stage, u2, u0, wuy, wuo, tiles_v)
-    half = tokens // 2
+    d_id = net.take(1)
+
+    def dy_cp():
+        return net.copy(dc, dy, d_id, d_id, tx=peer[2])
+
+    dy_cp().start()
 
     def corner(r, c):
         return da_v.at[pl.ds(r * dt, dt), pl.ds(c * width, width)]
@@ -840,9 +897,9 @@
     ag.start()
     for c in first:
         c.wait()
-    gate.step3()
+    gate.step2(True)
+    gate.send()
     gate.step1()
-    gate.step2()
     for c in second:
         c.wait()
 
@@ -853,10 +910,11 @@
         for step in range(3):
             pl.when(i == step)(lambda step=step: rsc.send_end(2 - step))
 
-    gate.sent_locally()
+    gate.cp(1).wait_send()
     up.step3()
     up.step1()
     up.step2()
+    up.send()
     rsc.send_mid(2)
     ag.step2()
     ag.step3_mid()
@@ -865,6 +923,7 @@
     gate.step0(st1)
     gate.sent()
 
+    n_tiles = ff // tile
     e_in = [net.here(e_h.at[:, pl.ds(0, dt)], wu_v.at[pl.ds(0, tokens), pl.ds(0, dt)])]
     for k in (1, 2, 3):
         e_in.append(net.here(ex_h.at[k - 1], wu_v.at[pl.ds(0, tokens), pl.ds(k * dt, dt)]))
@@ -874,26 +933,29 @@
 
     def u_load(j):
         cols = pl.ds(j * tile, tile)
+        if j == n_tiles - 1:
+            return [net.here(u_h.at[:, cols], u_place(j, 0)), net.here(d0, stage.at[pl.ds(0, tile), pl.ds(0, dt)]), net.here(dy, stage.at[pl.ds(0, tile), pl.ds(dt, dt)])]
         return [net.here(u_h.at[:, cols] if k == 0 else ux_h.at[k - 1, :, cols], u_place(j, k)) for k in range(4)]
 
     def down_tile(j, slot, loads):
         for c in loads:
             c.wait()
         acc = None
-        for k in range(4):
+        if j == n_tiles - 1:
+            acc = stage[pl.ds(0, tile), pl.ds(0, dt)].astype(F32) + stage[pl.ds(0, tile), pl.ds(dt, dt)].astype(F32)
+        for k in range(1 if j == n_tiles - 1 else 4):
             part = dot(u_place(j, k)[...], wu_v[pl.ds(0, tokens), pl.ds(k * dt, dt)], ROWS_ROWS)
             acc = part if acc is None else acc + part
         tiles_v[slot, pl.ds(0, tile), pl.ds(0, dt)] = acc
         return net.here(tiles_v.at[slot, pl.ds(0, tile), pl.ds(0, dt)], wdo.at[pl.ds(j * tile, tile), :])
 
-    n_tiles = ff // tile
     loads = {0: u_load(0), 1: u_load(1)}
     rsc.send_mid(1)
     rsc.send_mid(0)
     for c in e_in:
         c.wait()
     done = [down_tile(0, 0, loads[0]), down_tile(1, 1, loads[1])]
-    loads = {2: u_load(2), 3: u_load(3)}
+    loads = {2: u_load(2)}
     for c in third:
         c.wait()
     ag.step3_end()
@@ -917,6 +979,8 @@
         c.wait()
     qkv.step3()
     qkv.step1()
+    dy_cp().wait_recv()
+    loads[3] = u_load(3)
     done = [down_tile(2, 0, loads[2]), down_tile(3, 1, loads[3])]
     h_in.wait()
     rsc.finish()
@@ -953,6 +1017,7 @@
         h_cp(k, tx).start()
     h_own = net.here(st1.at[pl.ds(0, sub), pl.ds(0, dt)], dh_o.at[ds(tx * sub, sub), :])
     qkv.step2()
+    qkv.send()
     up.sent()
     for c in done:
         c.wait()
@@ -963,7 +1028,8 @@
     turned = wu_v.at[pl.ds(tokens, tokens), pl.ds(width, width)]
     net.here(qx, turned).wait()
     turn(turned, turned, tokens, width, q_width, tab_v, swap_v, False)
-    q_out = net.here(turned, q_o)
+    q_out = net.here(wu_v.at[pl.ds(tokens, tokens), pl.ds(width, q_width)], q_o)
+    kv_out = net.here(wu_v.at[pl.ds(tokens, tokens), pl.ds(width + q_width, width - q_width)], kv_o)
     for k in far_first:
         t_cp(k).wait_recv()
     dgr[0] = dg_v[:, pl.ds(0, dt)] + dgr[1] + dgr[2] + dgr[3]
@@ -976,8 +1042,9 @@
     for k in far_first:
         h_cp(k, peer[k]).wait_recv()
     qkv.step0(cross_g.at[:, pl.ds(0, width)])
-    for c in (q_out, dg_out, h_own):
+    for c in (q_out, kv_out, dg_out, h_own):
         c.wait()
+    dy_cp().wait_send()
     qkv.sent_locally()
     qkv.sent()
     for k in far_first:
@@ -997,8 +1064,8 @@
     s = jax.ShapeDtypeStruct
     wf, wb = s((dt, ff), F32), s((dt, ff), BF16)
     qf, qb = s((dt, width), F32), s((dt, width), BF16)
-    shapes = (wf, wb, wf, wb, s((ff, dt), F32), qf, qb, s((tokens, width), BF16), s((tokens, dt), BF16), s((16, dt), F32),
-              wb, wb, wb, wb, qb, qb, s((tokens, width), BF16))
+    shapes = (wf, wb, wf, wb, s((ff, dt), F32), qf, qb, s((tokens, q_width), BF16), s((tokens, width - q_width), BF16), s((tokens, dt), BF16), s((16, dt), F32),
+              wb, wb, wb, qb, qb, s((tokens, width), BF16), s((tile, dt), BF16))
     return pl.pallas_call(
         functools.partial(kernel_c, q_width), out_shape=shapes, in_specs=[ANY] * len(args), out_specs=[ANY] * len(shapes),
         scratch_shapes=[
@@ -1019,31 +1086,26 @@
         q_heads, head_dim = w_q.shape[1:]
         kv_heads = w_kv.shape[1]
         q_width, kv_width = q_heads * head_dim, kv_heads * head_dim
-        width = q_width + kv_width
-
-        lane = jnp.arange(128)
-        inv_freq = ROPE_BASE ** (-((lane % head_dim) // 2 * 2).astype(F32) / head_dim)
-        angles = positions.astype(F32)[:, None] * inv_freq[None, :]
-        cos_t = jnp.cos(angles)
-        swap = (lane[:, None] == (lane + 1 - lane % 2 * 2)[None, :]).astype(BF16)
-        sin_t = jnp.sin(angles) * jnp.where(lane % 2 == 0, -1.0, 1.0)[None, :]
-
-        turns = lax.axis_index("ty") < mesh.shape["ty"] // 2
-        table = jnp.stack([cos_t, jnp.where(turns, cos_t, 1.0), sin_t, jnp.where(turns, sin_t, 0.0)])
-        table = table.reshape(4, 4, tokens // 4, 128).transpose(2, 0, 1, 3).reshape(tokens // 4, 2048)
-        back = jnp.concatenate([grad_q.reshape(tokens, q_width), grad_kv.reshape(tokens, kv_width)], axis=1)
+
+        lane = np.arange(128)
+        inv_freq = ROPE_BASE ** (-(lane % head_dim // 2 * 2).astype(np.float32) / head_dim)
+        angles = positions.astype(F32)[:, None] * jnp.asarray(inv_freq, F32)[None, :]
+        swap = np.zeros((128, 128), np.float32)
+        swap[lane, lane ^ 1] = np.where(lane % 2 == 0, 1.0, -1.0)
+        swap = jnp.asarray(swap, BF16)
         w_qkv_own = jnp.concatenate([w_q.reshape(dt, q_width), w_kv.reshape(dt, kv_width)], axis=1)
-        gin = jnp.concatenate([jnp.stack([g_ffn, g_attn]).astype(F32), jnp.zeros((6, dt), F32)])
+        gin = jnp.where(jnp.arange(8)[:, None] == 0, g_ffn[None, :], g_attn[None, :]).astype(F32)
 
         (normed_all, grad_gate, grad_up, u_all, gate_w, up_w, w_qkv, back_all, h_rows, gains, res_all, normed2, grad_res, resid_out, gattn8,
-         u_other, e_other) = call_ab(q_width, hidden, back, table, swap, grad_h2, w_gate, w_up, w_down, w_qkv_own, gin)
-        (grad_wgate, _, grad_wup, _, grad_wdown, grad_wqkv, _, qkv_out, grad_hidden, gain_grads, *_) = call_c(
+         u_other, e_other, table, wg_two, _, wd_zero, wd_cross) = call_ab(
+             hidden, grad_q.reshape(tokens, q_width), grad_kv.reshape(tokens, kv_width), angles, swap, grad_h2, w_gate, w_up, w_down, w_qkv_own, gin)
+        (grad_wgate, _, grad_wup, _, grad_wdown, grad_wqkv, _, q_flat, kv_flat, grad_hidden, gain_grads, *_) = call_c(
             q_width, grad_gate, grad_up, gate_w, up_w, normed_all, u_all, u_other, res_all, e_other, normed2, back_all, w_qkv,
-            h_rows, grad_res, gains, gattn8, table, swap)
+            h_rows, grad_res, gains, gattn8, table, swap, wg_two, wd_zero, wd_cross)
         grad_wq = grad_wqkv[:, :q_width].reshape(dt, q_heads, head_dim)
         grad_wkv = grad_wqkv[:, q_width:].reshape(dt, kv_heads, head_dim)
-        q_out = qkv_out[:, :q_width].reshape(tokens, q_heads, head_dim)
-        kv_out = qkv_out[:, q_width:].reshape(tokens, kv_heads, head_dim)
+        q_out = q_flat.reshape(tokens, q_heads, head_dim)
+        kv_out = kv_flat.reshape(tokens, kv_heads, head_dim)
         grad_gffn = jnp.sum(gain_grads[:8], axis=0)
         grad_gattn = jnp.sum(gain_grads[8:], axis=0)
         return (resid_out, q_out, kv_out, grad_hidden, grad_gffn, grad_gattn, grad_wgate, grad_wup, grad_wdown, grad_wq, grad_wkv)

time: 475 us -> 468 us (0.985)
    unnamed x21 -> x23, local copies, waits for them, and re-layouts: 12.5 us -> 12.5 us
where the time goes in v3:
time: 468 us; the launch traced here: 467 us
  Pallas kernels  437 us (93%)
  local copies, waits for them, and re-layouts  23 us (5%)
  other arithmetic  6.13 us (1%)
    pallas_call x1, Pallas kernels, call_ab(): pl.pallas_call(functools.partial(kernel_ab, q_width), out_shape=shapes, i...  275 us
    pallas_call x1, Pallas kernels, call_c(): pl.pallas_call(functools.partial(kernel_c, q_width), out_shape=shapes, in...  163 us
    unnamed x23, local copies, waits for them, and re-layouts  12.5 us

profile of v3, /device:TPU:0, one launch (start us, length us, event | category | flops | bytes accessed | tf_op | source)
XLA Modules:
  0.0 467.3 jit_solution(14113485490269099826)
XLA Ops:
  0.7 0.7 convert_element_type.6
  1.4 1.4 select_convert_fusion.gin
  2.8 1.1 copy.34
  3.9 1.7 broadcast_multiply_fusion.angh
  5.6 1.3 copy.33
  6.9 0.9 pad_maximum_fusion.wq
  7.8 1.0 copy.36.ekvh
  8.8 1.3 copy.35.eqh
  10.1 274.9 %phase_ab.1 = (bf16[1024,2048]{1,0:T(8,128)(2,1)}, bf16[1024,2048]{1,0:T(8,128)(2,1)}, bf16[1024,2048]{1,0:T(8,128)(2,1)}, bf16[1024,2048]{1,0:T(8,128)(2,1)}, b...) custom-call(bf16[1024,512]{1,0:T(8,128)(2,1)} %hid.1, ...), custom_call_target="tpu_custom_call" | custom-call | flops 85899345920 | bytes 100000000 | tf_op jit(solution)/shard_map/phase_ab/pallas_call | solution.py:826
  285.0 162.6 %phase_c.1 = (f32[512,2048]{1,0:T(8,128)}, bf16[512,2048]{1,0:T(8,128)(2,1)}, f32[512,2048]{1,0:T(8,128)}, bf16[512,2048]{1,0:T(8,128)(2,1)}, f32[2048,512]{1,0:...) custom-call(bf16[1024,2048]{1,0:T(8,128)(2,1)} %get-tuple-element.41, ...), custom_call_target="tpu_custom_call" | custom-call | flops 85899345920 | bytes 100000000 | tf_op jit(solution)/shard_map/phase_c/pallas_call | solution.py:1069
  447.6 2.4 copy.37
  450.0 1.3 slice_reduce_fusion
  451.4 1.0 copy.38
  452.4 0.1 slice.14
  452.6 1.3 copy.39
  453.9 1.0 copy.40
  454.9 1.0 copy.46
  455.9 1.0 copy.47
  456.8 1.1 copy-done.2
  457.9 2.1 copy.48
  460.0 1.6 copy-done.1
  461.6 2.1 copy.49
  463.7 1.6 copy-done
  465.3 2.0 copy.50
  (17 shorter events, 0.1 us)
Async XLA Ops:
  0.6 7.2 %copy-start.7 = (bf16[1024,4,64]{0,2,1:T(8,128)(2,1)S(1)}, bf16[1024,4,64]{0,2,1:T(8,128)(2,1)}, u32[]{:S(2)}) copy-start(bf16[1024,4,64]{0,2,1:T(8,128)(2,1)} %param.25) | copy-start | bytes 1572868
  3.9 4.9 %copy-start.4 = (bf16[1024,8,64]{0,2,1:T(8,128)(2,1)S(1)}, bf16[1024,8,64]{0,2,1:T(8,128)(2,1)}, u32[]{:S(2)}) copy-start(bf16[1024,8,64]{0,2,1:T(8,128)(2,1)} %param.24) | copy-start | bytes 3145732
  447.6 3.8 copy-start.8
  447.6 4.8 %copy-start.3 = (f32[512,768]{1,0:T(8,128)S(1)}, f32[512,768]{1,0:T(8,128)}, u32[]{:S(2)}) copy-start(f32[512,768]{1,0:T(8,128)} %get-tuple-element.68) | copy-start | bytes 4718596
  452.6 2.3 copy-start.5
  453.9 2.0 copy-start.6
  454.9 3.0 copy-start.2
  457.9 3.7 copy-start.1
  461.6 3.7 copy-start

commit v4 on v3

--- a/solution.py
+++ b/solution.py
@@ -262,43 +262,53 @@
     def __init__(self, net, w, full, pos, by_rows, chunks, direct=0):
         self.net, self.w, self.full, self.by_rows = net, w, full, by_rows
         self.dp, self.t1, self.t2 = pos
-        self.len = w.shape[0]
+        self.half = w.shape[0] // 2
         self.width = w.shape[0] if by_rows else w.shape[1]
-        self.chunks = chunks
-        self.piece = self.len // 2 // chunks
-        self.direct = direct
+        self.chunks, self.direct = chunks, direct
         self.base = net.take(1 + 4 * chunks + direct)
 
-    def dst(self, k, off, n):
+    def area(self, half, ch):
         if self.by_rows:
-            return self.full.at[ds(k * self.width + off, n, min(n, 16)), :]
-        return self.full.at[ds(off, n, 16), pl.ds(k * self.width, self.width)]
-
-    def off(self, half, ch):
-        return half * (self.len // 2) + ch * self.piece
+            n = self.w.shape[1] // self.chunks
+            return ds(half * self.half, self.half, 16), self.half, pl.ds(ch * n, n)
+        n = self.half // self.chunks
+        return ds(half * self.half + ch * n, n, 16), n, pl.ds(0, self.width)
+
+    def src(self, half, ch):
+        rows, _, cols = self.area(half, ch)
+        return self.w.at[rows, cols]
+
+    def dst(self, k, half, ch):
+        if self.by_rows:
+            _, _, cols = self.area(half, ch)
+            return self.full.at[ds(k * self.width + half * self.half, self.half, 16), cols]
+        rows, _, _ = self.area(half, ch)
+        return self.full.at[rows, pl.ds(k * self.width, self.width)]
+
+    def whole(self, k):
+        if self.by_rows:
+            return self.full.at[pl.ds(k * self.width, self.width), :]
+        return self.full.at[:, pl.ds(k * self.width, self.width)]
 
     def near(self, ch):
-        o = self.off(self.dp, ch)
         i = self.base + 1 + ch
-        return self.net.copy(self.w.at[ds(o, self.piece, 16), :], self.dst(2, o, self.piece), i, i, tx=self.t2)
+        return self.net.copy(self.src(self.dp, ch), self.dst(2, self.dp, ch), i, i, tx=self.t2)
 
     def cross(self, ch, half):
-        o = self.off(half, ch)
         i = self.base + 1 + self.chunks + ch
-        return self.net.copy(self.dst(2, o, self.piece), self.dst(2, o, self.piece), i, i, dp=1 - self.dp)
+        return self.net.copy(self.dst(2, half, ch), self.dst(2, half, ch), i, i, dp=1 - self.dp)
 
     def diag(self, ch, which, half):
-        o = self.off(half, ch)
         i = self.base + 1 + (2 + which) * self.chunks + ch
-        return self.net.copy(self.dst(2, o, self.piece), self.dst(3, o, self.piece), i, i, tx=self.t1)
+        return self.net.copy(self.dst(2, half, ch), self.dst(3, half, ch), i, i, tx=self.t1)
 
     def mate(self):
-        return self.net.copy(self.w, self.dst(1, 0, self.len), self.base, self.base, tx=self.t1)
+        return self.net.copy(self.w, self.whole(1), self.base, self.base, tx=self.t1)
 
     def straight(self, n, half):
-        o = self.off(half, self.chunks - 1 - n)
+        ch = self.chunks - 1 - n
         i = self.base + 1 + 4 * self.chunks + n
-        return self.net.copy(self.w.at[ds(o, self.piece, 16), :], self.dst(2, o, self.piece), i, i, tx=self.t2)
+        return self.net.copy(self.src(half, ch), self.dst(2, half, ch), i, i, tx=self.t2)
 
     def start_y(self):
         for ch in range(self.chunks):
@@ -307,7 +317,7 @@
             self.straight(n, 1 - self.dp).start()
 
     def start_local(self):
-        self.own = self.net.here(self.w, self.dst(0, 0, self.len))
+        self.own = self.net.here(self.w, self.whole(0))
         self.mate().start()
 
     def y_event(self, ch):
@@ -323,12 +333,13 @@
             self.straight(self.chunks - 1 - ch, 1 - self.dp).wait_recv()
         self.diag(ch, 1, 1 - self.dp).start()
 
-    def finish(self):
+    def finish_local(self):
         self.own.wait()
         self.mate().wait_recv()
-        for ch in range(self.chunks):
-            self.diag(ch, 0, self.dp).wait_recv()
-            self.diag(ch, 1, 1 - self.dp).wait_recv()
+
+    def finish(self, ch):
+        self.diag(ch, 0, self.dp).wait_recv()
+        self.diag(ch, 1, 1 - self.dp).wait_recv()
 
     def drain(self):
         self.mate().wait_send()
@@ -546,7 +557,8 @@
     ag.step1()
     qkv.y_event(0)
     qkv.x_event(0)
-    qkv.finish()
+    qkv.finish_local()
+    qkv.finish(0)
     for k in far_first:
         e_cp(k, tx).wait_send()
 
@@ -561,65 +573,83 @@
         n2_block(pick(3 - i, z))
         for step in range(3):
             pl.when(i == step)(lambda step=step: rsc.send_end(2 - step))
-
-    gate.y_event(0)
+        pl.when(i == 0)(lambda: gate.y_event(0))
+
+    wide = ff // 2
+
+    def gate_part(b, c):
+        cols = pl.ds(c * wide, wide)
+        a_v[ds(b * sub, sub), cols] = dot(n_v[ds(b * sub, sub), :], wg_v[:, cols]).astype(BF16)
+
+    def up_part(b, c):
+        cols = pl.ds(c * wide, wide)
+        bb = dot(n_v[ds(b * sub, sub), :], wu_v[:, cols]).astype(BF16)
+        b_v[ds(b * sub, sub), cols] = bb
+        aa = a_v[ds(b * sub, sub), cols].astype(F32)
+        wg_v[ds(b * sub, sub), cols] = (aa * jax.nn.sigmoid(aa) * bb.astype(F32)).astype(BF16)
+
+    def down_part(b, j):
+        cols = pl.ds(j * (dim // 2), dim // 2)
+        n_v[ds(b * sub, sub), cols] = dot(wg_v[ds(b * sub, sub), :], wd_v[:, cols]).astype(BF16)
+
+    outs += [net.here(wq_v, wq_o), net.here(eq_v, eq_o)]
+    gate.finish_local()
     gate.y_event(1)
-    gate.x_event(0)
     ag.step2()
     ag.step3_mid()
+    gate.x_event(0)
+    gate.finish(0)
+
+    @pl.loop(0, 3)
+    def _(i):
+        gate_part(pick(i, z), 0)
+
     up.y_event(0)
     gate.x_event(1)
-    gate.finish()
-
-    def gate_block(b):
-        @pl.loop(0, ff // wide)
-        def _(j):
-            cols = ds(j * wide, wide)
-            a_v[ds(b * sub, sub), cols] = dot(n_v[ds(b * sub, sub), :], wg_v[:, cols]).astype(BF16)
-
-    def up_block(b):
-        @pl.loop(0, ff // wide)
-        def _(j):
-            cols = ds(j * wide, wide)
-            bb = dot(n_v[ds(b * sub, sub), :], wu_v[:, cols]).astype(BF16)
-            b_v[ds(b * sub, sub), cols] = bb
-            aa = a_v[ds(b * sub, sub), cols].astype(F32)
-            wg_v[ds(b * sub, sub), cols] = (aa * jax.nn.sigmoid(aa) * bb.astype(F32)).astype(BF16)
-
+    rsc.send_mid(2)
+    gate.finish(1)
     wg_out = net.here(wg_v, wg_o)
-    outs += [net.here(wq_v, wq_o), net.here(eq_v, eq_o)]
-    def gate_events_2():
-        rsc.send_mid(2)
-
-    def gate_events_3():
-        up.y_event(1)
-        up.x_event(0)
-        ag.step3_end()
+
+    @pl.loop(0, 3)
+    def _(i):
+        gate_part(pick(i, z), 1)
+
+    up.finish_local()
+    up.y_event(1)
+    up.x_event(0)
+    up.finish(0)
+    ag.step3_end()
+
+    @pl.loop(0, 2)
+    def _(c):
+        cols = ds(c * wide, wide)
+        b = pick(3, z)
+        a_v[ds(b * sub, sub), cols] = dot(n_v[ds(b * sub, sub), :], wg_v[:, cols]).astype(BF16)
+
+    wg_out.wait()
+    n_out = net.here(n_v, n_o)
 
     @pl.loop(0, 4)
     def _(i):
-        pl.when(i == 2)(gate_events_2)
-        pl.when(i == 3)(gate_events_3)
-        gate_block(pick(i, z))
-
-    n_out = net.here(n_v, n_o)
-    wg_out.wait()
-    down.y_event(0)
-    up.x_event(1)
-    up.finish()
-    outs.append(net.here(wu_v, wu_o))
+        pl.when(i == 1)(lambda: down.y_event(0))
+        pl.when(i == 2)(lambda: down.y_event(1))
+        pl.when(i == 3)(lambda: up.x_event(1))
+        up_part(pick(i, z), 0)
 
     def up_events_1():
         rsc.send_mid(1)
         rsc.send_mid(0)
+        down.x_event(0)
 
     def up_events_2():
-        down.y_event(1)
-        down.x_event(0)
+        down.y_event(2)
 
     def up_events_3():
-        down.y_event(2)
+        down.y_event(3)
         down.x_event(1)
+
+    up.finish(1)
+    outs.append(net.here(wu_v, wu_o))
 
     @pl.loop(0, 4)
     def _(i):
@@ -627,7 +657,7 @@
         pl.when(i == 2)(up_events_2)
         pl.when(i == 3)(up_events_3)
         b = pick(i, z)
-        up_block(b)
+        up_part(b, 1)
         ux_cp(2, b).start()
         ux_cp(1, b).start()
 
@@ -635,20 +665,20 @@
     ag.drain()
     gate.drain()
     n_out.wait()
-    down.y_event(3)
-    down.x_event(2)
-    down.x_event(3)
-    down.finish()
-
-    def down_block(b):
-        @pl.loop(0, dim // dwide)
-        def _(j):
-            cols = ds(j * dwide, dwide)
-            n_v[ds(b * sub, sub), cols] = dot(wg_v[ds(b * sub, sub), :], wd_v[:, cols]).astype(BF16)
+    down.finish_local()
 
     @pl.loop(0, 4)
     def _(i):
-        down_block(pick(3 - i, z))
+        pl.when(i == 2)(lambda: down.x_event(2))
+        pl.when(i == 3)(lambda: down.x_event(3))
+        down_part(pick(3 - i, z), 0)
+
+    for ch in range(4):
+        down.finish(ch)
+
+    @pl.loop(0, 4)
+    def _(i):
+        down_part(pick(3 - i, z), 1)
         for step in range(3):
             pl.when(i == step)(lambda step=step: rs2[0].send_end(2 - step))
 
@@ -710,6 +740,7 @@
     tab_out.wait()
     norm_half(0)
     ag2[0].start()
+    spread(z, 0)
     rs2[1].send_end(1)
     rs2[1].send_end(0)
     rs2[1].send_mid(2)
@@ -718,11 +749,22 @@
     rs2[1].send_mid(1)
     rs2[1].send_mid(0)
     ag2[0].step3_mid()
-    spread(z, 0)
+
+    @pl.when(mid(z))
+    def _():
+        for b in (s1, s2, s3):
+            spread(b, 0)
+
+    @pl.when(end(z))
+    def _():
+        ag2[0].take(0)
+        spread(s1, 0)
+        ag2[0].take(1)
+        spread(s2, 0)
+
     rs2[1].finish()
     norm_half(1)
     ag2[1].start()
-    ag2[0].near_end()
     spread(z, 1)
     for k in far_first:
         o_cp(k, tx).start()
@@ -736,18 +778,22 @@
     def back_events_1():
         ag2[1].near_mid()
         ag2[1].far_mid()
-        spread(s1, 0)
-        ag2[0].step2()
-        spread(s2, 0)
-        ag2[1].near_end()
+
+        @pl.when(end(z))
+        def _():
+            ag2[1].take(0)
+
         spread(s1, 1)
 
     def back_events_2():
-        ag2[1].step2()
+        @pl.when(end(z))
+        def _():
+            ag2[1].take(1)
+            ag2[0].take(2)
+            spread(s3, 0)
+
+        ag2[1].step3_mid()
         spread(s2, 1)
-        ag2[0].step3_end()
-        spread(s3, 0)
-        ag2[1].step3_mid()
         for j in range(4):
             ux_cp(2, ag_order[j]).wait_recv()
             ux_cp(3, ag_order[j]).start()

time: 468 us -> 459 us (0.981)
  Pallas kernels: 437 us -> 429 us
    pallas_call x1, Pallas kernels: 275 us -> 268 us  [call_ab(): pl.pallas_call(functools.partial(kernel_ab, q_width), out_shape=shapes, i...]
where the time goes in v4:
time: 459 us; the launch traced here: 458 us
  Pallas kernels  429 us (93%)
  local copies, waits for them, and re-layouts  23 us (5%)
  other arithmetic  6.13 us (1%)
    pallas_call x1, Pallas kernels, call_ab(): pl.pallas_call(functools.partial(kernel_ab, q_width), out_shape=shapes, i...  268 us
    pallas_call x1, Pallas kernels, call_c(): pl.pallas_call(functools.partial(kernel_c, q_width), out_shape=shapes, in...  161 us
    unnamed x23, local copies, waits for them, and re-layouts  12.5 us

profile of v4, /device:TPU:0, one launch (start us, length us, event | category | flops | bytes accessed | tf_op | source)
XLA Modules:
  0.0 458.4 jit_solution(2705615903879551421)
XLA Ops:
  0.7 0.7 convert_element_type.6
  1.4 1.4 select_convert_fusion.gin
  2.8 1.1 copy.34
  3.9 1.7 broadcast_multiply_fusion.angh
  5.6 1.3 copy.33
  6.9 0.9 pad_maximum_fusion.wq
  7.8 1.0 copy.36.ekvh
  8.8 1.3 copy.35.eqh
  10.1 267.5 %phase_ab.1 = (bf16[1024,2048]{1,0:T(8,128)(2,1)}, bf16[1024,2048]{1,0:T(8,128)(2,1)}, bf16[1024,2048]{1,0:T(8,128)(2,1)}, bf16[1024,2048]{1,0:T(8,128)(2,1)}, b...) custom-call(bf16[1024,512]{1,0:T(8,128)(2,1)} %hid.1, ...), custom_call_target="tpu_custom_call" | custom-call | flops 85899345920 | bytes 100000000 | tf_op jit(solution)/shard_map/phase_ab/pallas_call | solution.py:872
  277.7 161.0 %phase_c.1 = (f32[512,2048]{1,0:T(8,128)}, bf16[512,2048]{1,0:T(8,128)(2,1)}, f32[512,2048]{1,0:T(8,128)}, bf16[512,2048]{1,0:T(8,128)(2,1)}, f32[2048,512]{1,0:...) custom-call(bf16[1024,2048]{1,0:T(8,128)(2,1)} %get-tuple-element.41, ...), custom_call_target="tpu_custom_call" | custom-call | flops 85899345920 | bytes 100000000 | tf_op jit(solution)/shard_map/phase_c/pallas_call | solution.py:1115
  438.7 2.4 copy.37
  441.1 1.3 slice_reduce_fusion
  442.4 1.0 copy.38
  443.5 0.1 slice.14
  443.6 1.3 copy.39
  445.0 1.0 copy.40
  446.0 1.0 copy.46
  446.9 1.0 copy.47
  447.9 1.1 copy-done.2
  449.0 2.1 copy.48
  451.1 1.6 copy-done.1
  452.7 2.1 copy.49
  454.8 1.6 copy-done
  456.4 2.0 copy.50
  (17 shorter events, 0.1 us)
Async XLA Ops:
  0.6 7.2 %copy-start.7 = (bf16[1024,4,64]{0,2,1:T(8,128)(2,1)S(1)}, bf16[1024,4,64]{0,2,1:T(8,128)(2,1)}, u32[]{:S(2)}) copy-start(bf16[1024,4,64]{0,2,1:T(8,128)(2,1)} %param.25) | copy-start | bytes 1572868
  3.9 4.9 %copy-start.4 = (bf16[1024,8,64]{0,2,1:T(8,128)(2,1)S(1)}, bf16[1024,8,64]{0,2,1:T(8,128)(2,1)}, u32[]{:S(2)}) copy-start(bf16[1024,8,64]{0,2,1:T(8,128)(2,1)} %param.24) | copy-start | bytes 3145732
  438.7 3.8 copy-start.8
  438.7 4.8 %copy-start.3 = (f32[512,768]{1,0:T(8,128)S(1)}, f32[512,768]{1,0:T(8,128)}, u32[]{:S(2)}) copy-start(f32[512,768]{1,0:T(8,128)} %get-tuple-element.68) | copy-start | bytes 4718596
  443.6 2.3 copy-start.5
  445.0 2.0 copy-start.6
  446.0 3.0 copy-start.2
  449.0 3.7 copy-start.1
  452.7 3.7 copy-start

commit v5 on v4

--- a/solution.py
+++ b/solution.py
@@ -450,7 +450,7 @@
     tile = min(512, ff)
     dwide = min(1024, dim)
     dtile = min(512, dim)
-    hs = sub // 2
+    hs, cs = sub // 2, sub // 4
     net = Wires(send, recv, local)
     turn_in = [net.here(eqh, p_v.at[:, pl.ds(0, q_width)]), net.here(ekvh, p_v.at[:, pl.ds(q_width, width - q_width)]), net.here(swaph, swap_v)]
     turn_in += [net.here(angh.at[pl.ds(i * sub, sub), :], dres_v.at[:, pl.ds(i * 128, 128)]) for i in range(4)]
@@ -495,8 +495,8 @@
     qkv = WeightGather(net, wq, wq_v, pos, True, 1)
     ag = LineGather(net, n_v, sub, z)
     rsc = LineScatter(net, p_v, rbuf, sub, z)
-    rs2 = [LineScatter(net, n_v, rbuf2, sub, z, h * hs, hs) for h in range(2)]
-    ag2 = [LineGather(net, e_v, sub, z, h * hs, hs) for h in range(2)]
+    rs2 = [LineScatter(net, n_v, rbuf2, sub, z, c * cs, cs) for c in range(4)]
+    ag2 = [LineGather(net, e_v, sub, z, c * cs, cs) for c in range(4)]
 
     for k in far_first:
         g_cp(k).start()
@@ -682,20 +682,16 @@
         for step in range(3):
             pl.when(i == step)(lambda step=step: rs2[0].send_end(2 - step))
 
-    rs2[1].send_end(2)
+    for c in (1, 2, 3):
+        for i in (2, 1, 0):
+            rs2[c].send_end(i)
     dg_v[...] = jnp.zeros_like(dg_v)
-    for i in (2, 1, 0):
-        rs2[0].send_mid(i)
-    rsc.finish()
-    for k in far_first:
-        d_cp(k).wait_recv()
-    d_own.wait()
     step = 16
 
-    def norm_half(half):
-        @pl.loop(0, hs // step)
+    def norm_chunk(c):
+        @pl.loop(0, cs // step)
         def _(r):
-            at = half * hs + r * step
+            at = c * cs + r * step
             view, mine, far = ds(at, step), ds(z * sub + at, step), ds(4 * sub + at, step)
 
             def whole(part, got):
@@ -722,94 +718,82 @@
         for k in far_first:
             ex_cp(k, b, half).start()
 
-    def back_block(b):
-        view = ds(b * sub, sub)
-
-        @pl.loop(0, ff // tile)
-        def _(j):
-            cols = ds(j * tile, tile)
-            du = dot(wg_v[ds(tokens + b * sub, sub), :], wd_v[ds(j * tile, tile), :], NT_DIMS)
-            aa = a_v[view, cols].astype(F32)
-            bb = b_v[view, cols].astype(F32)
-            sig = jax.nn.sigmoid(aa)
-            a_v[view, cols] = (du * bb * sig * (1.0 + aa * (1.0 - sig))).astype(BF16)
-            b_v[view, cols] = (du * aa * sig).astype(BF16)
-
-    s1, s2, s3 = ag.slots
-    rs2[0].finish()
-    tab_out.wait()
-    norm_half(0)
-    ag2[0].start()
-    spread(z, 0)
-    rs2[1].send_end(1)
-    rs2[1].send_end(0)
-    rs2[1].send_mid(2)
-    ag2[0].near_mid()
-    ag2[0].far_mid()
-    rs2[1].send_mid(1)
-    rs2[1].send_mid(0)
-    ag2[0].step3_mid()
-
-    @pl.when(mid(z))
-    def _():
-        for b in (s1, s2, s3):
-            spread(b, 0)
-
-    @pl.when(end(z))
-    def _():
-        ag2[0].take(0)
-        spread(s1, 0)
-        ag2[0].take(1)
-        spread(s2, 0)
-
-    rs2[1].finish()
-    norm_half(1)
-    ag2[1].start()
-    spread(z, 1)
+    def back_tile(b, j):
+        view, cols = ds(b * sub, sub), ds(j * (ff // 4), ff // 4)
+        du = dot(wg_v[ds(tokens + b * sub, sub), :], wd_v[ds(j * (ff // 4), ff // 4), :], NT_DIMS)
+        aa = a_v[view, cols].astype(F32)
+        bb = b_v[view, cols].astype(F32)
+        sig = jax.nn.sigmoid(aa)
+        a_v[view, cols] = (du * bb * sig * (1.0 + aa * (1.0 - sig))).astype(BF16)
+        b_v[view, cols] = (du * aa * sig).astype(BF16)
+
+    def scatter(i, c):
+        return lambda: rs2[c].send_mid(i)
+
+    def gathered(i, c):
+        def go():
+            ag2[c].take(i)
+            pl.when(mid(z))(lambda: ag2[c].forward(i))
+            if c % 2 == 1:
+                spread(ag.slots[i], c // 2)
+        return go
+
+    def run(ops):
+        def go():
+            for op in ops:
+                op()
+        return go
+
+    before_mid = (
+        (scatter(2, 0), scatter(1, 0), scatter(0, 0)),
+        (scatter(2, 1), gathered(1, 0), scatter(1, 1), scatter(0, 1)),
+        (scatter(2, 2), scatter(1, 2), gathered(1, 1), scatter(0, 2), scatter(2, 3)),
+        (scatter(1, 3), scatter(0, 3), gathered(1, 2), gathered(0, 0)))
+    before_end = ((), (gathered(0, 0), gathered(1, 0)), (gathered(0, 1), gathered(1, 1)), (gathered(0, 2),))
+    after_mid = {0: (gathered(0, 1),), 1: (gathered(2, 0),), 2: (gathered(0, 2),), 3: (gathered(1, 3),), 5: (gathered(0, 3),), 7: (gathered(2, 1),),
+                 10: (gathered(2, 2),), 12: (gathered(2, 3),)}
+    after_end = {3: (gathered(1, 2),), 4: (gathered(0, 3),), 7: (gathered(2, 0),), 8: (gathered(1, 3),),
+                 12: (gathered(2, 1), gathered(2, 2), gathered(2, 3))}
+
+    for c in range(4):
+        pl.when(mid(z))(run(before_mid[c]))
+        pl.when(end(z))(run(before_end[c]))
+        if c == 0:
+            rsc.finish()
+            for k in far_first:
+                d_cp(k).wait_recv()
+            d_own.wait()
+            tab_out.wait()
+        rs2[c].finish()
+        norm_chunk(c)
+        ag2[c].start()
+        if c % 2 == 1:
+            spread(z, c // 2)
+
     for k in far_first:
         o_cp(k, tx).start()
     outs += [net.here(res_v.at[:, pl.ds(0, dt)], home_o.at[ds(tx * sub, sub), :]), net.here(n2_v, n2_o), net.here(dres_v.at[:, pl.ds(0, dim)], dres_o), net.here(dg_v, dg_o)]
-
     rsc.drain()
-    for h in range(2):
-        rs2[h].drain()
+    for c in range(4):
+        rs2[c].drain()
     n_in = net.here(n_o, p_v)
-
-    def back_events_1():
-        ag2[1].near_mid()
-        ag2[1].far_mid()
-
-        @pl.when(end(z))
-        def _():
-            ag2[1].take(0)
-
-        spread(s1, 1)
-
-    def back_events_2():
-        @pl.when(end(z))
-        def _():
-            ag2[1].take(1)
-            ag2[0].take(2)
-            spread(s3, 0)
-
-        ag2[1].step3_mid()
-        spread(s2, 1)
-        for j in range(4):
-            ux_cp(2, ag_order[j]).wait_recv()
-            ux_cp(3, ag_order[j]).start()
-
-    def back_events_3():
-        ag2[1].step3_end()
-        spread(s3, 1)
-
-    ag_order = (z, s1, s2, s3)
-
-    @pl.loop(0, 4)
-    def _(i):
-        pl.when(i == 1)(back_events_1)
-        pl.when(i == 2)(back_events_2)
-        pl.when(i == 3)(back_events_3)
-        back_block(pick(i, z))
+    middle = (z + 1) // 2 % 2
+
+    def u_forward():
+        for b in range(4):
+            ux_cp(2, b).wait_recv()
+            ux_cp(3, b).start()
+
+    @pl.loop(0, 16)
+    def _(t):
+        for at, ops in after_mid.items():
+            pl.when(jnp.logical_and(t == at, mid(z)))(run(ops))
+        for at, ops in after_end.items():
+            pl.when(jnp.logical_and(t == at, end(z)))(run(ops))
+        pl.when(t == 8)(u_forward)
+        i = t // 4
+        inner = (i + 1) // 2 % 2
+        back_tile(pick(i + middle * inner * (3 - 2 * i), z), t % 4)
 
     outs.append(net.here(e_v, e_o))
     outs += [net.here(a_v, da_o), net.here(b_v, db_o)]
@@ -852,8 +836,8 @@
             ex_cp(k, b, 1).wait_send()
     for w in (qkv, up, down):
         w.drain()
-    for h in range(2):
-        ag2[h].drain()
+    for c in range(4):
+        ag2[c].drain()
     part_d.cp(1).wait_recv()
     part_d.sent_locally()
     part_g.cp(0).wait_recv()
@@ -875,7 +859,7 @@
             vrow, vrow, vrow, vrow, VMEM((sub, max(dim, 2048)), F32), vtok, vff, vff, VMEM((dim, ff), BF16), VMEM((dim, ff), BF16), VMEM((ff, dim), BF16),
             VMEM((dim, width), BF16), VMEM((tokens, width), BF16), vtok, VMEM((5 * sub, dim), BF16), VMEM((5 * sub, dim), BF16),
             VMEM((8, dim), F32), VMEM((8, dim), F32), VMEM((128, 128), BF16),
-            pltpu.SemaphoreType.DMA((170,)), pltpu.SemaphoreType.DMA((170,)), pltpu.SemaphoreType.DMA((48,))],
+            pltpu.SemaphoreType.DMA((180,)), pltpu.SemaphoreType.DMA((180,)), pltpu.SemaphoreType.DMA((48,))],
         compiler_params=pltpu.CompilerParams(collective_id=0, has_side_effects=True, vmem_limit_bytes=VMEM_LIMIT),
         cost_estimate=pl.CostEstimate(flops=20 * tokens * dim * ff, bytes_accessed=100000000, transcendentals=0), name="phase_ab",
     )(hid, eqh, ekvh, ang, swap, dh2h, wg, wu, wd, wq, gin)

time: 459 us -> 446 us (0.972)
  Pallas kernels: 429 us -> 415 us
    pallas_call x1, Pallas kernels: 268 us -> 256 us  [call_ab(): pl.pallas_call(functools.partial(kernel_ab, q_width), out_shape=shapes, i...]
where the time goes in v5:
time: 446 us; the launch traced here: 445 us
  Pallas kernels  415 us (93%)
  local copies, waits for them, and re-layouts  23 us (5%)
  other arithmetic  6.13 us (1%)
    pallas_call x1, Pallas kernels, call_ab(): pl.pallas_call(functools.partial(kernel_ab, q_width), out_shape=shapes, i...  256 us
    pallas_call x1, Pallas kernels, call_c(): pl.pallas_call(functools.partial(kernel_c, q_width), out_shape=shapes, in...  159 us
    unnamed x23, local copies, waits for them, and re-layouts  12.5 us

profile of v5, /device:TPU:0, one launch (start us, length us, event | category | flops | bytes accessed | tf_op | source)
XLA Modules:
  0.0 445.3 jit_solution(17774659573719846240)
XLA Ops:
  0.7 0.7 convert_element_type.6
  1.4 1.4 select_convert_fusion.gin
  2.8 1.1 copy.34
  3.9 1.7 broadcast_multiply_fusion.angh
  5.6 1.3 copy.33
  6.9 0.9 pad_maximum_fusion.wq
  7.8 1.0 copy.36.ekvh
  8.8 1.3 copy.35.eqh
  10.1 255.9 %phase_ab.1 = (bf16[1024,2048]{1,0:T(8,128)(2,1)}, bf16[1024,2048]{1,0:T(8,128)(2,1)}, bf16[1024,2048]{1,0:T(8,128)(2,1)}, bf16[1024,2048]{1,0:T(8,128)(2,1)}, b...) custom-call(bf16[1024,512]{1,0:T(8,128)(2,1)} %hid.1, ...), custom_call_target="tpu_custom_call" | custom-call | flops 85899345920 | bytes 100000000 | tf_op jit(solution)/shard_map/phase_ab/pallas_call | solution.py:856
  266.1 159.5 %phase_c.1 = (f32[512,2048]{1,0:T(8,128)}, bf16[512,2048]{1,0:T(8,128)(2,1)}, f32[512,2048]{1,0:T(8,128)}, bf16[512,2048]{1,0:T(8,128)(2,1)}, f32[2048,512]{1,0:...) custom-call(bf16[1024,2048]{1,0:T(8,128)(2,1)} %get-tuple-element.41, ...), custom_call_target="tpu_custom_call" | custom-call | flops 85899345920 | bytes 100000000 | tf_op jit(solution)/shard_map/phase_c/pallas_call | solution.py:1099
  425.6 2.4 copy.37
  428.0 1.3 slice_reduce_fusion
  429.3 1.0 copy.38
  430.4 0.1 slice.14
  430.5 1.3 copy.39
  431.8 1.0 copy.40
  432.8 1.0 copy.46
  433.8 1.0 copy.47
  434.8 1.1 copy-done.2
  435.9 2.1 copy.48
  438.0 1.6 copy-done.1
  439.6 2.1 copy.49
  441.7 1.6 copy-done
  443.3 2.0 copy.50
  (17 shorter events, 0.1 us)
Async XLA Ops:
  0.6 7.2 %copy-start.7 = (bf16[1024,4,64]{0,2,1:T(8,128)(2,1)S(1)}, bf16[1024,4,64]{0,2,1:T(8,128)(2,1)}, u32[]{:S(2)}) copy-start(bf16[1024,4,64]{0,2,1:T(8,128)(2,1)} %param.25) | copy-start | bytes 1572868
  3.9 4.9 %copy-start.4 = (bf16[1024,8,64]{0,2,1:T(8,128)(2,1)S(1)}, bf16[1024,8,64]{0,2,1:T(8,128)(2,1)}, u32[]{:S(2)}) copy-start(bf16[1024,8,64]{0,2,1:T(8,128)(2,1)} %param.24) | copy-start | bytes 3145732
  425.6 3.8 copy-start.8
  425.6 4.8 %copy-start.3 = (f32[512,768]{1,0:T(8,128)S(1)}, f32[512,768]{1,0:T(8,128)}, u32[]{:S(2)}) copy-start(f32[512,768]{1,0:T(8,128)} %get-tuple-element.68) | copy-start | bytes 4718596
  430.5 2.3 copy-start.5
  431.8 2.0 copy-start.6
  432.8 3.0 copy-start.2
  435.9 3.7 copy-start.1
  439.6 3.7 copy-start

commit v6 on v5

--- a/solution.py
+++ b/solution.py
@@ -935,14 +935,17 @@
 
     @pl.loop(0, 4)
     def _(i):
-        pl.when(i == 1)(ag.step1)
+        @pl.when(i == 1)
+        def _():
+            up.step3()
+            gate.cp(1).wait_send()
+            up.step1()
+            ag.step1()
+
         dn_block(pick(3 - i, z))
         for step in range(3):
             pl.when(i == step)(lambda step=step: rsc.send_end(2 - step))
 
-    gate.cp(1).wait_send()
-    up.step3()
-    up.step1()
     up.step2()
     up.send()
     rsc.send_mid(2)
@@ -1011,6 +1014,8 @@
     qkv.step1()
     dy_cp().wait_recv()
     loads[3] = u_load(3)
+    qkv.step2()
+    qkv.send()
     done = [down_tile(2, 0, loads[2]), down_tile(3, 1, loads[3])]
     h_in.wait()
     rsc.finish()
@@ -1046,8 +1051,6 @@
     for k in far_first:
         h_cp(k, tx).start()
     h_own = net.here(st1.at[pl.ds(0, sub), pl.ds(0, dt)], dh_o.at[ds(tx * sub, sub), :])
-    qkv.step2()
-    qkv.send()
     up.sent()
     for c in done:
         c.wait()
@@ -1060,6 +1063,7 @@
     turn(turned, turned, tokens, width, q_width, tab_v, swap_v, False)
     q_out = net.here(wu_v.at[pl.ds(tokens, tokens), pl.ds(width, q_width)], q_o)
     kv_out = net.here(wu_v.at[pl.ds(tokens, tokens), pl.ds(width + q_width, width - q_width)], kv_o)
+    qkv.step0(cross_g.at[:, pl.ds(0, width)])
     for k in far_first:
         t_cp(k).wait_recv()
     dgr[0] = dg_v[:, pl.ds(0, dt)] + dgr[1] + dgr[2] + dgr[3]
@@ -1071,7 +1075,6 @@
     dg_out = net.here(dgz.at[0], dg_o)
     for k in far_first:
         h_cp(k, peer[k]).wait_recv()
-    qkv.step0(cross_g.at[:, pl.ds(0, width)])
     for c in (q_out, kv_out, dg_out, h_own):
         c.wait()
     dy_cp().wait_send()

time: 446 us -> 441 us (0.989)
  no operation moved by 1% of the time
where the time goes in v6:
time: 441 us
  Pallas kernels  411 us (93%)
  local copies, waits for them, and re-layouts  23 us (5%)
  other arithmetic  6.13 us (1%)
    pallas_call x1, Pallas kernels, call_ab(): pl.pallas_call(functools.partial(kernel_ab, q_width), out_shape=shapes, i...  256 us
    pallas_call x1, Pallas kernels, call_c(): pl.pallas_call(functools.partial(kernel_c, q_width), out_shape=shapes, in...  155 us
    unnamed x23, local copies, waits for them, and re-layouts  12.5 us

profile of v6, /device:TPU:0, one launch (start us, length us, event | category | flops | bytes accessed | tf_op | source)
XLA Modules:
  0.0 440.8 jit_solution(5100269373237363741)
XLA Ops:
  0.7 0.7 convert_element_type.6
  1.4 1.4 select_convert_fusion.gin
  2.8 1.1 copy.34
  3.9 1.7 broadcast_multiply_fusion.angh
  5.6 1.3 copy.33
  6.9 0.9 pad_maximum_fusion.wq
  7.8 1.0 copy.36.ekvh
  8.8 1.3 copy.35.eqh
  10.1 255.9 %phase_ab.1 = (bf16[1024,2048]{1,0:T(8,128)(2,1)}, bf16[1024,2048]{1,0:T(8,128)(2,1)}, bf16[1024,2048]{1,0:T(8,128)(2,1)}, bf16[1024,2048]{1,0:T(8,128)(2,1)}, b...) custom-call(bf16[1024,512]{1,0:T(8,128)(2,1)} %hid.1, ...), custom_call_target="tpu_custom_call" | custom-call | flops 85899345920 | bytes 100000000 | tf_op jit(solution)/shard_map/phase_ab/pallas_call | solution.py:856
  266.1 155.1 %phase_c.1 = (f32[512,2048]{1,0:T(8,128)}, bf16[512,2048]{1,0:T(8,128)(2,1)}, f32[512,2048]{1,0:T(8,128)}, bf16[512,2048]{1,0:T(8,128)(2,1)}, f32[2048,512]{1,0:...) custom-call(bf16[1024,2048]{1,0:T(8,128)(2,1)} %get-tuple-element.41, ...), custom_call_target="tpu_custom_call" | custom-call | flops 85899345920 | bytes 100000000 | tf_op jit(solution)/shard_map/phase_c/pallas_call | solution.py:1102
  421.1 2.4 copy.37
  423.6 1.3 slice_reduce_fusion
  424.9 1.0 copy.38
  425.9 0.1 slice.14
  426.1 1.3 copy.39
  427.4 1.0 copy.40
  428.4 1.0 copy.46
  429.4 1.0 copy.47
  430.3 1.1 copy-done.2
  431.4 2.1 copy.48
  433.6 1.6 copy-done.1
  435.1 2.1 copy.49
  437.3 1.6 copy-done
  438.8 2.0 copy.50
  (17 shorter events, 0.1 us)
Async XLA Ops:
  0.6 7.2 %copy-start.7 = (bf16[1024,4,64]{0,2,1:T(8,128)(2,1)S(1)}, bf16[1024,4,64]{0,2,1:T(8,128)(2,1)}, u32[]{:S(2)}) copy-start(bf16[1024,4,64]{0,2,1:T(8,128)(2,1)} %param.25) | copy-start | bytes 1572868
  3.9 4.9 %copy-start.4 = (bf16[1024,8,64]{0,2,1:T(8,128)(2,1)S(1)}, bf16[1024,8,64]{0,2,1:T(8,128)(2,1)}, u32[]{:S(2)}) copy-start(bf16[1024,8,64]{0,2,1:T(8,128)(2,1)} %param.24) | copy-start | bytes 3145732
  421.1 3.8 copy-start.8
  421.1 4.8 %copy-start.3 = (f32[512,768]{1,0:T(8,128)S(1)}, f32[512,768]{1,0:T(8,128)}, u32[]{:S(2)}) copy-start(f32[512,768]{1,0:T(8,128)} %get-tuple-element.68) | copy-start | bytes 4718596
  426.1 2.3 copy-start.5
  427.4 2.0 copy-start.6
  428.4 3.0 copy-start.2
  431.4 3.7 copy-start.1
  435.1 3.7 copy-start

commit v7 on v6

--- a/solution.py
+++ b/solution.py
@@ -43,18 +43,19 @@
     return (z + 1 - 2 * (z % 2), 2 - z // 2, 3 - 3 * (z // 2))
 
 
-def turn(src, dst, rows, width, q_width, table_ref, swap_ref, back):
-    step = rows // 4
-
-    @pl.loop(0, 4)
+def turn(x_ref, width, q_width, tokens, table_ref, swap_ref, back):
+    step = min(256, tokens)
+
+    @pl.loop(0, tokens // step)
     def _(r):
-        for c in range(width // 128):
-            cols = pl.ds(c * 128, 128)
-            table = ds(r * 128 + (0 if c * 128 < q_width else 512), 128)
-            x = src[ds(r * step, step), cols]
-            main = x.astype(F32) * table_ref[:, table]
-            side = dot(x, swap_ref[...]) * table_ref[:, ds(r * 128 + (1024 if c * 128 < q_width else 1536), 128)]
-            dst[ds(r * step, step), cols] = (main - side if back else main + side).astype(BF16)
+        cols = ds(r * step, step)
+        for g in range(width // 128):
+            rows = pl.ds(g * 128, 128)
+            base = pl.ds(0 if g * 128 < q_width else 128, 128)
+            x = x_ref[rows, cols]
+            main = x.astype(F32) * table_ref[base, cols]
+            side = dot(swap_ref[...], x) * table_ref[base, ds(tokens + r * step, step)]
+            x_ref[rows, cols] = (main - side if back else main + side).astype(BF16)
 
 
 def pick(i, z):
@@ -368,7 +369,7 @@
         self.got2, self.got0, self.got_y, self.out, self.out_tiles = got2, got0, got_y, out, out_tiles
         self.src = None
         self.base = net.take(3)
-        self.w = out.shape[1] // tiles
+        self.rows, self.w = out.shape[0], out.shape[1] // tiles
 
     def cp(self, i):
         src, dst, to = ((self.st3, self.got2, 1), (self.st1, self.got0, 1), (self.src or self.cross, self.got_y, 2))[i]
@@ -411,7 +412,7 @@
         self.net.n_local += 2
 
         def put(j, slot):
-            src = self.out_tiles.at[slot, :, pl.ds(0, self.w)]
+            src = self.out_tiles.at[slot, pl.ds(0, self.rows), pl.ds(0, self.w)]
             return pltpu.make_async_copy(src, self.out.at[:, ds(j * self.w, self.w)], self.net.local.at[base + slot])
 
         @pl.loop(0, self.tiles)
@@ -423,7 +424,7 @@
             def _():
                 put(j, slot).wait()
 
-            self.out_tiles[slot, :, pl.ds(0, self.w)] = self.tile(0, j) + (self.stage[:, cols].astype(F32) + far[:, cols].astype(F32))
+            self.out_tiles[slot, pl.ds(0, self.rows), pl.ds(0, self.w)] = self.tile(0, j) + (self.stage[:, cols].astype(F32) + far[:, cols].astype(F32))
             put(j, slot).start()
 
         for slot in range(min(2, self.tiles)):
@@ -437,13 +438,13 @@
         self.cp(2).wait_send()
 
 
-def kernel_ab(q_width, hid, eqh, ekvh, angh, swaph, dh2h, wg, wu, wd, wq, gin,
+def kernel_ab(q_width, hid, eqh, ekvh, angh, swaph, dh2h, wg, wu, wd, wq, wkv, gin,
               n_o, da_o, db_o, u_o, wg_o, wu_o, wq_o, eq_o, h_o, g_o, e_o, n2_o, dres_o, home_o, dg_o, ux_o, ex_o, tab_o, g2_o, d2_o, d0_o, dc_o,
               rows, dh2_v, n2_v, res_v, dres_v, n_v, a_v, b_v, wg_v, wu_v, wd_v, wq_v, eq_v, p_v, rbuf, rbuf2, gains, dg_v, swap_v, send, recv, local):
     dp, z, tx, peer = places()
     sub, dim = rows.shape
     tokens = 4 * sub
-    width = eq_v.shape[1]
+    width = eq_v.shape[0]
     dt = dim // 4
     ff = wg.shape[1]
     wide = min(1024, ff)
@@ -452,8 +453,8 @@
     dtile = min(512, dim)
     hs, cs = sub // 2, sub // 4
     net = Wires(send, recv, local)
-    turn_in = [net.here(eqh, p_v.at[:, pl.ds(0, q_width)]), net.here(ekvh, p_v.at[:, pl.ds(q_width, width - q_width)]), net.here(swaph, swap_v)]
-    turn_in += [net.here(angh.at[pl.ds(i * sub, sub), :], dres_v.at[:, pl.ds(i * 128, 128)]) for i in range(4)]
+    turn_in = [net.here(eqh, p_v.at[pl.ds(0, q_width), pl.ds(0, tokens)]), net.here(ekvh, p_v.at[pl.ds(q_width, width - q_width), pl.ds(0, tokens)]),
+               net.here(swaph, swap_v), net.here(angh, dres_v.at[pl.ds(0, 128), pl.ds(0, tokens)])]
     entry_barrier([{"tx": peer[1]}, {"tx": peer[2]}, {"tx": peer[3]}, {"dp": 1 - dp}], z)
 
     pos = (dp, peer[1], peer[2])
@@ -469,7 +470,7 @@
         return net.copy(hid.at[ds(peer[k] * sub, sub), :], rows.at[:, pl.ds(k * dt, dt)], h_id + k, h_id + k, tx=peer[k])
 
     def e_cp(k, block):
-        return net.copy(p_v.at[ds(peer[k] * sub, sub), pl.ds(0, width)], eq_v.at[ds(block * sub, sub), :], e_id + k, e_id + k, tx=peer[k])
+        return net.copy(p_v.at[pl.ds(0, width), ds(peer[k] * sub, sub)], eq_v.at[:, ds(block * sub, sub)], e_id + k, e_id + k, tx=peer[k])
 
     def d_cp(k):
         return net.copy(dh2h.at[ds(peer[k] * sub, sub), :], dh2_v.at[:, pl.ds(k * dt, dt)], d_id + k, d_id + k, tx=peer[k])
@@ -492,7 +493,8 @@
     gate = WeightGather(net, wg, wg_v, pos, True, 2)
     up = WeightGather(net, wu, wu_v, pos, True, 2)
     down = WeightGather(net, wd, wd_v, pos, False, 4, 1)
-    qkv = WeightGather(net, wq, wq_v, pos, True, 1)
+    q_w = WeightGather(net, wq, wq_v.at[pl.ds(0, q_width), :], pos, False, 1)
+    kv_w = WeightGather(net, wkv, wq_v.at[pl.ds(q_width, width - q_width), :], pos, False, 1)
     ag = LineGather(net, n_v, sub, z)
     rsc = LineScatter(net, p_v, rbuf, sub, z)
     rs2 = [LineScatter(net, n_v, rbuf2, sub, z, c * cs, cs) for c in range(4)]
@@ -504,34 +506,36 @@
         h_cp(k).start()
     g_own = net.here(gin, gains.at[:, pl.ds(0, dt)])
     h_own = net.here(hid.at[ds(tx * sub, sub), :], rows.at[:, pl.ds(0, dt)])
-    for w in (qkv, gate, up, down):
+    for w in (q_w, kv_w, gate, up, down):
         w.start_local()
     for c in turn_in:
         c.wait()
 
     @pl.loop(0, 4)
     def _(i):
-        cos_q, cos_kv, sin_q, sin_kv = (ds(i * 128 + n * 512, 128) for n in range(4))
-        angles = dres_v[:, cos_q]
-        dres_v[:, sin_q] = jnp.sin(angles)
-        dres_v[:, cos_q] = jnp.cos(angles)
+        part = tokens // 4
+        cos_c, sin_c = ds(i * part, part), ds(tokens + i * part, part)
+        q_r, kv_r = pl.ds(0, 128), pl.ds(128, 128)
+        angles = dres_v[q_r, cos_c]
+        dres_v[q_r, sin_c] = jnp.sin(angles)
+        dres_v[q_r, cos_c] = jnp.cos(angles)
 
         @pl.when(z < 2)
         def _():
-            dres_v[:, cos_kv] = dres_v[:, cos_q]
-            dres_v[:, sin_kv] = dres_v[:, sin_q]
+            dres_v[kv_r, cos_c] = dres_v[q_r, cos_c]
+            dres_v[kv_r, sin_c] = dres_v[q_r, sin_c]
 
         @pl.when(z >= 2)
         def _():
-            dres_v[:, cos_kv] = jnp.ones((sub, 128), F32)
-            dres_v[:, sin_kv] = jnp.zeros((sub, 128), F32)
-
-    tab_out = net.here(dres_v.at[:, pl.ds(0, 2048)], tab_o)
-    turn(p_v, p_v, tokens, width, q_width, dres_v, swap_v, True)
+            dres_v[kv_r, cos_c] = jnp.ones((128, part), F32)
+            dres_v[kv_r, sin_c] = jnp.zeros((128, part), F32)
+
+    tab_out = net.here(dres_v.at[pl.ds(0, 256), pl.ds(0, 2 * tokens)], tab_o)
+    turn(p_v, width, q_width, tokens, dres_v, swap_v, True)
     for k in far_first:
         e_cp(k, tx).start()
-    e_own = net.here(p_v.at[ds(tx * sub, sub), pl.ds(0, width)], eq_v.at[ds(tx * sub, sub), :])
-    for w in (qkv, gate, up, down):
+    e_own = net.here(p_v.at[pl.ds(0, width), ds(tx * sub, sub)], eq_v.at[:, ds(tx * sub, sub)])
+    for w in (q_w, kv_w, gate, up, down):
         w.start_y()
     for k in far_first:
         d_cp(k).start()
@@ -555,18 +559,21 @@
         e_cp(k, peer[k]).wait_recv()
     e_own.wait()
     ag.step1()
-    qkv.y_event(0)
-    qkv.x_event(0)
-    qkv.finish_local()
-    qkv.finish(0)
+    for w in (q_w, kv_w):
+        w.y_event(0)
+    for w in (q_w, kv_w):
+        w.x_event(0)
+    for w in (q_w, kv_w):
+        w.finish_local()
+        w.finish(0)
     for k in far_first:
         e_cp(k, tx).wait_send()
 
     def n2_block(b):
         @pl.loop(0, dim // dtile)
         def _(j):
-            w = wq_v[ds(j * dtile, dtile), :]
-            p_v[ds(b * sub, sub), ds(j * dtile, dtile)] = dot(eq_v[ds(b * sub, sub), :], w, NT_DIMS).astype(BF16)
+            cols = ds(j * dtile, dtile)
+            p_v[ds(b * sub, sub), cols] = dot(eq_v[:, ds(b * sub, sub)], wq_v[:, cols], ROWS_ROWS).astype(BF16)
 
     @pl.loop(0, 4)
     def _(i):
@@ -772,7 +779,7 @@
 
     for k in far_first:
         o_cp(k, tx).start()
-    outs += [net.here(res_v.at[:, pl.ds(0, dt)], home_o.at[ds(tx * sub, sub), :]), net.here(n2_v, n2_o), net.here(dres_v.at[:, pl.ds(0, dim)], dres_o), net.here(dg_v, dg_o)]
+    outs += [net.here(res_v.at[:, pl.ds(0, dt)], home_o.at[ds(tx * sub, sub), :]), net.here(n2_v, n2_o), net.here(dres_v.at[pl.ds(0, sub), pl.ds(0, dim)], dres_o), net.here(dg_v, dg_o)]
     rsc.drain()
     for c in range(4):
         rs2[c].drain()
@@ -834,7 +841,7 @@
             ux_cp(k, b).wait_send()
             ex_cp(k, b, 0).wait_send()
             ex_cp(k, b, 1).wait_send()
-    for w in (qkv, up, down):
+    for w in (q_w, kv_w, up, down):
         w.drain()
     for c in range(4):
         ag2[c].drain()
@@ -844,36 +851,37 @@
     part_g.cp(0).wait_send()
 
 
-def call_ab(hid, eqh, ekvh, ang, swap, dh2h, wg, wu, wd, wq, gin):
+def call_ab(hid, eqh, ekvh, ang, swap, dh2h, wg, wu, wd, wq, wkv, gin):
     tokens, dt = hid.shape
-    sub, dim, ff, width, q_width = tokens // 4, dt * 4, wg.shape[1], wq.shape[1], eqh.shape[1]
+    sub, dim, ff, q_width = tokens // 4, dt * 4, wg.shape[1], wq.shape[0]
+    width = q_width + wkv.shape[0]
     s = jax.ShapeDtypeStruct
     tok_ff, tok_d, row = s((tokens, ff), BF16), s((tokens, dim), BF16), s((sub, dim), BF16)
-    shapes = (tok_d, tok_ff, tok_ff, tok_ff, s((dim, ff), BF16), s((dim, ff), BF16), s((dim, width), BF16), s((tokens, width), BF16),
+    shapes = (tok_d, tok_ff, tok_ff, tok_ff, s((dim, ff), BF16), s((dim, ff), BF16), s((width, dim), BF16), s((width, tokens), BF16),
               row, s((8, dim), F32), tok_d, row, s((sub, dim), F32), s((tokens, dt), BF16), s((8, dim), F32),
-              s((3, tokens, ff - ff // 4), BF16), s((3, tokens, dt), BF16), s((sub, 2048), F32), s((dt, ff), BF16)) + (s((ff // 4, dt), BF16),) * 3
+              s((3, tokens, ff - ff // 4), BF16), s((3, tokens, dt), BF16), s((256, 2 * tokens), F32), s((dt, ff), BF16)) + (s((ff // 4, dt), BF16),) * 3
     vrow, vtok, vff = VMEM((sub, dim), BF16), VMEM((tokens, dim), BF16), VMEM((tokens, ff), BF16)
     return pl.pallas_call(
-        functools.partial(kernel_ab, q_width), out_shape=shapes, in_specs=[ANY] * 11, out_specs=[ANY] * len(shapes),
+        functools.partial(kernel_ab, q_width), out_shape=shapes, in_specs=[ANY] * 12, out_specs=[ANY] * len(shapes),
         scratch_shapes=[
-            vrow, vrow, vrow, vrow, VMEM((sub, max(dim, 2048)), F32), vtok, vff, vff, VMEM((dim, ff), BF16), VMEM((dim, ff), BF16), VMEM((ff, dim), BF16),
-            VMEM((dim, width), BF16), VMEM((tokens, width), BF16), vtok, VMEM((5 * sub, dim), BF16), VMEM((5 * sub, dim), BF16),
+            vrow, vrow, vrow, vrow, VMEM((max(sub, 256), max(dim, 2 * tokens)), F32), vtok, vff, vff, VMEM((dim, ff), BF16), VMEM((dim, ff), BF16), VMEM((ff, dim), BF16),
+            VMEM((width, dim), BF16), VMEM((width, tokens), BF16), vtok, VMEM((5 * sub, dim), BF16), VMEM((5 * sub, dim), BF16),
             VMEM((8, dim), F32), VMEM((8, dim), F32), VMEM((128, 128), BF16),
             pltpu.SemaphoreType.DMA((180,)), pltpu.SemaphoreType.DMA((180,)), pltpu.SemaphoreType.DMA((48,))],
         compiler_params=pltpu.CompilerParams(collective_id=0, has_side_effects=True, vmem_limit_bytes=VMEM_LIMIT),
         cost_estimate=pl.CostEstimate(flops=20 * tokens * dim * ff, bytes_accessed=100000000, transcendentals=0), name="phase_ab",
-    )(hid, eqh, ekvh, ang, swap, dh2h, wg, wu, wd, wq, gin)
+    )(hid, eqh, ekvh, ang, swap, dh2h, wg, wu, wd, wq, wkv, gin)
 
 
 def kernel_c(q_width, da_h, db_h, wg_h, wu_h, n_h, u_h, ux_h, e_h, ex_h, n2_h, eq_h, wq_h, h_h, dres_h, g_h, dga_h, tabh, swaph, g2, d0, dc,
-             wgo, wgy, wuo, wuy, wdo, wqo, wqy, q_o, kv_o, dh_o, dg_o, g0, u2, u0, q2, q0, qx, dy,
+             wgo, wgy, wuo, wuy, wdo, wqo, wqy, wvo, wvy, q_o, kv_o, dh_o, dg_o, g0, u2, u0, q2, q0, v2, v0, qx, dy,
              wg_v, wu_v, da_v, db_v, n_v, p_v, rbuf, n2_v, st3, st1, cross_g, cross_u, stage, tiles_v, dres_v, wq_v, eq_v,
              gains, dg_v, dgr, dgz, tab_v, swap_v, send, recv, local):
     dp, z, tx, peer = places()
     tokens, ff = da_v.shape
     sub, dim = dres_v.shape
     dt = dim // 4
-    width = eq_v.shape[1]
+    width = eq_v.shape[0]
     tile = ff // 4
     dtile = min(512, dim)
     qt = min(256, tile)
@@ -909,11 +917,15 @@
 
     dy_cp().start()
 
-    def corner(r, c):
-        return da_v.at[pl.ds(r * dt, dt), pl.ds(c * width, width)]
-
-    qkv = GradReduce(net, peer, grad_tile(n2_v, eq_v, qt), width // qt, corner(0, 0), corner(1, 0), corner(0, 1), corner(1, 1),
-                     q2, q0, wqy, wqo, tiles_v)
+    def head_grad(first, rows, got2, got0, got_y, out):
+        corner = [da_v.at[pl.ds(first, rows), pl.ds(c * dt, dt)] for c in range(4)]
+
+        def tile_of(k, j):
+            return dot(eq_v[pl.ds(first, rows), :], n2_v[:, ds(k * dt + j * qt, qt)])
+
+        return GradReduce(net, peer, tile_of, dt // qt, *corner, got2, got0, got_y, out, tiles_v)
+
+    heads = (head_grad(0, q_width, q2, q0, wqy, wqo), head_grad(q_width, width - q_width, v2, v0, wvy, wvo))
 
     def dn_block(b):
         rows = ds(b * sub, sub)
@@ -993,29 +1005,26 @@
         c.wait()
     ag.step3_end()
 
-    @pl.loop(0, 4)
-    def _(b):
-        rows = ds(b * sub, sub)
-
-        @pl.loop(0, width // qt)
-        def _(j):
-            cols = ds(j * qt, qt)
-            wu_v[ds(tokens + b * sub, sub), cols] = dot(n2_v[rows, :], wq_v[:, cols]).astype(BF16)
+    @pl.loop(0, width // qt)
+    def _(j):
+        wu_v[ds(tokens + j * qt, qt), pl.ds(0, tokens)] = dot(wq_v[ds(j * qt, qt), :], n2_v[...], NT_DIMS).astype(BF16)
 
     def q_cp(k, block):
-        return net.copy(wu_v.at[ds(tokens + peer[k] * sub, sub), pl.ds(0, width)], qx.at[ds(block * sub, sub), :], q_id + k, q_id + k, tx=peer[k])
+        return net.copy(wu_v.at[pl.ds(tokens, width), ds(peer[k] * sub, sub)], qx.at[:, ds(block * sub, sub)], q_id + k, q_id + k, tx=peer[k])
 
     for k in far_first:
         q_cp(k, tx).start()
-    q_own = net.here(wu_v.at[ds(tokens + tx * sub, sub), pl.ds(0, width)], qx.at[ds(tx * sub, sub), :])
+    q_own = net.here(wu_v.at[pl.ds(tokens, width), ds(tx * sub, sub)], qx.at[:, ds(tx * sub, sub)])
     for c in done:
         c.wait()
-    qkv.step3()
-    qkv.step1()
+    for part in heads:
+        part.step3()
+        part.step1()
     dy_cp().wait_recv()
     loads[3] = u_load(3)
-    qkv.step2()
-    qkv.send()
+    for part in heads:
+        part.step2()
+        part.send()
     done = [down_tile(2, 0, loads[2]), down_tile(3, 1, loads[3])]
     h_in.wait()
     rsc.finish()
@@ -1058,12 +1067,13 @@
     for k in far_first:
         q_cp(k, peer[k]).wait_recv()
     q_own.wait()
-    turned = wu_v.at[pl.ds(tokens, tokens), pl.ds(width, width)]
+    turned = wu_v.at[pl.ds(tokens, width), pl.ds(tokens, tokens)]
     net.here(qx, turned).wait()
-    turn(turned, turned, tokens, width, q_width, tab_v, swap_v, False)
-    q_out = net.here(wu_v.at[pl.ds(tokens, tokens), pl.ds(width, q_width)], q_o)
-    kv_out = net.here(wu_v.at[pl.ds(tokens, tokens), pl.ds(width + q_width, width - q_width)], kv_o)
-    qkv.step0(cross_g.at[:, pl.ds(0, width)])
+    turn(turned, width, q_width, tokens, tab_v, swap_v, False)
+    q_out = net.here(wu_v.at[pl.ds(tokens, q_width), pl.ds(tokens, tokens)], q_o)
+    kv_out = net.here(wu_v.at[pl.ds(tokens + q_width, width - q_width), pl.ds(tokens, tokens)], kv_o)
+    heads[0].step0(cross_g.at[pl.ds(0, q_width), pl.ds(0, dt)])
+    heads[1].step0(cross_g.at[pl.ds(0, width - q_width), pl.ds(dt, dt)])
     for k in far_first:
         t_cp(k).wait_recv()
     dgr[0] = dg_v[:, pl.ds(0, dt)] + dgr[1] + dgr[2] + dgr[3]
@@ -1078,8 +1088,9 @@
     for c in (q_out, kv_out, dg_out, h_own):
         c.wait()
     dy_cp().wait_send()
-    qkv.sent_locally()
-    qkv.sent()
+    for part in heads:
+        part.sent_locally()
+        part.sent()
     for k in far_first:
         q_cp(k, tx).wait_send()
         h_cp(k, tx).wait_send()
@@ -1092,21 +1103,22 @@
 def call_c(q_width, *args):
     tokens, ff = args[0].shape
     sub, dim = args[9].shape
-    dt, width = dim // 4, args[10].shape[1]
+    dt, width = dim // 4, args[10].shape[0]
+    rest = width - q_width
     tile = ff // 4
     s = jax.ShapeDtypeStruct
     wf, wb = s((dt, ff), F32), s((dt, ff), BF16)
-    qf, qb = s((dt, width), F32), s((dt, width), BF16)
-    shapes = (wf, wb, wf, wb, s((ff, dt), F32), qf, qb, s((tokens, q_width), BF16), s((tokens, width - q_width), BF16), s((tokens, dt), BF16), s((16, dt), F32),
-              wb, wb, wb, qb, qb, s((tokens, width), BF16), s((tile, dt), BF16))
+    qf, qb, vf, vb = s((q_width, dt), F32), s((q_width, dt), BF16), s((rest, dt), F32), s((rest, dt), BF16)
+    shapes = (wf, wb, wf, wb, s((ff, dt), F32), qf, qb, vf, vb, s((q_width, tokens), BF16), s((rest, tokens), BF16), s((tokens, dt), BF16), s((16, dt), F32),
+              wb, wb, wb, qb, qb, vb, vb, s((width, tokens), BF16), s((tile, dt), BF16))
     return pl.pallas_call(
         functools.partial(kernel_c, q_width), out_shape=shapes, in_specs=[ANY] * len(args), out_specs=[ANY] * len(shapes),
         scratch_shapes=[
             VMEM((dim, ff), BF16), VMEM((dim, ff), BF16), VMEM((tokens, ff), BF16), VMEM((tokens, ff), BF16), VMEM((tokens, dim), BF16),
             VMEM((tokens, dim), BF16), VMEM((5 * sub, dim), BF16), VMEM((tokens, dim), BF16),
             VMEM((dt, ff), BF16), VMEM((dt, ff), BF16), VMEM((dt, ff), BF16), VMEM((dt, ff), BF16), VMEM((dt, ff), BF16),
-            VMEM((2, max(dt, tile), max(dt, tile)), F32), VMEM((sub, dim), F32), VMEM((dim, width), BF16), VMEM((tokens, width), BF16),
-            VMEM((8, dim), F32), VMEM((16, dim), F32), VMEM((4, 16, dt), F32), VMEM((4, 16, dt), F32), VMEM((sub, 2048), F32), VMEM((128, 128), BF16),
+            VMEM((2, max(dt, tile), max(dt, tile)), F32), VMEM((sub, dim), F32), VMEM((width, dim), BF16), VMEM((width, tokens), BF16),
+            VMEM((8, dim), F32), VMEM((16, dim), F32), VMEM((4, 16, dt), F32), VMEM((4, 16, dt), F32), VMEM((256, 2 * tokens), F32), VMEM((128, 128), BF16),
             pltpu.SemaphoreType.DMA((48,)), pltpu.SemaphoreType.DMA((48,)), pltpu.SemaphoreType.DMA((72,))],
         compiler_params=pltpu.CompilerParams(collective_id=2, has_side_effects=True, vmem_limit_bytes=VMEM_LIMIT),
         cost_estimate=pl.CostEstimate(flops=20 * tokens * dim * ff, bytes_accessed=100000000, transcendentals=0), name="phase_c",
@@ -1117,28 +1129,30 @@
     def local_step(hidden, positions, g_ffn, w_gate, w_up, w_down, g_attn, w_q, w_kv, grad_h2, grad_q, grad_kv):
         tokens, dt = hidden.shape
         q_heads, head_dim = w_q.shape[1:]
-        kv_heads = w_kv.shape[1]
-        q_width, kv_width = q_heads * head_dim, kv_heads * head_dim
+        q_width = q_heads * head_dim
 
         lane = np.arange(128)
         inv_freq = ROPE_BASE ** (-(lane % head_dim // 2 * 2).astype(np.float32) / head_dim)
-        angles = positions.astype(F32)[:, None] * jnp.asarray(inv_freq, F32)[None, :]
+        angles = jnp.asarray(inv_freq, F32)[:, None] * positions.astype(F32)[None, :]
         swap = np.zeros((128, 128), np.float32)
-        swap[lane, lane ^ 1] = np.where(lane % 2 == 0, 1.0, -1.0)
+        swap[lane, lane ^ 1] = np.where(lane % 2 == 0, -1.0, 1.0)
         swap = jnp.asarray(swap, BF16)
-        w_qkv_own = jnp.concatenate([w_q.reshape(dt, q_width), w_kv.reshape(dt, kv_width)], axis=1)
+
+        def heads_first(x):
+            return x.transpose(1, 2, 0).reshape(-1, x.shape[0])
+
+        def heads_last(x):
+            return x.reshape(-1, head_dim, x.shape[1]).transpose(2, 0, 1)
+
         gin = jnp.where(jnp.arange(8)[:, None] == 0, g_ffn[None, :], g_attn[None, :]).astype(F32)
 
         (normed_all, grad_gate, grad_up, u_all, gate_w, up_w, w_qkv, back_all, h_rows, gains, res_all, normed2, grad_res, resid_out, gattn8,
          u_other, e_other, table, wg_two, _, wd_zero, wd_cross) = call_ab(
-             hidden, grad_q.reshape(tokens, q_width), grad_kv.reshape(tokens, kv_width), angles, swap, grad_h2, w_gate, w_up, w_down, w_qkv_own, gin)
-        (grad_wgate, _, grad_wup, _, grad_wdown, grad_wqkv, _, q_flat, kv_flat, grad_hidden, gain_grads, *_) = call_c(
+             hidden, heads_first(grad_q), heads_first(grad_kv), angles, swap, grad_h2, w_gate, w_up, w_down, heads_first(w_q), heads_first(w_kv), gin)
+        (grad_wgate, _, grad_wup, _, grad_wdown, grad_wq, _, grad_wkv, _, q_out, kv_out, grad_hidden, gain_grads, *_) = call_c(
             q_width, grad_gate, grad_up, gate_w, up_w, normed_all, u_all, u_other, res_all, e_other, normed2, back_all, w_qkv,
             h_rows, grad_res, gains, gattn8, table, swap, wg_two, wd_zero, wd_cross)
-        grad_wq = grad_wqkv[:, :q_width].reshape(dt, q_heads, head_dim)
-        grad_wkv = grad_wqkv[:, q_width:].reshape(dt, kv_heads, head_dim)
-        q_out = q_flat.reshape(tokens, q_heads, head_dim)
-        kv_out = kv_flat.reshape(tokens, kv_heads, head_dim)
+        q_out, kv_out, grad_wq, grad_wkv = (heads_last(x) for x in (q_out, kv_out, grad_wq, grad_wkv))
         grad_gffn = jnp.sum(gain_grads[:8], axis=0)
         grad_gattn = jnp.sum(gain_grads[8:], axis=0)
         return (resid_out, q_out, kv_out, grad_hidden, grad_gffn, grad_gattn, grad_wgate, grad_wup, grad_wdown, grad_wq, grad_wkv)

time: 441 us -> 435 us (0.986)
  local copies, waits for them, and re-layouts: 23 us -> 17.6 us
    unnamed x23, local copies, waits for them, and re-layouts: 12.5 us -> 17.6 us
    reshape x4 -> x0, local copies, waits for them, and re-layouts: 4.65 us -> none  [the longest x1 1.32 us: local_step(): grad_q.reshape(tokens, q_width)]
where the time goes in v7:
time: 435 us; the launch traced here: 434 us
  Pallas kernels  411 us (94%)
  local copies, waits for them, and re-layouts  17.6 us (4%)
  other arithmetic  5.07 us (1%)
    pallas_call x1, Pallas kernels, call_ab(): pl.pallas_call(functools.partial(kernel_ab, q_width), out_shape=shapes, i...  253 us
    pallas_call x1, Pallas kernels, call_c(): pl.pallas_call(functools.partial(kernel_c, q_width), out_shape=shapes, in...  158 us
    unnamed x23, local copies, waits for them, and re-layouts  17.6 us

profile of v7, /device:TPU:0, one launch (start us, length us, event | category | flops | bytes accessed | tf_op | source)
XLA Modules:
  0.0 434.1 jit_solution(16704942621499527317)
XLA Ops:
  0.7 0.7 convert_element_type.6
  1.3 1.4 select_convert_fusion.gin
  2.7 1.5 broadcast_multiply_fusion.angh
  4.3 252.8 %phase_ab.1 = (bf16[1024,2048]{1,0:T(8,128)(2,1)}, bf16[1024,2048]{1,0:T(8,128)(2,1)}, bf16[1024,2048]{1,0:T(8,128)(2,1)}, bf16[1024,2048]{1,0:T(8,128)(2,1)}, b...) custom-call(bf16[1024,512]{1,0:T(8,128)(2,1)} %hid.1, ...), custom_call_target="tpu_custom_call" | custom-call | flops 85899345920 | bytes 100000000 | tf_op jit(solution)/shard_map/phase_ab/pallas_call | solution.py:864
  257.1 157.9 %phase_c.1 = (f32[512,2048]{1,0:T(8,128)}, bf16[512,2048]{1,0:T(8,128)(2,1)}, f32[512,2048]{1,0:T(8,128)}, bf16[512,2048]{1,0:T(8,128)(2,1)}, f32[2048,512]{1,0:...) custom-call(bf16[1024,2048]{1,0:T(8,128)(2,1)} %get-tuple-element.42, ...), custom_call_target="tpu_custom_call" | custom-call | flops 85899345920 | bytes 100000000 | tf_op jit(solution)/shard_map/phase_c/pallas_call | solution.py:1114
  415.0 0.0 copy-start.6
  415.0 0.0 copy-start.4
  415.0 1.4 slice_reduce_fusion
  416.5 2.3 copy.34
  418.8 2.4 copy.35
  421.2 0.0 copy-done.6
  421.2 0.8 copy.36
  422.0 0.0 copy-done.4
  422.0 1.0 copy.37
  422.9 0.0 copy-done.2
  422.9 2.1 copy.38
  425.1 1.6 copy-done.1
  426.6 2.1 copy.39
  428.8 1.6 copy-done
  430.4 2.0 copy.40
  432.4 0.0 copy-done.3
  432.4 1.0 copy.41
  433.3 0.0 copy-done.5
  433.3 0.8 copy.42
  (6 shorter events, 0.0 us)
Async XLA Ops:
  415.0 6.1 %copy-start.6 = (bf16[256,1024]{1,0:T(8,128)(2,1)S(1)}, bf16[256,1024]{1,0:T(8,128)(2,1)}, u32[]{:S(2)}) copy-start(bf16[256,1024]{1,0:T(8,128)(2,1)} %get-tuple-element.63) | copy-start | bytes 1572868
  415.0 6.9 %copy-start.4 = (bf16[1024,512]{1,0:T(8,128)(2,1)S(1)}, bf16[1024,512]{1,0:T(8,128)(2,1)}, u32[]{:S(2)}) copy-start(bf16[1024,512]{1,0:T(8,128)(2,1)} %get-tuple-element.87) | copy-start | bytes 3145732
  418.8 4.2 copy-start.2
  422.9 3.7 copy-start.1
  426.6 3.7 copy-start
  430.3 2.0 copy-start.3
  430.3 3.0 copy-start.5

commit v8 on v7

--- a/solution.py
+++ b/solution.py
@@ -438,9 +438,9 @@
         self.cp(2).wait_send()
 
 
-def kernel_ab(q_width, hid, eqh, ekvh, angh, swaph, dh2h, wg, wu, wd, wq, wkv, gin,
+def kernel_ab(q_width, hid, eqh, ekvh, posh, invh, swaph, dh2h, wg, wu, wd, wq, wkv, gfh, gah,
               n_o, da_o, db_o, u_o, wg_o, wu_o, wq_o, eq_o, h_o, g_o, e_o, n2_o, dres_o, home_o, dg_o, ux_o, ex_o, tab_o, g2_o, d2_o, d0_o, dc_o,
-              rows, dh2_v, n2_v, res_v, dres_v, n_v, a_v, b_v, wg_v, wu_v, wd_v, wq_v, eq_v, p_v, rbuf, rbuf2, gains, dg_v, swap_v, send, recv, local):
+              rows, dh2_v, n2_v, res_v, dres_v, n_v, a_v, b_v, wg_v, wu_v, wd_v, wq_v, eq_v, p_v, rbuf, rbuf2, gains, dg_v, swap_v, pos_v, inv_v, gf_v, ga_v, gin, send, recv, local):
     dp, z, tx, peer = places()
     sub, dim = rows.shape
     tokens = 4 * sub
@@ -453,8 +453,9 @@
     dtile = min(512, dim)
     hs, cs = sub // 2, sub // 4
     net = Wires(send, recv, local)
+    gain_in = [net.here(gfh, gf_v), net.here(gah, ga_v)]
     turn_in = [net.here(eqh, p_v.at[pl.ds(0, q_width), pl.ds(0, tokens)]), net.here(ekvh, p_v.at[pl.ds(q_width, width - q_width), pl.ds(0, tokens)]),
-               net.here(swaph, swap_v), net.here(angh, dres_v.at[pl.ds(0, 128), pl.ds(0, tokens)])]
+               net.here(swaph, swap_v), net.here(posh, pos_v), net.here(invh, inv_v)]
     entry_barrier([{"tx": peer[1]}, {"tx": peer[2]}, {"tx": peer[3]}, {"dp": 1 - dp}], z)
 
     pos = (dp, peer[1], peer[2])
@@ -501,22 +502,26 @@
     ag2 = [LineGather(net, e_v, sub, z, c * cs, cs) for c in range(4)]
 
     for k in far_first:
-        g_cp(k).start()
-    for k in far_first:
         h_cp(k).start()
+    for c in gain_in:
+        c.wait()
+    gin[...] = jnp.broadcast_to(gf_v[...].astype(F32), gin.shape)
+    gin[1:2, :] = ga_v[...].astype(F32)
     g_own = net.here(gin, gains.at[:, pl.ds(0, dt)])
     h_own = net.here(hid.at[ds(tx * sub, sub), :], rows.at[:, pl.ds(0, dt)])
     for w in (q_w, kv_w, gate, up, down):
         w.start_local()
+    for k in far_first:
+        g_cp(k).start()
     for c in turn_in:
         c.wait()
 
-    @pl.loop(0, 4)
+    @pl.loop(0, tokens // 128)
     def _(i):
-        part = tokens // 4
+        part = 128
         cos_c, sin_c = ds(i * part, part), ds(tokens + i * part, part)
         q_r, kv_r = pl.ds(0, 128), pl.ds(128, 128)
-        angles = dres_v[q_r, cos_c]
+        angles = inv_v[...] * pos_v[:, cos_c].astype(F32)
         dres_v[q_r, sin_c] = jnp.sin(angles)
         dres_v[q_r, cos_c] = jnp.cos(angles)
 
@@ -851,7 +856,7 @@
     part_g.cp(0).wait_send()
 
 
-def call_ab(hid, eqh, ekvh, ang, swap, dh2h, wg, wu, wd, wq, wkv, gin):
+def call_ab(hid, eqh, ekvh, pos, inv, swap, dh2h, wg, wu, wd, wq, wkv, gf, ga):
     tokens, dt = hid.shape
     sub, dim, ff, q_width = tokens // 4, dt * 4, wg.shape[1], wq.shape[0]
     width = q_width + wkv.shape[0]
@@ -862,15 +867,16 @@
               s((3, tokens, ff - ff // 4), BF16), s((3, tokens, dt), BF16), s((256, 2 * tokens), F32), s((dt, ff), BF16)) + (s((ff // 4, dt), BF16),) * 3
     vrow, vtok, vff = VMEM((sub, dim), BF16), VMEM((tokens, dim), BF16), VMEM((tokens, ff), BF16)
     return pl.pallas_call(
-        functools.partial(kernel_ab, q_width), out_shape=shapes, in_specs=[ANY] * 12, out_specs=[ANY] * len(shapes),
+        functools.partial(kernel_ab, q_width), out_shape=shapes, in_specs=[ANY] * 14, out_specs=[ANY] * len(shapes),
         scratch_shapes=[
             vrow, vrow, vrow, vrow, VMEM((max(sub, 256), max(dim, 2 * tokens)), F32), vtok, vff, vff, VMEM((dim, ff), BF16), VMEM((dim, ff), BF16), VMEM((ff, dim), BF16),
             VMEM((width, dim), BF16), VMEM((width, tokens), BF16), vtok, VMEM((5 * sub, dim), BF16), VMEM((5 * sub, dim), BF16),
-            VMEM((8, dim), F32), VMEM((8, dim), F32), VMEM((128, 128), BF16),
+            VMEM((8, dim), F32), VMEM((8, dim), F32), VMEM((128, 128), BF16), VMEM((1, tokens), jnp.int32), VMEM((128, 128), F32),
+            VMEM((1, dt), BF16), VMEM((1, dt), BF16), VMEM((8, dt), F32),
             pltpu.SemaphoreType.DMA((180,)), pltpu.SemaphoreType.DMA((180,)), pltpu.SemaphoreType.DMA((48,))],
         compiler_params=pltpu.CompilerParams(collective_id=0, has_side_effects=True, vmem_limit_bytes=VMEM_LIMIT),
         cost_estimate=pl.CostEstimate(flops=20 * tokens * dim * ff, bytes_accessed=100000000, transcendentals=0), name="phase_ab",
-    )(hid, eqh, ekvh, ang, swap, dh2h, wg, wu, wd, wq, wkv, gin)
+    )(hid, eqh, ekvh, pos, inv, swap, dh2h, wg, wu, wd, wq, wkv, gf, ga)
 
 
 def kernel_c(q_width, da_h, db_h, wg_h, wu_h, n_h, u_h, ux_h, e_h, ex_h, n2_h, eq_h, wq_h, h_h, dres_h, g_h, dga_h, tabh, swaph, g2, d0, dc,
@@ -1125,6 +1131,43 @@
     )(*args)
 
 
+def kernel_out(pieces, n, *refs):
+    ins, outs, bufs = refs[:n], refs[n + 1:2 * n + 1], refs[2 * n + 3:3 * n + 3]
+    gains, gain_a, gain_b = refs[n], refs[2 * n + 1], refs[2 * n + 2]
+    read, write = refs[3 * n + 3:]
+
+    def part(ref, i, c):
+        rows = ref.shape[0] // pieces[i]
+        return ref.at[pl.ds(c * rows, rows), :]
+
+    jobs = [(i, c) for i in range(n) for c in range(pieces[i])]
+    get = [pltpu.make_async_copy(part(ins[i], i, c), part(bufs[i], i, c), read.at[m]) for m, (i, c) in enumerate(jobs)]
+    put = [pltpu.make_async_copy(part(bufs[i], i, c), part(outs[i], i, c), write.at[m]) for m, (i, c) in enumerate(jobs)]
+    for g in get:
+        g.start()
+    gain_a[...] = jnp.sum(gains[pl.ds(0, 8), :], axis=0, keepdims=True)
+    gain_b[...] = jnp.sum(gains[pl.ds(8, 8), :], axis=0, keepdims=True)
+    for g, p in zip(get, put):
+        g.wait()
+        p.start()
+    for p in put:
+        p.wait()
+
+
+def call_out(results, gains):
+    n = len(results)
+    pieces = tuple(max(1, x.size * x.dtype.itemsize // 2**20) for x in results)
+    row = jax.ShapeDtypeStruct((1, gains.shape[1]), F32)
+    whole = pl.BlockSpec(memory_space=pltpu.VMEM)
+    return pl.pallas_call(
+        functools.partial(kernel_out, pieces, n), out_shape=tuple(jax.ShapeDtypeStruct(x.shape, x.dtype) for x in results) + (row, row),
+        in_specs=[ANY] * n + [whole], out_specs=[ANY] * n + [whole, whole],
+        scratch_shapes=[VMEM(x.shape, x.dtype) for x in results] + [pltpu.SemaphoreType.DMA((sum(pieces),))] * 2,
+        compiler_params=pltpu.CompilerParams(vmem_limit_bytes=VMEM_LIMIT),
+        cost_estimate=pl.CostEstimate(flops=1000000, bytes_accessed=35000000, transcendentals=0), name="results",
+    )(*results, gains)
+
+
 def solution(mesh):
     def local_step(hidden, positions, g_ffn, w_gate, w_up, w_down, g_attn, w_q, w_kv, grad_h2, grad_q, grad_kv):
         tokens, dt = hidden.shape
@@ -1133,7 +1176,7 @@
 
         lane = np.arange(128)
         inv_freq = ROPE_BASE ** (-(lane % head_dim // 2 * 2).astype(np.float32) / head_dim)
-        angles = jnp.asarray(inv_freq, F32)[:, None] * positions.astype(F32)[None, :]
+        inv_freq = jnp.asarray(np.tile(inv_freq.astype(np.float32)[:, None], (1, 128)))
         swap = np.zeros((128, 128), np.float32)
         swap[lane, lane ^ 1] = np.where(lane % 2 == 0, -1.0, 1.0)
         swap = jnp.asarray(swap, BF16)
@@ -1144,17 +1187,17 @@
         def heads_last(x):
             return x.reshape(-1, head_dim, x.shape[1]).transpose(2, 0, 1)
 
-        gin = jnp.where(jnp.arange(8)[:, None] == 0, g_ffn[None, :], g_attn[None, :]).astype(F32)
-
         (normed_all, grad_gate, grad_up, u_all, gate_w, up_w, w_qkv, back_all, h_rows, gains, res_all, normed2, grad_res, resid_out, gattn8,
          u_other, e_other, table, wg_two, _, wd_zero, wd_cross) = call_ab(
-             hidden, heads_first(grad_q), heads_first(grad_kv), angles, swap, grad_h2, w_gate, w_up, w_down, heads_first(w_q), heads_first(w_kv), gin)
+             hidden, heads_first(grad_q), heads_first(grad_kv), positions.reshape(1, tokens), inv_freq, swap, grad_h2,
+             w_gate, w_up, w_down, heads_first(w_q), heads_first(w_kv), g_ffn.reshape(1, dt), g_attn.reshape(1, dt))
         (grad_wgate, _, grad_wup, _, grad_wdown, grad_wq, _, grad_wkv, _, q_out, kv_out, grad_hidden, gain_grads, *_) = call_c(
             q_width, grad_gate, grad_up, gate_w, up_w, normed_all, u_all, u_other, res_all, e_other, normed2, back_all, w_qkv,
             h_rows, grad_res, gains, gattn8, table, swap, wg_two, wd_zero, wd_cross)
+        (resid_out, grad_wgate, grad_wup, grad_wdown, grad_wq, grad_wkv, q_out, kv_out, grad_hidden, grad_gffn, grad_gattn) = call_out(
+            (resid_out, grad_wgate, grad_wup, grad_wdown, grad_wq, grad_wkv, q_out, kv_out, grad_hidden), gain_grads)
         q_out, kv_out, grad_wq, grad_wkv = (heads_last(x) for x in (q_out, kv_out, grad_wq, grad_wkv))
-        grad_gffn = jnp.sum(gain_grads[:8], axis=0)
-        grad_gattn = jnp.sum(gain_grads[8:], axis=0)
+        grad_gffn, grad_gattn = grad_gffn[0], grad_gattn[0]
         return (resid_out, q_out, kv_out, grad_hidden, grad_gffn, grad_gattn, grad_wgate, grad_wup, grad_wdown, grad_wq, grad_wkv)
 
     row_spec = P(("dp", "ty"), "tx")

time: 435 us -> 428 us (0.984)
  local copies, waits for them, and re-layouts: 17.6 us -> 2.52 us
  Pallas kernels: 411 us -> 425 us
  other arithmetic: 5.07 us -> 0 us
    unnamed x23 -> x0, local copies, waits for them, and re-layouts: 17.6 us -> none
    pallas_call x0 -> x1, Pallas kernels: none -> 14.3 us  [call_out(): pl.pallas_call(functools.partial(kernel_out, pieces, n), out_shape=tuple(...]
where the time goes in v8:
time: 428 us
  Pallas kernels  425 us (99%)
    pallas_call x1, Pallas kernels, call_ab(): pl.pallas_call(functools.partial(kernel_ab, q_width), out_shape=shapes, i...  255 us
    pallas_call x1, Pallas kernels, call_c(): pl.pallas_call(functools.partial(kernel_c, q_width), out_shape=shapes, in...  155 us
    pallas_call x1, Pallas kernels, call_out(): pl.pallas_call(functools.partial(kernel_out, pieces, n), out_shape=tuple(...  14.3 us

profile of v8, /device:TPU:0, one launch (start us, length us, event | category | flops | bytes accessed | tf_op | source)
XLA Modules:
  0.0 427.9 jit_solution(16538370999528335968)
XLA Ops:
  0.6 1.3 reshape.60.gfh
  1.9 1.3 reshape.61.gah
  3.2 255.0 %phase_ab.1 = (bf16[1024,2048]{1,0:T(8,128)(2,1)}, bf16[1024,2048]{1,0:T(8,128)(2,1)}, bf16[1024,2048]{1,0:T(8,128)(2,1)}, bf16[1024,2048]{1,0:T(8,128)(2,1)}, b...) custom-call(bf16[1024,512]{1,0:T(8,128)(2,1)} %hid.1, ...), custom_call_target="tpu_custom_call" | custom-call | flops 85899345920 | bytes 100000000 | tf_op jit(solution)/shard_map/phase_ab/pallas_call | solution.py:869
  258.2 155.2 %phase_c.1 = (f32[512,2048]{1,0:T(8,128)}, bf16[512,2048]{1,0:T(8,128)(2,1)}, f32[512,2048]{1,0:T(8,128)}, bf16[512,2048]{1,0:T(8,128)(2,1)}, f32[2048,512]{1,0:...) custom-call(bf16[1024,2048]{1,0:T(8,128)(2,1)} %get-tuple-element.53, ...), custom_call_target="tpu_custom_call" | custom-call | flops 85899345920 | bytes 100000000 | tf_op jit(solution)/shard_map/phase_c/pallas_call | solution.py:1120
  413.4 14.3 %results.1 = (bf16[1024,512]{1,0:T(8,128)(2,1)}, f32[512,2048]{1,0:T(8,128)}, f32[512,2048]{1,0:T(8,128)}, f32[2048,512]{1,0:T(8,128)}, f32[512,512]{1,0:T(8,128...) custom-call(bf16[1024,512]{1,0:T(8,128)(2,1)} %get-tuple-element.52., ...), custom_call_target="tpu_custom_call" | custom-call | flops 1000000 | bytes 35000000 | tf_op jit(solution)/shard_map/results/pallas_call | solution.py:1162

commit v9 on v8

--- a/solution.py
+++ b/solution.py
@@ -354,6 +354,10 @@
             self.diag(ch, 1, 1 - self.dp).wait_send()
 
 
+def down_split(ff):
+    return ff * 5 // 8
+
+
 def places():
     dp, z, tx = lax.axis_index("dp"), lax.axis_index("ty"), lax.axis_index("tx")
     return dp, z, tx, (tx, tx + 1 - 2 * (tx % 2), (tx + 2) % 4, 3 - tx)
@@ -438,9 +442,9 @@
         self.cp(2).wait_send()
 
 
-def kernel_ab(q_width, hid, eqh, ekvh, posh, invh, swaph, dh2h, wg, wu, wd, wq, wkv, gfh, gah,
-              n_o, da_o, db_o, u_o, wg_o, wu_o, wq_o, eq_o, h_o, g_o, e_o, n2_o, dres_o, home_o, dg_o, ux_o, ex_o, tab_o, g2_o, d2_o, d0_o, dc_o,
-              rows, dh2_v, n2_v, res_v, dres_v, n_v, a_v, b_v, wg_v, wu_v, wd_v, wq_v, eq_v, p_v, rbuf, rbuf2, gains, dg_v, swap_v, pos_v, inv_v, gf_v, ga_v, gin, send, recv, local):
+def kernel_ab(q_width, hid, eqh, ekvh, posh, invh, swaph, dh2h, wg, wu, wd, wq, wkv, gh,
+              n_o, da_o, db_o, u_o, wg_o, wu_o, wq_o, eq_o, h_o, g_o, e_o, n2_o, dres_o, home_o, dg_o, ux_o, ex_o, tab_o, d2_o, d0_o, dc_o,
+              rows, dh2_v, n2_v, res_v, dres_v, n_v, a_v, b_v, wg_v, wu_v, wd_v, wq_v, eq_v, p_v, rbuf, rbuf2, gains, dg_v, swap_v, pos_v, inv_v, g_v, gin, send, recv, local):
     dp, z, tx, peer = places()
     sub, dim = rows.shape
     tokens = 4 * sub
@@ -451,9 +455,10 @@
     tile = min(512, ff)
     dwide = min(1024, dim)
     dtile = min(512, dim)
-    hs, cs = sub // 2, sub // 4
+    hs, cs = sub // 2, sub // 8
+    split = down_split(ff)
     net = Wires(send, recv, local)
-    gain_in = [net.here(gfh, gf_v), net.here(gah, ga_v)]
+    gain_in = net.here(gh, g_v)
     turn_in = [net.here(eqh, p_v.at[pl.ds(0, q_width), pl.ds(0, tokens)]), net.here(ekvh, p_v.at[pl.ds(q_width, width - q_width), pl.ds(0, tokens)]),
                net.here(swaph, swap_v), net.here(posh, pos_v), net.here(invh, inv_v)]
     entry_barrier([{"tx": peer[1]}, {"tx": peer[2]}, {"tx": peer[3]}, {"dp": 1 - dp}], z)
@@ -481,7 +486,7 @@
 
     def ux_cp(k, b):
         view = ds(b * sub, sub)
-        cols = pl.ds(0, ff - ff // 4)
+        cols = pl.ds(0, split)
         src = ux_o.at[1, view, :] if k == 3 else wg_v.at[view, cols]
         i = u_id + (k - 1) * 4 + b
         return net.copy(src, ux_o.at[k - 1, view, :], i, i, tx=peer[1] if k == 3 else peer[k])
@@ -498,15 +503,15 @@
     kv_w = WeightGather(net, wkv, wq_v.at[pl.ds(q_width, width - q_width), :], pos, False, 1)
     ag = LineGather(net, n_v, sub, z)
     rsc = LineScatter(net, p_v, rbuf, sub, z)
-    rs2 = [LineScatter(net, n_v, rbuf2, sub, z, c * cs, cs) for c in range(4)]
-    ag2 = [LineGather(net, e_v, sub, z, c * cs, cs) for c in range(4)]
+    rs2 = [LineScatter(net, n_v, rbuf2, sub, z, c * cs, cs) for c in range(8)]
+    ag2 = [LineGather(net, e_v, sub, z, c * cs, cs) for c in range(8)]
 
     for k in far_first:
         h_cp(k).start()
-    for c in gain_in:
-        c.wait()
-    gin[...] = jnp.broadcast_to(gf_v[...].astype(F32), gin.shape)
-    gin[1:2, :] = ga_v[...].astype(F32)
+    gain_in.wait()
+    both = g_v[...].astype(F32)
+    gin[...] = jnp.broadcast_to(both[0:1, :], gin.shape)
+    gin[1:2, :] = both[1:2, :]
     g_own = net.here(gin, gains.at[:, pl.ds(0, dt)])
     h_own = net.here(hid.at[ds(tx * sub, sub), :], rows.at[:, pl.ds(0, dt)])
     for w in (q_w, kv_w, gate, up, down):
@@ -694,7 +699,7 @@
         for step in range(3):
             pl.when(i == step)(lambda step=step: rs2[0].send_end(2 - step))
 
-    for c in (1, 2, 3):
+    for c in range(1, 8):
         for i in (2, 1, 0):
             rs2[c].send_end(i)
     dg_v[...] = jnp.zeros_like(dg_v)
@@ -746,8 +751,8 @@
         def go():
             ag2[c].take(i)
             pl.when(mid(z))(lambda: ag2[c].forward(i))
-            if c % 2 == 1:
-                spread(ag.slots[i], c // 2)
+            if c % 4 == 3:
+                spread(ag.slots[i], c // 4)
         return go
 
     def run(ops):
@@ -758,16 +763,40 @@
 
     before_mid = (
         (scatter(2, 0), scatter(1, 0), scatter(0, 0)),
-        (scatter(2, 1), gathered(1, 0), scatter(1, 1), scatter(0, 1)),
-        (scatter(2, 2), scatter(1, 2), gathered(1, 1), scatter(0, 2), scatter(2, 3)),
-        (scatter(1, 3), scatter(0, 3), gathered(1, 2), gathered(0, 0)))
-    before_end = ((), (gathered(0, 0), gathered(1, 0)), (gathered(0, 1), gathered(1, 1)), (gathered(0, 2),))
-    after_mid = {0: (gathered(0, 1),), 1: (gathered(2, 0),), 2: (gathered(0, 2),), 3: (gathered(1, 3),), 5: (gathered(0, 3),), 7: (gathered(2, 1),),
-                 10: (gathered(2, 2),), 12: (gathered(2, 3),)}
-    after_end = {3: (gathered(1, 2),), 4: (gathered(0, 3),), 7: (gathered(2, 0),), 8: (gathered(1, 3),),
-                 12: (gathered(2, 1), gathered(2, 2), gathered(2, 3))}
-
-    for c in range(4):
+        (scatter(2, 1), scatter(1, 1), gathered(1, 0), scatter(0, 1), scatter(2, 2)),
+        (scatter(1, 2), scatter(0, 2), gathered(1, 1), scatter(2, 3)),
+        (scatter(1, 3), scatter(0, 3), gathered(1, 2), scatter(2, 4)),
+        (scatter(1, 4), scatter(0, 4), gathered(1, 3), scatter(2, 5)),
+        (scatter(1, 5), scatter(0, 5), gathered(1, 4), scatter(2, 6)),
+        (scatter(1, 6), scatter(0, 6), gathered(1, 5), scatter(2, 7)),
+        (scatter(1, 7), scatter(0, 7), gathered(1, 6), gathered(0, 0)))
+    before_end = (
+        (),
+        (gathered(0, 0), gathered(1, 0)),
+        (gathered(0, 1),),
+        (gathered(1, 1), gathered(0, 2)),
+        (gathered(1, 2), gathered(0, 3)),
+        (gathered(1, 3), gathered(0, 4)),
+        (gathered(1, 4), gathered(0, 5)),
+        (gathered(1, 5), gathered(0, 6)))
+    after_mid = {1: (gathered(0, 1),),
+                 2: (gathered(2, 0),),
+                 3: (gathered(0, 2),),
+                 4: (gathered(1, 7),),
+                 5: (gathered(0, 3),),
+                 6: (gathered(2, 1),),
+                 7: (gathered(0, 4),),
+                 8: (gathered(2, 2), gathered(0, 5), gathered(2, 3), gathered(0, 6), gathered(2, 4), gathered(0, 7)),
+                 10: (gathered(2, 5),),
+                 12: (gathered(2, 6), gathered(2, 7))}
+    after_end = {2: (gathered(1, 6),),
+                 4: (gathered(0, 7),),
+                 7: (gathered(2, 0),),
+                 8: (gathered(1, 7),),
+                 11: (gathered(2, 1),),
+                 12: (gathered(2, 2), gathered(2, 3), gathered(2, 4), gathered(2, 5), gathered(2, 6), gathered(2, 7))}
+
+    for c in range(8):
         pl.when(mid(z))(run(before_mid[c]))
         pl.when(end(z))(run(before_end[c]))
         if c == 0:
@@ -779,16 +808,15 @@
         rs2[c].finish()
         norm_chunk(c)
         ag2[c].start()
-        if c % 2 == 1:
-            spread(z, c // 2)
+        if c % 4 == 3:
+            spread(z, c // 4)
 
     for k in far_first:
         o_cp(k, tx).start()
     outs += [net.here(res_v.at[:, pl.ds(0, dt)], home_o.at[ds(tx * sub, sub), :]), net.here(n2_v, n2_o), net.here(dres_v.at[pl.ds(0, sub), pl.ds(0, dim)], dres_o), net.here(dg_v, dg_o)]
     rsc.drain()
-    for c in range(4):
+    for c in range(8):
         rs2[c].drain()
-    n_in = net.here(n_o, p_v)
     middle = (z + 1) // 2 % 2
 
     def u_forward():
@@ -810,21 +838,13 @@
     outs.append(net.here(e_v, e_o))
     outs += [net.here(a_v, da_o), net.here(b_v, db_o)]
 
-    last = pl.ds(ff - ff // 4, ff // 4)
-
     def down_tile(k, j):
-        return dot(wg_v[pl.ds(0, tokens), last], wg_v[pl.ds(tokens, tokens), pl.ds(k * dt, dt)], ROWS_ROWS)
-
-    def gate_tile(k, j):
-        return dot(p_v[:, pl.ds(k * dt, dt)], a_v[:, ds(j * (ff // 4), ff // 4)], ROWS_ROWS)
-
-    quarter = [rbuf.at[pl.ds(0, ff // 4), pl.ds(i * dt, dt)] for i in range(4)]
-    part_d = GradReduce(net, peer, down_tile, 1, quarter[0], quarter[1], quarter[2], quarter[3], d2_o, d0_o, None, dc_o, None)
-    part_g = GradReduce(net, peer, gate_tile, 4, n_v.at[pl.ds(0, dt), :], None, None, None, g2_o, None, None, wg_o, None)
-    n_in.wait()
+        return dot(wg_v[pl.ds(0, tokens), pl.ds(split, ff - split)], wg_v[pl.ds(tokens, tokens), ds(k * dt + j * (dt // 2), dt // 2)], ROWS_ROWS)
+
+    quarter = [rbuf.at[pl.ds(0, ff - split), pl.ds(i * dt, dt)] for i in range(4)]
+    part_d = GradReduce(net, peer, down_tile, 2, quarter[0], quarter[1], quarter[2], quarter[3], d2_o, d0_o, None, dc_o, None)
     part_d.step3()
     part_d.step1()
-    part_g.step3()
     part_d.step2()
     outs.append(net.here(quarter[2], dc_o))
     for k in far_first:
@@ -848,15 +868,13 @@
             ex_cp(k, b, 1).wait_send()
     for w in (q_w, kv_w, up, down):
         w.drain()
-    for c in range(4):
+    for c in range(8):
         ag2[c].drain()
     part_d.cp(1).wait_recv()
     part_d.sent_locally()
-    part_g.cp(0).wait_recv()
-    part_g.cp(0).wait_send()
-
-
-def call_ab(hid, eqh, ekvh, pos, inv, swap, dh2h, wg, wu, wd, wq, wkv, gf, ga):
+
+
+def call_ab(hid, eqh, ekvh, pos, inv, swap, dh2h, wg, wu, wd, wq, wkv, g):
     tokens, dt = hid.shape
     sub, dim, ff, q_width = tokens // 4, dt * 4, wg.shape[1], wq.shape[0]
     width = q_width + wkv.shape[0]
@@ -864,23 +882,23 @@
     tok_ff, tok_d, row = s((tokens, ff), BF16), s((tokens, dim), BF16), s((sub, dim), BF16)
     shapes = (tok_d, tok_ff, tok_ff, tok_ff, s((dim, ff), BF16), s((dim, ff), BF16), s((width, dim), BF16), s((width, tokens), BF16),
               row, s((8, dim), F32), tok_d, row, s((sub, dim), F32), s((tokens, dt), BF16), s((8, dim), F32),
-              s((3, tokens, ff - ff // 4), BF16), s((3, tokens, dt), BF16), s((256, 2 * tokens), F32), s((dt, ff), BF16)) + (s((ff // 4, dt), BF16),) * 3
+              s((3, tokens, down_split(ff)), BF16), s((3, tokens, dt), BF16), s((256, 2 * tokens), F32)) + (s((ff - down_split(ff), dt), BF16),) * 3
     vrow, vtok, vff = VMEM((sub, dim), BF16), VMEM((tokens, dim), BF16), VMEM((tokens, ff), BF16)
     return pl.pallas_call(
-        functools.partial(kernel_ab, q_width), out_shape=shapes, in_specs=[ANY] * 14, out_specs=[ANY] * len(shapes),
+        functools.partial(kernel_ab, q_width), out_shape=shapes, in_specs=[ANY] * 13, out_specs=[ANY] * len(shapes),
         scratch_shapes=[
             vrow, vrow, vrow, vrow, VMEM((max(sub, 256), max(dim, 2 * tokens)), F32), vtok, vff, vff, VMEM((dim, ff), BF16), VMEM((dim, ff), BF16), VMEM((ff, dim), BF16),
             VMEM((width, dim), BF16), VMEM((width, tokens), BF16), vtok, VMEM((5 * sub, dim), BF16), VMEM((5 * sub, dim), BF16),
             VMEM((8, dim), F32), VMEM((8, dim), F32), VMEM((128, 128), BF16), VMEM((1, tokens), jnp.int32), VMEM((128, 128), F32),
-            VMEM((1, dt), BF16), VMEM((1, dt), BF16), VMEM((8, dt), F32),
-            pltpu.SemaphoreType.DMA((180,)), pltpu.SemaphoreType.DMA((180,)), pltpu.SemaphoreType.DMA((48,))],
+            VMEM((2, dt), BF16), VMEM((8, dt), F32),
+            pltpu.SemaphoreType.DMA((232,)), pltpu.SemaphoreType.DMA((232,)), pltpu.SemaphoreType.DMA((48,))],
         compiler_params=pltpu.CompilerParams(collective_id=0, has_side_effects=True, vmem_limit_bytes=VMEM_LIMIT),
         cost_estimate=pl.CostEstimate(flops=20 * tokens * dim * ff, bytes_accessed=100000000, transcendentals=0), name="phase_ab",
-    )(hid, eqh, ekvh, pos, inv, swap, dh2h, wg, wu, wd, wq, wkv, gf, ga)
-
-
-def kernel_c(q_width, da_h, db_h, wg_h, wu_h, n_h, u_h, ux_h, e_h, ex_h, n2_h, eq_h, wq_h, h_h, dres_h, g_h, dga_h, tabh, swaph, g2, d0, dc,
-             wgo, wgy, wuo, wuy, wdo, wqo, wqy, wvo, wvy, q_o, kv_o, dh_o, dg_o, g0, u2, u0, q2, q0, v2, v0, qx, dy,
+    )(hid, eqh, ekvh, pos, inv, swap, dh2h, wg, wu, wd, wq, wkv, g)
+
+
+def kernel_c(q_width, da_h, db_h, wg_h, wu_h, n_h, u_h, ux_h, e_h, ex_h, n2_h, eq_h, wq_h, h_h, dres_h, g_h, dga_h, tabh, swaph, d0, dc,
+             wgo, wgy, wuo, wuy, wdo, wqo, wqy, wvo, wvy, q_o, kv_o, dh_o, dg_o, g2, g0, u2, u0, q2, q0, v2, v0, qx, dy,
              wg_v, wu_v, da_v, db_v, n_v, p_v, rbuf, n2_v, st3, st1, cross_g, cross_u, stage, tiles_v, dres_v, wq_v, eq_v,
              gains, dg_v, dgr, dgz, tab_v, swap_v, send, recv, local):
     dp, z, tx, peer = places()
@@ -945,9 +963,10 @@
     ag.start()
     for c in first:
         c.wait()
-    gate.step2(True)
+    gate.step3()
+    gate.step1()
+    gate.step2()
     gate.send()
-    gate.step1()
     for c in second:
         c.wait()
 
@@ -955,8 +974,8 @@
     def _(i):
         @pl.when(i == 1)
         def _():
+            gate.sent_locally()
             up.step3()
-            gate.cp(1).wait_send()
             up.step1()
             ag.step1()
 
@@ -974,39 +993,50 @@
     gate.step0(st1)
     gate.sent()
 
-    n_tiles = ff // tile
     e_in = [net.here(e_h.at[:, pl.ds(0, dt)], wu_v.at[pl.ds(0, tokens), pl.ds(0, dt)])]
     for k in (1, 2, 3):
         e_in.append(net.here(ex_h.at[k - 1], wu_v.at[pl.ds(0, tokens), pl.ds(k * dt, dt)]))
 
+    piece = ff // 8
+    exchanged, n_pieces = down_split(ff) // piece, 8
+
     def u_place(j, k):
-        return wg_v.at[pl.ds((j % 2) * tokens, tokens), pl.ds(k * tile, tile)]
+        return wg_v.at[pl.ds((j % 2) * tokens, tokens), pl.ds(k * piece, piece)]
+
+    def sums(j, n):
+        return stage.at[pl.ds((j % 2) * piece, piece), pl.ds(n * dt, dt)]
 
     def u_load(j):
-        cols = pl.ds(j * tile, tile)
-        if j == n_tiles - 1:
-            return [net.here(u_h.at[:, cols], u_place(j, 0)), net.here(d0, stage.at[pl.ds(0, tile), pl.ds(0, dt)]), net.here(dy, stage.at[pl.ds(0, tile), pl.ds(dt, dt)])]
-        return [net.here(u_h.at[:, cols] if k == 0 else ux_h.at[k - 1, :, cols], u_place(j, k)) for k in range(4)]
-
-    def down_tile(j, slot, loads):
-        for c in loads:
-            c.wait()
-        acc = None
-        if j == n_tiles - 1:
-            acc = stage[pl.ds(0, tile), pl.ds(0, dt)].astype(F32) + stage[pl.ds(0, tile), pl.ds(dt, dt)].astype(F32)
-        for k in range(1 if j == n_tiles - 1 else 4):
-            part = dot(u_place(j, k)[...], wu_v[pl.ds(0, tokens), pl.ds(k * dt, dt)], ROWS_ROWS)
-            acc = part if acc is None else acc + part
-        tiles_v[slot, pl.ds(0, tile), pl.ds(0, dt)] = acc
-        return net.here(tiles_v.at[slot, pl.ds(0, tile), pl.ds(0, dt)], wdo.at[pl.ds(j * tile, tile), :])
-
-    loads = {0: u_load(0), 1: u_load(1)}
+        cols = pl.ds(j * piece, piece)
+        if j < exchanged:
+            return [net.here(u_h.at[:, cols] if k == 0 else ux_h.at[k - 1, :, cols], u_place(j, k)) for k in range(4)]
+        rows = pl.ds((j - exchanged) * piece, piece)
+        return [net.here(u_h.at[:, cols], u_place(j, 0)), net.here(d0.at[rows, :], sums(j, 0)), net.here(dy.at[rows, :], sums(j, 1))]
+
+    loads, stores = {}, {}
+
+    def down_run(js):
+        for j in js:
+            for c in loads.pop(j):
+                c.wait()
+            if j >= 2:
+                stores.pop(j - 2).wait()
+            acc = None if j < exchanged else sums(j, 0)[...].astype(F32) + sums(j, 1)[...].astype(F32)
+            for k in range(4 if j < exchanged else 1):
+                part = dot(u_place(j, k)[...], wu_v[pl.ds(0, tokens), pl.ds(k * dt, dt)], ROWS_ROWS)
+                acc = part if acc is None else acc + part
+            place = tiles_v.at[j % 2, pl.ds(0, piece), pl.ds(0, dt)]
+            tiles_v[j % 2, pl.ds(0, piece), pl.ds(0, dt)] = acc
+            stores[j] = net.here(place, wdo.at[pl.ds(j * piece, piece), :])
+            if j + 2 < n_pieces:
+                loads[j + 2] = u_load(j + 2)
+
+    loads[0], loads[1] = u_load(0), u_load(1)
     rsc.send_mid(1)
     rsc.send_mid(0)
     for c in e_in:
         c.wait()
-    done = [down_tile(0, 0, loads[0]), down_tile(1, 1, loads[1])]
-    loads = {2: u_load(2)}
+    down_run((0, 1))
     for c in third:
         c.wait()
     ag.step3_end()
@@ -1021,17 +1051,14 @@
     for k in far_first:
         q_cp(k, tx).start()
     q_own = net.here(wu_v.at[pl.ds(tokens, width), ds(tx * sub, sub)], qx.at[:, ds(tx * sub, sub)])
-    for c in done:
-        c.wait()
     for part in heads:
         part.step3()
         part.step1()
     dy_cp().wait_recv()
-    loads[3] = u_load(3)
     for part in heads:
         part.step2()
         part.send()
-    done = [down_tile(2, 0, loads[2]), down_tile(3, 1, loads[3])]
+    down_run(range(2, n_pieces))
     h_in.wait()
     rsc.finish()
     dg_v[pl.ds(0, 8), :] = jnp.zeros((8, dim), F32)
@@ -1067,7 +1094,7 @@
         h_cp(k, tx).start()
     h_own = net.here(st1.at[pl.ds(0, sub), pl.ds(0, dt)], dh_o.at[ds(tx * sub, sub), :])
     up.sent()
-    for c in done:
+    for c in stores.values():
         c.wait()
     up.step0(cross_g)
     for k in far_first:
@@ -1116,7 +1143,7 @@
     wf, wb = s((dt, ff), F32), s((dt, ff), BF16)
     qf, qb, vf, vb = s((q_width, dt), F32), s((q_width, dt), BF16), s((rest, dt), F32), s((rest, dt), BF16)
     shapes = (wf, wb, wf, wb, s((ff, dt), F32), qf, qb, vf, vb, s((q_width, tokens), BF16), s((rest, tokens), BF16), s((tokens, dt), BF16), s((16, dt), F32),
-              wb, wb, wb, qb, qb, vb, vb, s((width, tokens), BF16), s((tile, dt), BF16))
+              wb, wb, wb, wb, qb, qb, vb, vb, s((width, tokens), BF16), s((ff - down_split(ff), dt), BF16))
     return pl.pallas_call(
         functools.partial(kernel_c, q_width), out_shape=shapes, in_specs=[ANY] * len(args), out_specs=[ANY] * len(shapes),
         scratch_shapes=[
@@ -1125,7 +1152,7 @@
             VMEM((dt, ff), BF16), VMEM((dt, ff), BF16), VMEM((dt, ff), BF16), VMEM((dt, ff), BF16), VMEM((dt, ff), BF16),
             VMEM((2, max(dt, tile), max(dt, tile)), F32), VMEM((sub, dim), F32), VMEM((width, dim), BF16), VMEM((width, tokens), BF16),
             VMEM((8, dim), F32), VMEM((16, dim), F32), VMEM((4, 16, dt), F32), VMEM((4, 16, dt), F32), VMEM((256, 2 * tokens), F32), VMEM((128, 128), BF16),
-            pltpu.SemaphoreType.DMA((48,)), pltpu.SemaphoreType.DMA((48,)), pltpu.SemaphoreType.DMA((72,))],
+            pltpu.SemaphoreType.DMA((48,)), pltpu.SemaphoreType.DMA((48,)), pltpu.SemaphoreType.DMA((96,))],
         compiler_params=pltpu.CompilerParams(collective_id=2, has_side_effects=True, vmem_limit_bytes=VMEM_LIMIT),
         cost_estimate=pl.CostEstimate(flops=20 * tokens * dim * ff, bytes_accessed=100000000, transcendentals=0), name="phase_c",
     )(*args)
@@ -1188,12 +1215,12 @@
             return x.reshape(-1, head_dim, x.shape[1]).transpose(2, 0, 1)
 
         (normed_all, grad_gate, grad_up, u_all, gate_w, up_w, w_qkv, back_all, h_rows, gains, res_all, normed2, grad_res, resid_out, gattn8,
-         u_other, e_other, table, wg_two, _, wd_zero, wd_cross) = call_ab(
+         u_other, e_other, table, _, wd_zero, wd_cross) = call_ab(
              hidden, heads_first(grad_q), heads_first(grad_kv), positions.reshape(1, tokens), inv_freq, swap, grad_h2,
-             w_gate, w_up, w_down, heads_first(w_q), heads_first(w_kv), g_ffn.reshape(1, dt), g_attn.reshape(1, dt))
+             w_gate, w_up, w_down, heads_first(w_q), heads_first(w_kv), jnp.where(jnp.arange(2)[:, None] == 0, g_ffn[None, :], g_attn[None, :]))
         (grad_wgate, _, grad_wup, _, grad_wdown, grad_wq, _, grad_wkv, _, q_out, kv_out, grad_hidden, gain_grads, *_) = call_c(
             q_width, grad_gate, grad_up, gate_w, up_w, normed_all, u_all, u_other, res_all, e_other, normed2, back_all, w_qkv,
-            h_rows, grad_res, gains, gattn8, table, swap, wg_two, wd_zero, wd_cross)
+            h_rows, grad_res, gains, gattn8, table, swap, wd_zero, wd_cross)
         (resid_out, grad_wgate, grad_wup, grad_wdown, grad_wq, grad_wkv, q_out, kv_out, grad_hidden, grad_gffn, grad_gattn) = call_out(
             (resid_out, grad_wgate, grad_wup, grad_wdown, grad_wq, grad_wkv, q_out, kv_out, grad_hidden), gain_grads)
         q_out, kv_out, grad_wq, grad_wkv = (heads_last(x) for x in (q_out, kv_out, grad_wq, grad_wkv))

time: 428 us -> 426 us (level)
    pallas_call x1, Pallas kernels: 255 us -> 245 us  [call_ab(): pl.pallas_call(functools.partial(kernel_ab, q_width), out_shape=shapes, i...]
    pallas_call x1, Pallas kernels: 155 us -> 163 us  [call_c(): pl.pallas_call(functools.partial(kernel_c, q_width), out_shape=shapes, in...]
where the time goes in v9:
time: 426 us; the launch traced here: 425 us
  Pallas kernels  423 us (99%)
    pallas_call x1, Pallas kernels, call_ab(): pl.pallas_call(functools.partial(kernel_ab, q_width), out_shape=shapes, i...  245 us
    pallas_call x1, Pallas kernels, call_c(): pl.pallas_call(functools.partial(kernel_c, q_width), out_shape=shapes, in...  163 us
    pallas_call x1, Pallas kernels, call_out(): pl.pallas_call(functools.partial(kernel_out, pieces, n), out_shape=tuple(...  14.3 us

profile of v9, /device:TPU:0, one launch (start us, length us, event | category | flops | bytes accessed | tf_op | source)
XLA Modules:
  0.0 425.1 jit_solution(7472349797274966145)
XLA Ops:
  0.7 1.4 broadcast_select_fusion.gh
  2.0 245.3 %phase_ab.1 = (bf16[1024,2048]{1,0:T(8,128)(2,1)}, bf16[1024,2048]{1,0:T(8,128)(2,1)}, bf16[1024,2048]{1,0:T(8,128)(2,1)}, bf16[1024,2048]{1,0:T(8,128)(2,1)}, b...) custom-call(bf16[1024,512]{1,0:T(8,128)(2,1)} %hid.1, ...), custom_call_target="tpu_custom_call" | custom-call | flops 85899345920 | bytes 100000000 | tf_op jit(solution)/shard_map/phase_ab/pallas_call | solution.py:887
  247.3 163.3 %phase_c.1 = (f32[512,2048]{1,0:T(8,128)}, bf16[512,2048]{1,0:T(8,128)(2,1)}, f32[512,2048]{1,0:T(8,128)}, bf16[512,2048]{1,0:T(8,128)(2,1)}, f32[2048,512]{1,0:...) custom-call(bf16[1024,2048]{1,0:T(8,128)(2,1)} %get-tuple-element.52, ...), custom_call_target="tpu_custom_call" | custom-call | flops 85899345920 | bytes 100000000 | tf_op jit(solution)/shard_map/phase_c/pallas_call | solution.py:1147
  410.6 14.3 %results.1 = (bf16[1024,512]{1,0:T(8,128)(2,1)}, f32[512,2048]{1,0:T(8,128)}, f32[512,2048]{1,0:T(8,128)}, f32[2048,512]{1,0:T(8,128)}, f32[512,512]{1,0:T(8,128...) custom-call(bf16[1024,512]{1,0:T(8,128)(2,1)} %get-tuple-element.51., ...), custom_call_target="tpu_custom_call" | custom-call | flops 1000000 | bytes 35000000 | tf_op jit(solution)/shard_map/results/pallas_call | solution.py:1189
  (1 shorter events, 0.0 us)

commit v10 on v9

--- a/solution.py
+++ b/solution.py
@@ -465,7 +465,7 @@
 
     pos = (dp, peer[1], peer[2])
     far_first = (2, 3, 1)
-    g_id, h_id, e_id, d_id, o_id, u_id, x_id = (net.take(4), net.take(4), net.take(4), net.take(4), net.take(4), net.take(12), net.take(24))
+    g_id, h_id, e_id, d_id, o_id, u_id, x_id = (net.take(4), net.take(4), net.take(4), net.take(4), net.take(8), net.take(12), net.take(24))
     u_v = wg_v.at[pl.ds(0, tokens), :]
     e_v = wg_v.at[pl.ds(tokens, tokens), :]
 
@@ -481,8 +481,9 @@
     def d_cp(k):
         return net.copy(dh2h.at[ds(peer[k] * sub, sub), :], dh2_v.at[:, pl.ds(k * dt, dt)], d_id + k, d_id + k, tx=peer[k])
 
-    def o_cp(k, block):
-        return net.copy(res_v.at[:, pl.ds(k * dt, dt)], home_o.at[ds(block * sub, sub), :], o_id + k, o_id + k, tx=peer[k])
+    def o_cp(k, block, half):
+        i = o_id + half * 4 + k
+        return net.copy(res_v.at[pl.ds(half * hs, hs), pl.ds(k * dt, dt)], home_o.at[ds(block * sub + half * hs, hs), :], i, i, tx=peer[k])
 
     def ux_cp(k, b):
         view = ds(b * sub, sub)
@@ -810,9 +811,9 @@
         ag2[c].start()
         if c % 4 == 3:
             spread(z, c // 4)
-
-    for k in far_first:
-        o_cp(k, tx).start()
+            for k in far_first:
+                o_cp(k, tx, c // 4).start()
+
     outs += [net.here(res_v.at[:, pl.ds(0, dt)], home_o.at[ds(tx * sub, sub), :]), net.here(n2_v, n2_o), net.here(dres_v.at[pl.ds(0, sub), pl.ds(0, dim)], dres_o), net.here(dg_v, dg_o)]
     rsc.drain()
     for c in range(8):
@@ -848,7 +849,8 @@
     part_d.step2()
     outs.append(net.here(quarter[2], dc_o))
     for k in far_first:
-        o_cp(k, peer[k]).wait_recv()
+        o_cp(k, peer[k], 0).wait_recv()
+        o_cp(k, peer[k], 1).wait_recv()
         for b in range(4):
             ex_cp(k, b, 0).wait_recv()
             ex_cp(k, b, 1).wait_recv()
@@ -861,7 +863,8 @@
         g_cp(k).wait_send()
         h_cp(k).wait_send()
         d_cp(k).wait_send()
-        o_cp(k, tx).wait_send()
+        o_cp(k, tx, 0).wait_send()
+        o_cp(k, tx, 1).wait_send()
         for b in range(4):
             ux_cp(k, b).wait_send()
             ex_cp(k, b, 0).wait_send()
@@ -891,7 +894,7 @@
             VMEM((width, dim), BF16), VMEM((width, tokens), BF16), vtok, VMEM((5 * sub, dim), BF16), VMEM((5 * sub, dim), BF16),
             VMEM((8, dim), F32), VMEM((8, dim), F32), VMEM((128, 128), BF16), VMEM((1, tokens), jnp.int32), VMEM((128, 128), F32),
             VMEM((2, dt), BF16), VMEM((8, dt), F32),
-            pltpu.SemaphoreType.DMA((232,)), pltpu.SemaphoreType.DMA((232,)), pltpu.SemaphoreType.DMA((48,))],
+            pltpu.SemaphoreType.DMA((236,)), pltpu.SemaphoreType.DMA((236,)), pltpu.SemaphoreType.DMA((48,))],
         compiler_params=pltpu.CompilerParams(collective_id=0, has_side_effects=True, vmem_limit_bytes=VMEM_LIMIT),
         cost_estimate=pl.CostEstimate(flops=20 * tokens * dim * ff, bytes_accessed=100000000, transcendentals=0), name="phase_ab",
     )(hid, eqh, ekvh, pos, inv, swap, dh2h, wg, wu, wd, wq, wkv, g)

time: 426 us -> 420 us (0.986)
  Pallas kernels: 423 us -> 418 us
    pallas_call x1, Pallas kernels: 163 us -> 158 us  [call_c(): pl.pallas_call(functools.partial(kernel_c, q_width), out_shape=shapes, in...]
where the time goes in v10:
time: 420 us
  Pallas kernels  418 us (100%)
    pallas_call x1, Pallas kernels, call_ab(): pl.pallas_call(functools.partial(kernel_ab, q_width), out_shape=shapes, i...  245 us
    pallas_call x1, Pallas kernels, call_c(): pl.pallas_call(functools.partial(kernel_c, q_width), out_shape=shapes, in...  158 us
    pallas_call x1, Pallas kernels, call_out(): pl.pallas_call(functools.partial(kernel_out, pieces, n), out_shape=tuple(...  14.3 us

profile of v10, /device:TPU:0, one launch (start us, length us, event | category | flops | bytes accessed | tf_op | source)
XLA Modules:
  0.0 419.9 jit_solution(7403646427165555692)
XLA Ops:
  0.7 1.4 broadcast_select_fusion.gh
  2.0 245.3 %phase_ab.1 = (bf16[1024,2048]{1,0:T(8,128)(2,1)}, bf16[1024,2048]{1,0:T(8,128)(2,1)}, bf16[1024,2048]{1,0:T(8,128)(2,1)}, bf16[1024,2048]{1,0:T(8,128)(2,1)}, b...) custom-call(bf16[1024,512]{1,0:T(8,128)(2,1)} %hid.1, ...), custom_call_target="tpu_custom_call" | custom-call | flops 85899345920 | bytes 100000000 | tf_op jit(solution)/shard_map/phase_ab/pallas_call | solution.py:890
  247.3 158.0 %phase_c.1 = (f32[512,2048]{1,0:T(8,128)}, bf16[512,2048]{1,0:T(8,128)(2,1)}, f32[512,2048]{1,0:T(8,128)}, bf16[512,2048]{1,0:T(8,128)(2,1)}, f32[2048,512]{1,0:...) custom-call(bf16[1024,2048]{1,0:T(8,128)(2,1)} %get-tuple-element.52, ...), custom_call_target="tpu_custom_call" | custom-call | flops 85899345920 | bytes 100000000 | tf_op jit(solution)/shard_map/phase_c/pallas_call | solution.py:1150
  405.4 14.3 %results.1 = (bf16[1024,512]{1,0:T(8,128)(2,1)}, f32[512,2048]{1,0:T(8,128)}, f32[512,2048]{1,0:T(8,128)}, f32[2048,512]{1,0:T(8,128)}, f32[512,512]{1,0:T(8,128...) custom-call(bf16[1024,512]{1,0:T(8,128)(2,1)} %get-tuple-element.51., ...), custom_call_target="tpu_custom_call" | custom-call | flops 1000000 | bytes 35000000 | tf_op jit(solution)/shard_map/results/pallas_call | solution.py:1192
  (1 shorter events, 0.0 us)

commit v11 on v10

--- a/solution.py
+++ b/solution.py
@@ -442,9 +442,9 @@
         self.cp(2).wait_send()
 
 
-def kernel_ab(q_width, hid, eqh, ekvh, posh, invh, swaph, dh2h, wg, wu, wd, wq, wkv, gh,
+def kernel_ab(q_width, hid, eqh, ekvh, posh, invh, swaph, dh2h, wg, wu, wd, wq, wkv, gfh, gah,
               n_o, da_o, db_o, u_o, wg_o, wu_o, wq_o, eq_o, h_o, g_o, e_o, n2_o, dres_o, home_o, dg_o, ux_o, ex_o, tab_o, d2_o, d0_o, dc_o,
-              rows, dh2_v, n2_v, res_v, dres_v, n_v, a_v, b_v, wg_v, wu_v, wd_v, wq_v, eq_v, p_v, rbuf, rbuf2, gains, dg_v, swap_v, pos_v, inv_v, g_v, gin, send, recv, local):
+              rows, dh2_v, n2_v, res_v, dres_v, n_v, a_v, b_v, wg_v, wu_v, wd_v, wq_v, eq_v, p_v, rbuf, rbuf2, gains, dg_v, swap_v, pos_v, inv_v, gf_v, ga_v, gin, send, recv, local):
     dp, z, tx, peer = places()
     sub, dim = rows.shape
     tokens = 4 * sub
@@ -458,7 +458,7 @@
     hs, cs = sub // 2, sub // 8
     split = down_split(ff)
     net = Wires(send, recv, local)
-    gain_in = net.here(gh, g_v)
+    gain_in = [net.here(gfh, gf_v), net.here(gah, ga_v)]
     turn_in = [net.here(eqh, p_v.at[pl.ds(0, q_width), pl.ds(0, tokens)]), net.here(ekvh, p_v.at[pl.ds(q_width, width - q_width), pl.ds(0, tokens)]),
                net.here(swaph, swap_v), net.here(posh, pos_v), net.here(invh, inv_v)]
     entry_barrier([{"tx": peer[1]}, {"tx": peer[2]}, {"tx": peer[3]}, {"dp": 1 - dp}], z)
@@ -509,10 +509,10 @@
 
     for k in far_first:
         h_cp(k).start()
-    gain_in.wait()
-    both = g_v[...].astype(F32)
-    gin[...] = jnp.broadcast_to(both[0:1, :], gin.shape)
-    gin[1:2, :] = both[1:2, :]
+    for c in gain_in:
+        c.wait()
+    gin[...] = jnp.broadcast_to(gf_v[...].astype(F32)[None, :], gin.shape)
+    gin[1:2, :] = ga_v[...].astype(F32)[None, :]
     g_own = net.here(gin, gains.at[:, pl.ds(0, dt)])
     h_own = net.here(hid.at[ds(tx * sub, sub), :], rows.at[:, pl.ds(0, dt)])
     for w in (q_w, kv_w, gate, up, down):
@@ -877,7 +877,7 @@
     part_d.sent_locally()
 
 
-def call_ab(hid, eqh, ekvh, pos, inv, swap, dh2h, wg, wu, wd, wq, wkv, g):
+def call_ab(hid, eqh, ekvh, pos, inv, swap, dh2h, wg, wu, wd, wq, wkv, gf, ga):
     tokens, dt = hid.shape
     sub, dim, ff, q_width = tokens // 4, dt * 4, wg.shape[1], wq.shape[0]
     width = q_width + wkv.shape[0]
@@ -888,16 +888,16 @@
               s((3, tokens, down_split(ff)), BF16), s((3, tokens, dt), BF16), s((256, 2 * tokens), F32)) + (s((ff - down_split(ff), dt), BF16),) * 3
     vrow, vtok, vff = VMEM((sub, dim), BF16), VMEM((tokens, dim), BF16), VMEM((tokens, ff), BF16)
     return pl.pallas_call(
-        functools.partial(kernel_ab, q_width), out_shape=shapes, in_specs=[ANY] * 13, out_specs=[ANY] * len(shapes),
+        functools.partial(kernel_ab, q_width), out_shape=shapes, in_specs=[ANY] * 14, out_specs=[ANY] * len(shapes),
         scratch_shapes=[
             vrow, vrow, vrow, vrow, VMEM((max(sub, 256), max(dim, 2 * tokens)), F32), vtok, vff, vff, VMEM((dim, ff), BF16), VMEM((dim, ff), BF16), VMEM((ff, dim), BF16),
             VMEM((width, dim), BF16), VMEM((width, tokens), BF16), vtok, VMEM((5 * sub, dim), BF16), VMEM((5 * sub, dim), BF16),
             VMEM((8, dim), F32), VMEM((8, dim), F32), VMEM((128, 128), BF16), VMEM((1, tokens), jnp.int32), VMEM((128, 128), F32),
-            VMEM((2, dt), BF16), VMEM((8, dt), F32),
+            VMEM((dt,), BF16), VMEM((dt,), BF16), VMEM((8, dt), F32),
             pltpu.SemaphoreType.DMA((236,)), pltpu.SemaphoreType.DMA((236,)), pltpu.SemaphoreType.DMA((48,))],
         compiler_params=pltpu.CompilerParams(collective_id=0, has_side_effects=True, vmem_limit_bytes=VMEM_LIMIT),
         cost_estimate=pl.CostEstimate(flops=20 * tokens * dim * ff, bytes_accessed=100000000, transcendentals=0), name="phase_ab",
-    )(hid, eqh, ekvh, pos, inv, swap, dh2h, wg, wu, wd, wq, wkv, g)
+    )(hid, eqh, ekvh, pos, inv, swap, dh2h, wg, wu, wd, wq, wkv, gf, ga)
 
 
 def kernel_c(q_width, da_h, db_h, wg_h, wu_h, n_h, u_h, ux_h, e_h, ex_h, n2_h, eq_h, wq_h, h_h, dres_h, g_h, dga_h, tabh, swaph, d0, dc,
@@ -1220,7 +1220,7 @@
         (normed_all, grad_gate, grad_up, u_all, gate_w, up_w, w_qkv, back_all, h_rows, gains, res_all, normed2, grad_res, resid_out, gattn8,
          u_other, e_other, table, _, wd_zero, wd_cross) = call_ab(
              hidden, heads_first(grad_q), heads_first(grad_kv), positions.reshape(1, tokens), inv_freq, swap, grad_h2,
-             w_gate, w_up, w_down, heads_first(w_q), heads_first(w_kv), jnp.where(jnp.arange(2)[:, None] == 0, g_ffn[None, :], g_attn[None, :]))
+             w_gate, w_up, w_down, heads_first(w_q), heads_first(w_kv), g_ffn, g_attn)
         (grad_wgate, _, grad_wup, _, grad_wdown, grad_wq, _, grad_wkv, _, q_out, kv_out, grad_hidden, gain_grads, *_) = call_c(
             q_width, grad_gate, grad_up, gate_w, up_w, normed_all, u_all, u_other, res_all, e_other, normed2, back_all, w_qkv,
             h_rows, grad_res, gains, gattn8, table, swap, wd_zero, wd_cross)

time: 420 us -> 419 us (level)
  no operation moved by 1% of the time
where the time goes in v11:
time: 419 us
  Pallas kernels  418 us (100%)
    pallas_call x1, Pallas kernels, call_ab(): pl.pallas_call(functools.partial(kernel_ab, q_width), out_shape=shapes, i...  245 us
    pallas_call x1, Pallas kernels, call_c(): pl.pallas_call(functools.partial(kernel_c, q_width), out_shape=shapes, in...  158 us
    pallas_call x1, Pallas kernels, call_out(): pl.pallas_call(functools.partial(kernel_out, pieces, n), out_shape=tuple(...  14.3 us

profile of v11, /device:TPU:0, one launch (start us, length us, event | category | flops | bytes accessed | tf_op | source)
XLA Modules:
  0.0 418.6 jit_solution(10968067961007643273)
XLA Ops:
  0.6 245.4 %phase_ab.1 = (bf16[1024,2048]{1,0:T(8,128)(2,1)}, bf16[1024,2048]{1,0:T(8,128)(2,1)}, bf16[1024,2048]{1,0:T(8,128)(2,1)}, bf16[1024,2048]{1,0:T(8,128)(2,1)}, b...) custom-call(bf16[1024,512]{1,0:T(8,128)(2,1)} %hid.1, ...), custom_call_target="tpu_custom_call" | custom-call | flops 85899345920 | bytes 100000000 | tf_op jit(solution)/shard_map/phase_ab/pallas_call | solution.py:890
  246.1 158.0 %phase_c.1 = (f32[512,2048]{1,0:T(8,128)}, bf16[512,2048]{1,0:T(8,128)(2,1)}, f32[512,2048]{1,0:T(8,128)}, bf16[512,2048]{1,0:T(8,128)(2,1)}, f32[2048,512]{1,0:...) custom-call(bf16[1024,2048]{1,0:T(8,128)(2,1)} %get-tuple-element.52, ...), custom_call_target="tpu_custom_call" | custom-call | flops 85899345920 | bytes 100000000 | tf_op jit(solution)/shard_map/phase_c/pallas_call | solution.py:1150
  404.1 14.3 %results.1 = (bf16[1024,512]{1,0:T(8,128)(2,1)}, f32[512,2048]{1,0:T(8,128)}, f32[512,2048]{1,0:T(8,128)}, f32[2048,512]{1,0:T(8,128)}, f32[512,512]{1,0:T(8,128...) custom-call(bf16[1024,512]{1,0:T(8,128)(2,1)} %get-tuple-element.51., ...), custom_call_target="tpu_custom_call" | custom-call | flops 1000000 | bytes 35000000 | tf_op jit(solution)/shard_map/results/pallas_call | solution.py:1192

commit v12 on v11

--- a/solution.py
+++ b/solution.py
@@ -1173,13 +1173,16 @@
     jobs = [(i, c) for i in range(n) for c in range(pieces[i])]
     get = [pltpu.make_async_copy(part(ins[i], i, c), part(bufs[i], i, c), read.at[m]) for m, (i, c) in enumerate(jobs)]
     put = [pltpu.make_async_copy(part(bufs[i], i, c), part(outs[i], i, c), write.at[m]) for m, (i, c) in enumerate(jobs)]
-    for g in get:
+    ahead = min(8, len(get))
+    for g in get[:ahead]:
         g.start()
     gain_a[...] = jnp.sum(gains[pl.ds(0, 8), :], axis=0, keepdims=True)
     gain_b[...] = jnp.sum(gains[pl.ds(8, 8), :], axis=0, keepdims=True)
-    for g, p in zip(get, put):
+    for m, (g, p) in enumerate(zip(get, put)):
         g.wait()
         p.start()
+        if m + ahead < len(get):
+            get[m + ahead].start()
     for p in put:
         p.wait()
 

time: 419 us -> 419 us (level)
  no operation moved by 1% of the time
where the time goes in v12:
time: 419 us; the launch traced here: 418 us
  Pallas kernels  417 us (100%)
    pallas_call x1, Pallas kernels, call_ab(): pl.pallas_call(functools.partial(kernel_ab, q_width), out_shape=shapes, i...  245 us
    pallas_call x1, Pallas kernels, call_c(): pl.pallas_call(functools.partial(kernel_c, q_width), out_shape=shapes, in...  158 us
    pallas_call x1, Pallas kernels, call_out(): pl.pallas_call(functools.partial(kernel_out, pieces, n), out_shape=tuple(...  14 us

profile of v12, /device:TPU:0, one launch (start us, length us, event | category | flops | bytes accessed | tf_op | source)
XLA Modules:
  0.0 418.3 jit_solution(904906963610019665)
XLA Ops:
  0.6 245.4 %phase_ab.1 = (bf16[1024,2048]{1,0:T(8,128)(2,1)}, bf16[1024,2048]{1,0:T(8,128)(2,1)}, bf16[1024,2048]{1,0:T(8,128)(2,1)}, bf16[1024,2048]{1,0:T(8,128)(2,1)}, b...) custom-call(bf16[1024,512]{1,0:T(8,128)(2,1)} %hid.1, ...), custom_call_target="tpu_custom_call" | custom-call | flops 85899345920 | bytes 100000000 | tf_op jit(solution)/shard_map/phase_ab/pallas_call | solution.py:890
  246.1 158.0 %phase_c.1 = (f32[512,2048]{1,0:T(8,128)}, bf16[512,2048]{1,0:T(8,128)(2,1)}, f32[512,2048]{1,0:T(8,128)}, bf16[512,2048]{1,0:T(8,128)(2,1)}, f32[2048,512]{1,0:...) custom-call(bf16[1024,2048]{1,0:T(8,128)(2,1)} %get-tuple-element.52, ...), custom_call_target="tpu_custom_call" | custom-call | flops 85899345920 | bytes 100000000 | tf_op jit(solution)/shard_map/phase_c/pallas_call | solution.py:1150
  404.1 14.0 %results.1 = (bf16[1024,512]{1,0:T(8,128)(2,1)}, f32[512,2048]{1,0:T(8,128)}, f32[512,2048]{1,0:T(8,128)}, f32[2048,512]{1,0:T(8,128)}, f32[512,512]{1,0:T(8,128...) custom-call(bf16[1024,512]{1,0:T(8,128)(2,1)} %get-tuple-element.51., ...), custom_call_target="tpu_custom_call" | custom-call | flops 1000000 | bytes 35000000 | tf_op jit(solution)/shard_map/results/pallas_call | solution.py:1195

commit v13 on v12

--- a/solution.py
+++ b/solution.py
@@ -499,7 +499,7 @@
 
     gate = WeightGather(net, wg, wg_v, pos, True, 2)
     up = WeightGather(net, wu, wu_v, pos, True, 2)
-    down = WeightGather(net, wd, wd_v, pos, False, 4, 1)
+    down = WeightGather(net, wd, wd_v, pos, False, 8, 1)
     q_w = WeightGather(net, wq, wq_v.at[pl.ds(0, q_width), :], pos, False, 1)
     kv_w = WeightGather(net, wkv, wq_v.at[pl.ds(q_width, width - q_width), :], pos, False, 1)
     ag = LineGather(net, n_v, sub, z)
@@ -610,6 +610,10 @@
         cols = pl.ds(j * (dim // 2), dim // 2)
         n_v[ds(b * sub, sub), cols] = dot(wg_v[ds(b * sub, sub), :], wd_v[:, cols]).astype(BF16)
 
+    def both(event, ch):
+        event(ch)
+        event(ch + 1)
+
     outs += [net.here(wq_v, wq_o), net.here(eq_v, eq_o)]
     gate.finish_local()
     gate.y_event(1)
@@ -649,8 +653,8 @@
 
     @pl.loop(0, 4)
     def _(i):
-        pl.when(i == 1)(lambda: down.y_event(0))
-        pl.when(i == 2)(lambda: down.y_event(1))
+        pl.when(i == 1)(lambda: both(down.y_event, 0))
+        pl.when(i == 2)(lambda: both(down.y_event, 2))
         pl.when(i == 3)(lambda: up.x_event(1))
         up_part(pick(i, z), 0)
 
@@ -658,13 +662,17 @@
         rsc.send_mid(1)
         rsc.send_mid(0)
         down.x_event(0)
+        down.x_event(1)
 
     def up_events_2():
-        down.y_event(2)
+        down.y_event(4)
+        down.y_event(5)
 
     def up_events_3():
-        down.y_event(3)
-        down.x_event(1)
+        down.y_event(6)
+        down.y_event(7)
+        down.x_event(2)
+        down.x_event(3)
 
     up.finish(1)
     outs.append(net.here(wu_v, wu_o))
@@ -687,11 +695,11 @@
 
     @pl.loop(0, 4)
     def _(i):
-        pl.when(i == 2)(lambda: down.x_event(2))
-        pl.when(i == 3)(lambda: down.x_event(3))
+        pl.when(i == 2)(lambda: both(down.x_event, 4))
+        pl.when(i == 3)(lambda: both(down.x_event, 6))
         down_part(pick(3 - i, z), 0)
 
-    for ch in range(4):
+    for ch in range(8):
         down.finish(ch)
 
     @pl.loop(0, 4)
@@ -894,7 +902,7 @@
             VMEM((width, dim), BF16), VMEM((width, tokens), BF16), vtok, VMEM((5 * sub, dim), BF16), VMEM((5 * sub, dim), BF16),
             VMEM((8, dim), F32), VMEM((8, dim), F32), VMEM((128, 128), BF16), VMEM((1, tokens), jnp.int32), VMEM((128, 128), F32),
             VMEM((dt,), BF16), VMEM((dt,), BF16), VMEM((8, dt), F32),
-            pltpu.SemaphoreType.DMA((236,)), pltpu.SemaphoreType.DMA((236,)), pltpu.SemaphoreType.DMA((48,))],
+            pltpu.SemaphoreType.DMA((256,)), pltpu.SemaphoreType.DMA((256,)), pltpu.SemaphoreType.DMA((48,))],
         compiler_params=pltpu.CompilerParams(collective_id=0, has_side_effects=True, vmem_limit_bytes=VMEM_LIMIT),
         cost_estimate=pl.CostEstimate(flops=20 * tokens * dim * ff, bytes_accessed=100000000, transcendentals=0), name="phase_ab",
     )(hid, eqh, ekvh, pos, inv, swap, dh2h, wg, wu, wd, wq, wkv, gf, ga)

time: 419 us -> 420 us (level)
  no operation moved by 1% of the time
where the time goes in v13:
time: 420 us
  Pallas kernels  419 us (100%)
    pallas_call x1, Pallas kernels, call_ab(): pl.pallas_call(functools.partial(kernel_ab, q_width), out_shape=shapes, i...  247 us
    pallas_call x1, Pallas kernels, call_c(): pl.pallas_call(functools.partial(kernel_c, q_width), out_shape=shapes, in...  158 us
    pallas_call x1, Pallas kernels, call_out(): pl.pallas_call(functools.partial(kernel_out, pieces, n), out_shape=tuple(...  14 us

profile of v13, /device:TPU:0, one launch (start us, length us, event | category | flops | bytes accessed | tf_op | source)
XLA Modules:
  0.0 419.6 jit_solution(9349828760341623445)
XLA Ops:
  0.6 247.2 %phase_ab.1 = (bf16[1024,2048]{1,0:T(8,128)(2,1)}, bf16[1024,2048]{1,0:T(8,128)(2,1)}, bf16[1024,2048]{1,0:T(8,128)(2,1)}, bf16[1024,2048]{1,0:T(8,128)(2,1)}, b...) custom-call(bf16[1024,512]{1,0:T(8,128)(2,1)} %hid.1, ...), custom_call_target="tpu_custom_call" | custom-call | flops 85899345920 | bytes 100000000 | tf_op jit(solution)/shard_map/phase_ab/pallas_call | solution.py:898
  247.8 157.5 %phase_c.1 = (f32[512,2048]{1,0:T(8,128)}, bf16[512,2048]{1,0:T(8,128)(2,1)}, f32[512,2048]{1,0:T(8,128)}, bf16[512,2048]{1,0:T(8,128)(2,1)}, f32[2048,512]{1,0:...) custom-call(bf16[1024,2048]{1,0:T(8,128)(2,1)} %get-tuple-element.52, ...), custom_call_target="tpu_custom_call" | custom-call | flops 85899345920 | bytes 100000000 | tf_op jit(solution)/shard_map/phase_c/pallas_call | solution.py:1158
  405.4 14.0 %results.1 = (bf16[1024,512]{1,0:T(8,128)(2,1)}, f32[512,2048]{1,0:T(8,128)}, f32[512,2048]{1,0:T(8,128)}, f32[2048,512]{1,0:T(8,128)}, f32[512,512]{1,0:T(8,128...) custom-call(bf16[1024,512]{1,0:T(8,128)(2,1)} %get-tuple-element.51., ...), custom_call_target="tpu_custom_call" | custom-call | flops 1000000 | bytes 35000000 | tf_op jit(solution)/shard_map/results/pallas_call | solution.py:1203

commit v14 on v12

--- a/solution.py
+++ b/solution.py
@@ -1173,7 +1173,7 @@
     jobs = [(i, c) for i in range(n) for c in range(pieces[i])]
     get = [pltpu.make_async_copy(part(ins[i], i, c), part(bufs[i], i, c), read.at[m]) for m, (i, c) in enumerate(jobs)]
     put = [pltpu.make_async_copy(part(bufs[i], i, c), part(outs[i], i, c), write.at[m]) for m, (i, c) in enumerate(jobs)]
-    ahead = min(8, len(get))
+    ahead = min(6, len(get))
     for g in get[:ahead]:
         g.start()
     gain_a[...] = jnp.sum(gains[pl.ds(0, 8), :], axis=0, keepdims=True)
@@ -1189,7 +1189,7 @@
 
 def call_out(results, gains):
     n = len(results)
-    pieces = tuple(max(1, x.size * x.dtype.itemsize // 2**20) for x in results)
+    pieces = tuple(max(1, x.size * x.dtype.itemsize // 2**21) for x in results)
     row = jax.ShapeDtypeStruct((1, gains.shape[1]), F32)
     whole = pl.BlockSpec(memory_space=pltpu.VMEM)
     return pl.pallas_call(

time: 419 us -> 418 us (level)
  no operation moved by 1% of the time
where the time goes in v14:
time: 418 us
  Pallas kernels  417 us (100%)
    pallas_call x1, Pallas kernels, call_ab(): pl.pallas_call(functools.partial(kernel_ab, q_width), out_shape=shapes, i...  245 us
    pallas_call x1, Pallas kernels, call_c(): pl.pallas_call(functools.partial(kernel_c, q_width), out_shape=shapes, in...  158 us
    pallas_call x1, Pallas kernels, call_out(): pl.pallas_call(functools.partial(kernel_out, pieces, n), out_shape=tuple(...  13.6 us

profile of v14, /device:TPU:0, one launch (start us, length us, event | category | flops | bytes accessed | tf_op | source)
XLA Modules:
  0.0 417.9 jit_solution(11478597698268272753)
XLA Ops:
  0.6 245.4 %phase_ab.1 = (bf16[1024,2048]{1,0:T(8,128)(2,1)}, bf16[1024,2048]{1,0:T(8,128)(2,1)}, bf16[1024,2048]{1,0:T(8,128)(2,1)}, bf16[1024,2048]{1,0:T(8,128)(2,1)}, b...) custom-call(bf16[1024,512]{1,0:T(8,128)(2,1)} %hid.1, ...), custom_call_target="tpu_custom_call" | custom-call | flops 85899345920 | bytes 100000000 | tf_op jit(solution)/shard_map/phase_ab/pallas_call | solution.py:890
  246.1 158.0 %phase_c.1 = (f32[512,2048]{1,0:T(8,128)}, bf16[512,2048]{1,0:T(8,128)(2,1)}, f32[512,2048]{1,0:T(8,128)}, bf16[512,2048]{1,0:T(8,128)(2,1)}, f32[2048,512]{1,0:...) custom-call(bf16[1024,2048]{1,0:T(8,128)(2,1)} %get-tuple-element.52, ...), custom_call_target="tpu_custom_call" | custom-call | flops 85899345920 | bytes 100000000 | tf_op jit(solution)/shard_map/phase_c/pallas_call | solution.py:1150
  404.1 13.6 %results.1 = (bf16[1024,512]{1,0:T(8,128)(2,1)}, f32[512,2048]{1,0:T(8,128)}, f32[512,2048]{1,0:T(8,128)}, f32[2048,512]{1,0:T(8,128)}, f32[512,512]{1,0:T(8,128...) custom-call(bf16[1024,512]{1,0:T(8,128)(2,1)} %get-tuple-element.51., ...), custom_call_target="tpu_custom_call" | custom-call | flops 1000000 | bytes 35000000 | tf_op jit(solution)/shard_map/results/pallas_call | solution.py:1195
